TPU v7x, 32 devices: a whole 2x2x4 slice. The times are simulated.
32 devices in a mesh: scan: 8 (over z, y), grp: 4 (over x, core).
Axes of the slice: x: 2, y: 2, z: 4, core: 2. Of those that a mesh axis runs over, the one named last changes fastest.
Arguments:
- samples: float32 [128, 64, 6, 128], P('scan', 'grp'), may hold values from -6 to 6
- point_count: int32 [128], P('scan'), may hold values from 4096 to 8192
- corr_scan: int32 [128, 64], P('scan', 'grp'), may hold values from 0 to 127, as said below
- corr_tile: int32 [128, 64], P('scan', 'grp'), may hold values from 0 to 63
- corr_src: int32 [128, 64, 128], P('scan', 'grp'), may hold values from 0 to 2047
Outputs:
- hessian: float32 [128, 6, 6, 128], P('scan', None, None, 'grp')
- gradient: float32 [128, 6], P(('scan', 'grp'))
Inputs may be any that keep to these rules, and one draw needn't show every extreme that they name: Never the scan of the entry's own row. A named tile is held by the device with scan index corr_scan // 16 and grp index corr_tile // 16; the 256 entries of one device name at most 16 tiles held by any one device, and in every draw some device is named exactly 16 times by every device.
All inputs are finite; a program needn't handle non-finite values.
Results may differ from a plain program's by a relative error of at most 0.00021.
Values sent between devices are 32-bit elements; how exact they have to be, the bound alone decides.
No kernel may reach another device: no remote copies, remote signals or barrier semaphores. Data moves between devices by JAX's collectives and lax.ppermute only.
A program may use at most 64 MiB of HBM per device.

v0:
```python
import jax
import jax.numpy as jnp
from jax import lax
from jax.sharding import PartitionSpec as P


def pair_blocks(pos_x, pos_y, pos_z, source_mask, tile_data):
    diff_x = pos_x - tile_data[:, 0, :]
    diff_y = pos_y - tile_data[:, 1, :]
    diff_z = pos_z - tile_data[:, 2, :]
    normal_x = tile_data[:, 3, :]
    normal_y = tile_data[:, 4, :]
    normal_z = tile_data[:, 5, :]
    residual = normal_x * diff_x + normal_y * diff_y + normal_z * diff_z
    weight = source_mask / (1.0 + residual * residual)
    jacobian = jnp.stack(
        [
            pos_y * normal_z - pos_z * normal_y,
            pos_z * normal_x - pos_x * normal_z,
            pos_x * normal_y - pos_y * normal_x,
            normal_x,
            normal_y,
            normal_z,
        ],
        axis=1,
    )
    blocks = jnp.einsum(
        "nik,njk->nij", jacobian * weight[:, None, :], jacobian, precision=lax.Precision.HIGHEST
    )
    vectors = jnp.einsum("nik,nk->ni", jacobian, weight * residual, precision=lax.Precision.HIGHEST)
    return (blocks.reshape(-1, 36), vectors)


def pick_points(samples, point_ids):
    scan_local = samples.shape[0]
    tiles_local = samples.shape[1]
    group_points = tiles_local * 128
    pick_total = point_ids.shape[1]
    block = pick_total
    while block > 128 and block % 2 == 0 and (group_points * block > 4194304):
        block = block // 2
    positions = samples[:, :, 0:3, :].transpose(0, 2, 1, 3).reshape(scan_local, 3, group_points)
    point_iota = jnp.arange(group_points, dtype=jnp.int32)[:, None]

    def one_scan(operands):
        position, picks = operands
        picks = picks.reshape(pick_total // block, block)

        def one_block(wanted):
            selector = (point_iota == wanted[None, :]).astype(jnp.float32)
            return jnp.dot(
                position,
                selector,
                precision=lax.Precision.HIGHEST,
                preferred_element_type=jnp.float32,
            )

        chosen = lax.map(one_block, picks)
        return chosen.transpose(1, 0, 2).reshape(3, pick_total)

    picked = lax.map(one_scan, (positions, point_ids))
    return picked.transpose(1, 0, 2).reshape(3, -1, 128)


def masked_tiles(samples, point_count, codes, group_index):
    tiles_local = samples.shape[1]
    safe_codes = jnp.maximum(codes, 0)
    scan_local = safe_codes // tiles_local
    tile_local = safe_codes % tiles_local
    tile_table = samples.reshape(-1, 6, 128)
    picked = tile_table[safe_codes]
    limits = point_count[scan_local]
    point_ids = (group_index * tiles_local + tile_local)[..., None] * 128 + jnp.arange(128)
    valid_rows = (point_ids < limits[..., None]).astype(jnp.float32)
    return jnp.concatenate(
        [picked[..., 0:3, :], picked[..., 3:6, :] * valid_rows[..., None, :]], axis=-2
    )


def assemble(row_ids, own_scan, other_scan, blocks, vectors, row_count, column_count):
    row_hot = (row_ids[:, None] == jnp.arange(row_count)[None, :]).astype(jnp.float32)
    columns = jnp.arange(column_count)
    column_mix = (own_scan[:, None] == columns[None, :]).astype(jnp.float32) - (
        other_scan[:, None] == columns[None, :]
    ).astype(jnp.float32)
    weighted = (row_hot[:, :, None] * blocks[:, None, :]).reshape(blocks.shape[0], row_count * 36)
    hessian = jnp.einsum(
        "sk,sc->kc", weighted, column_mix, precision=lax.Precision.HIGHEST
    ).reshape(row_count, 6, 6, column_count)
    gradient = jnp.einsum("sl,sj->lj", row_hot, vectors, precision=lax.Precision.HIGHEST)
    return (hessian, gradient)


def local(samples, point_count, corr_scan, corr_tile, corr_src):
    scan_local = samples.shape[0]
    tiles_local = samples.shape[1]
    per_scan = corr_scan.shape[1]
    request_count = scan_local * per_scan
    device_count = lax.axis_size(("scan", "grp"))
    group_count = lax.axis_size("grp")
    slot_cap = 2 * request_count // device_count
    scan_index = lax.axis_index("scan")
    group_index = lax.axis_index("grp")
    scan_total = scan_local * lax.axis_size("scan")
    group_points = tiles_local * 128
    point_ids = corr_src.reshape(scan_local, per_scan * 128)
    picked = pick_points(samples, point_ids)
    coords = [picked[0], picked[1], picked[2]]
    source_mask = (
        (group_index * group_points + point_ids < point_count[:, None])
        .astype(jnp.float32)
        .reshape(request_count, 128)
    )
    target_scan = corr_scan.reshape(-1)
    target_tile = corr_tile.reshape(-1)
    destination = target_scan // scan_local * group_count + target_tile // tiles_local
    codes = target_scan % scan_local * tiles_local + target_tile % tiles_local
    onehot = (destination[:, None] == jnp.arange(device_count)[None, :]).astype(jnp.int32)
    earlier = jnp.cumsum(onehot, axis=0) - onehot
    slot_rank = jnp.sum(earlier * onehot, axis=1)
    slot_ids = destination * slot_cap + slot_rank
    source_scan = scan_index * scan_local + jnp.arange(request_count) // per_scan
    request_ids = jnp.full((device_count * slot_cap, 2), -1, jnp.int32)
    request_ids = (
        request_ids.at[slot_ids]
        .set(jnp.stack([codes, source_scan], axis=1))
        .reshape(device_count, slot_cap, 2)
    )
    requests = lax.all_to_all(request_ids, ("scan", "grp"), split_axis=0, concat_axis=0, tiled=True)
    fetched = masked_tiles(samples, point_count, requests[..., 0], group_index)
    returned = lax.all_to_all(fetched, ("scan", "grp"), split_axis=0, concat_axis=0, tiled=True)
    my_tiles = returned.reshape(-1, 6, 128)[slot_ids]
    out_blocks, out_vectors = pair_blocks(coords[0], coords[1], coords[2], source_mask, my_tiles)
    block_buf = (
        jnp.zeros((device_count * slot_cap, 36), jnp.float32)
        .at[slot_ids]
        .set(out_blocks)
        .reshape(device_count, slot_cap, 36)
    )
    vector_buf = (
        jnp.zeros((device_count * slot_cap, 6), jnp.float32)
        .at[slot_ids]
        .set(out_vectors)
        .reshape(device_count, slot_cap, 6)
    )
    in_blocks, in_vectors = (
        lax.all_to_all(block_buf, ("scan", "grp"), split_axis=0, concat_axis=0, tiled=True),
        lax.all_to_all(vector_buf, ("scan", "grp"), split_axis=0, concat_axis=0, tiled=True),
    )
    in_codes = requests[..., 0].reshape(-1)
    in_source = requests[..., 1].reshape(-1)
    in_local = jnp.maximum(in_codes, 0) // tiles_local
    row_ids = jnp.concatenate([jnp.arange(request_count) // per_scan, in_local])
    own_scan = scan_index * scan_local + row_ids
    other_scan = jnp.concatenate([target_scan, in_source])
    all_blocks = jnp.concatenate([out_blocks, in_blocks.reshape(-1, 36)], axis=0)
    all_vectors = jnp.concatenate([out_vectors, -in_vectors.reshape(-1, 6)], axis=0)
    hess_part, grad_part = assemble(
        row_ids, own_scan, other_scan, all_blocks, all_vectors, scan_local, scan_total
    )
    hessian, gradient = (
        lax.psum_scatter(hess_part, "grp", scatter_dimension=3, tiled=True),
        lax.psum_scatter(grad_part, "grp", scatter_dimension=0, tiled=True),
    )
    return (hessian, gradient)


def solution(mesh):
    placed = (
        P("scan", "grp", None, None),
        P("scan"),
        P("scan", "grp"),
        P("scan", "grp"),
        P("scan", "grp", None),
    )
    return jax.shard_map(
        local,
        mesh=mesh,
        in_specs=placed,
        out_specs=(P("scan", None, None, "grp"), P(("scan", "grp"), None)),
        check_vma=False,
    )
```

profile of v0, /device:TPU:0, one launch (start us, length us, event | category | flops | bytes accessed | tf_op | source)
XLA Modules:
  0.0 203.9 jit_solution(4460691769309137609)
XLA Ops:
  15.2 7.3 %all-to-all-start = ((s32[32,16,2]{1,2,0:T(2,128)}), s32[32,16,2]{1,2,0:T(2,128)S(1)}, u32[]{:S(2)}, u32[]{:S(2)}) async-start(s32[32,16,2]{1,2,0:T(2,128)} %copy.143), calls=%async_computation | async-start | bytes 65536 | tf_op jit(solution)/shard_map/all_to_all | solution.py:129
  25.1 4.6 %all-to-all-done = s32[32,16,2]{1,2,0:T(2,128)S(1)} async-done(((s32[32,16,2]{1,2,0:T(2,128)}), s32[32,16,2]{1,2,0:T(2,128)S(1)}, u32[]{:S(2)}, u32[]{:S(2)}) %all-to-all-start) | async-done | bytes 4128 | tf_op jit(solution)/shard_map/all_to_all | solution.py:129
  30.1 3.3 %gather_fusion.1 = s32[512]{0:T(512)S(1)} fusion(s32[16]{0:T(128)S(1)} %copy-done, s32[1024]{0:T(1024)S(1)} %pad_clamp_fusion.1), kind=kCustom, calls=%fused_computation.1 | custom fusion | bytes 6144 | tf_op jit(solution)/shard_map/gather | solution.py:72
  41.0 95.8 %while.11 = (s32[]{:T(128)}, f32[16,3,2048]{2,1,0:T(4,128)S(1)}, f32[16,3,2048]{2,1,0:T(4,128)}, s32[16,2048]{1,0:T(8,128)S(1)}, s32[]{:T(128)}) while((s32[]{:T(128)}, f32[16,3,2048]{2,1,0:T(4,128)S(1)}, f32[16,3,2048]{2,1,0:T(4,128)}, s32[16,2048]{1,0:T(8,128)S(1)}, s32[]{:T(128)}) %tuple.56), condition=%wide.region_5.6_spmd.clone, body=%wide.region_4.5_spmd.clone.sunk | while | flops 155189248 | bytes 91201 | solution.py:61
  41.0 6.0 %fusion.69 = f32[16,3,2048]{2,1,0:T(4,128)S(1)} fusion(f32[16,3,2048]{2,1,0:T(4,128)S(1)} %get-tuple-element.140, s32[]{:T(128)} %get-tuple-element.139, s32[2048]{0:T(1024)S(1)} %bitcast.199, f32[16,3,2048]{2,1,0:T(4,128)} %get-tuple-element.146), kind=kOutput, calls=%fused_computation.11.clone.1 | convolution fusion | flops 155189248 | bytes 74752 | tf_op jit(solution)/shard_map/while/body/eval_jaxpr/while/body/eval_jaxpr/dot_general | solution.py:51
  47.0 6.0 %fusion.69 = f32[16,3,2048]{2,1,0:T(4,128)S(1)} fusion(f32[16,3,2048]{2,1,0:T(4,128)S(1)} %get-tuple-element.140, s32[]{:T(128)} %get-tuple-element.139, s32[2048]{0:T(1024)S(1)} %bitcast.199, f32[16,3,2048]{2,1,0:T(4,128)} %get-tuple-element.146), kind=kOutput, calls=%fused_computation.11.clone.1 | convolution fusion | flops 155189248 | bytes 74752 | tf_op jit(solution)/shard_map/while/body/eval_jaxpr/while/body/eval_jaxpr/dot_general | solution.py:51
  53.0 6.0 %fusion.69 = f32[16,3,2048]{2,1,0:T(4,128)S(1)} fusion(f32[16,3,2048]{2,1,0:T(4,128)S(1)} %get-tuple-element.140, s32[]{:T(128)} %get-tuple-element.139, s32[2048]{0:T(1024)S(1)} %bitcast.199, f32[16,3,2048]{2,1,0:T(4,128)} %get-tuple-element.146), kind=kOutput, calls=%fused_computation.11.clone.1 | convolution fusion | flops 155189248 | bytes 74752 | tf_op jit(solution)/shard_map/while/body/eval_jaxpr/while/body/eval_jaxpr/dot_general | solution.py:51
  59.0 6.0 %fusion.69 = f32[16,3,2048]{2,1,0:T(4,128)S(1)} fusion(f32[16,3,2048]{2,1,0:T(4,128)S(1)} %get-tuple-element.140, s32[]{:T(128)} %get-tuple-element.139, s32[2048]{0:T(1024)S(1)} %bitcast.199, f32[16,3,2048]{2,1,0:T(4,128)} %get-tuple-element.146), kind=kOutput, calls=%fused_computation.11.clone.1 | convolution fusion | flops 155189248 | bytes 74752 | tf_op jit(solution)/shard_map/while/body/eval_jaxpr/while/body/eval_jaxpr/dot_general | solution.py:51
  65.0 6.0 %fusion.69 = f32[16,3,2048]{2,1,0:T(4,128)S(1)} fusion(f32[16,3,2048]{2,1,0:T(4,128)S(1)} %get-tuple-element.140, s32[]{:T(128)} %get-tuple-element.139, s32[2048]{0:T(1024)S(1)} %bitcast.199, f32[16,3,2048]{2,1,0:T(4,128)} %get-tuple-element.146), kind=kOutput, calls=%fused_computation.11.clone.1 | convolution fusion | flops 155189248 | bytes 74752 | tf_op jit(solution)/shard_map/while/body/eval_jaxpr/while/body/eval_jaxpr/dot_general | solution.py:51
  70.9 6.0 %fusion.69 = f32[16,3,2048]{2,1,0:T(4,128)S(1)} fusion(f32[16,3,2048]{2,1,0:T(4,128)S(1)} %get-tuple-element.140, s32[]{:T(128)} %get-tuple-element.139, s32[2048]{0:T(1024)S(1)} %bitcast.199, f32[16,3,2048]{2,1,0:T(4,128)} %get-tuple-element.146), kind=kOutput, calls=%fused_computation.11.clone.1 | convolution fusion | flops 155189248 | bytes 74752 | tf_op jit(solution)/shard_map/while/body/eval_jaxpr/while/body/eval_jaxpr/dot_general | solution.py:51
  76.9 6.0 %fusion.69 = f32[16,3,2048]{2,1,0:T(4,128)S(1)} fusion(f32[16,3,2048]{2,1,0:T(4,128)S(1)} %get-tuple-element.140, s32[]{:T(128)} %get-tuple-element.139, s32[2048]{0:T(1024)S(1)} %bitcast.199, f32[16,3,2048]{2,1,0:T(4,128)} %get-tuple-element.146), kind=kOutput, calls=%fused_computation.11.clone.1 | convolution fusion | flops 155189248 | bytes 74752 | tf_op jit(solution)/shard_map/while/body/eval_jaxpr/while/body/eval_jaxpr/dot_general | solution.py:51
  82.9 6.0 %fusion.69 = f32[16,3,2048]{2,1,0:T(4,128)S(1)} fusion(f32[16,3,2048]{2,1,0:T(4,128)S(1)} %get-tuple-element.140, s32[]{:T(128)} %get-tuple-element.139, s32[2048]{0:T(1024)S(1)} %bitcast.199, f32[16,3,2048]{2,1,0:T(4,128)} %get-tuple-element.146), kind=kOutput, calls=%fused_computation.11.clone.1 | convolution fusion | flops 155189248 | bytes 74752 | tf_op jit(solution)/shard_map/while/body/eval_jaxpr/while/body/eval_jaxpr/dot_general | solution.py:51
  88.9 6.0 %fusion.69 = f32[16,3,2048]{2,1,0:T(4,128)S(1)} fusion(f32[16,3,2048]{2,1,0:T(4,128)S(1)} %get-tuple-element.140, s32[]{:T(128)} %get-tuple-element.139, s32[2048]{0:T(1024)S(1)} %bitcast.199, f32[16,3,2048]{2,1,0:T(4,128)} %get-tuple-element.146), kind=kOutput, calls=%fused_computation.11.clone.1 | convolution fusion | flops 155189248 | bytes 74752 | tf_op jit(solution)/shard_map/while/body/eval_jaxpr/while/body/eval_jaxpr/dot_general | solution.py:51
  94.9 6.0 %fusion.69 = f32[16,3,2048]{2,1,0:T(4,128)S(1)} fusion(f32[16,3,2048]{2,1,0:T(4,128)S(1)} %get-tuple-element.140, s32[]{:T(128)} %get-tuple-element.139, s32[2048]{0:T(1024)S(1)} %bitcast.199, f32[16,3,2048]{2,1,0:T(4,128)} %get-tuple-element.146), kind=kOutput, calls=%fused_computation.11.clone.1 | convolution fusion | flops 155189248 | bytes 74752 | tf_op jit(solution)/shard_map/while/body/eval_jaxpr/while/body/eval_jaxpr/dot_general | solution.py:51
  100.9 6.0 %fusion.69 = f32[16,3,2048]{2,1,0:T(4,128)S(1)} fusion(f32[16,3,2048]{2,1,0:T(4,128)S(1)} %get-tuple-element.140, s32[]{:T(128)} %get-tuple-element.139, s32[2048]{0:T(1024)S(1)} %bitcast.199, f32[16,3,2048]{2,1,0:T(4,128)} %get-tuple-element.146), kind=kOutput, calls=%fused_computation.11.clone.1 | convolution fusion | flops 155189248 | bytes 74752 | tf_op jit(solution)/shard_map/while/body/eval_jaxpr/while/body/eval_jaxpr/dot_general | solution.py:51
  106.9 6.0 %fusion.69 = f32[16,3,2048]{2,1,0:T(4,128)S(1)} fusion(f32[16,3,2048]{2,1,0:T(4,128)S(1)} %get-tuple-element.140, s32[]{:T(128)} %get-tuple-element.139, s32[2048]{0:T(1024)S(1)} %bitcast.199, f32[16,3,2048]{2,1,0:T(4,128)} %get-tuple-element.146), kind=kOutput, calls=%fused_computation.11.clone.1 | convolution fusion | flops 155189248 | bytes 74752 | tf_op jit(solution)/shard_map/while/body/eval_jaxpr/while/body/eval_jaxpr/dot_general | solution.py:51
  112.8 6.0 %fusion.69 = f32[16,3,2048]{2,1,0:T(4,128)S(1)} fusion(f32[16,3,2048]{2,1,0:T(4,128)S(1)} %get-tuple-element.140, s32[]{:T(128)} %get-tuple-element.139, s32[2048]{0:T(1024)S(1)} %bitcast.199, f32[16,3,2048]{2,1,0:T(4,128)} %get-tuple-element.146), kind=kOutput, calls=%fused_computation.11.clone.1 | convolution fusion | flops 155189248 | bytes 74752 | tf_op jit(solution)/shard_map/while/body/eval_jaxpr/while/body/eval_jaxpr/dot_general | solution.py:51
  118.8 6.0 %fusion.69 = f32[16,3,2048]{2,1,0:T(4,128)S(1)} fusion(f32[16,3,2048]{2,1,0:T(4,128)S(1)} %get-tuple-element.140, s32[]{:T(128)} %get-tuple-element.139, s32[2048]{0:T(1024)S(1)} %bitcast.199, f32[16,3,2048]{2,1,0:T(4,128)} %get-tuple-element.146), kind=kOutput, calls=%fused_computation.11.clone.1 | convolution fusion | flops 155189248 | bytes 74752 | tf_op jit(solution)/shard_map/while/body/eval_jaxpr/while/body/eval_jaxpr/dot_general | solution.py:51
  124.8 6.0 %fusion.69 = f32[16,3,2048]{2,1,0:T(4,128)S(1)} fusion(f32[16,3,2048]{2,1,0:T(4,128)S(1)} %get-tuple-element.140, s32[]{:T(128)} %get-tuple-element.139, s32[2048]{0:T(1024)S(1)} %bitcast.199, f32[16,3,2048]{2,1,0:T(4,128)} %get-tuple-element.146), kind=kOutput, calls=%fused_computation.11.clone.1 | convolution fusion | flops 155189248 | bytes 74752 | tf_op jit(solution)/shard_map/while/body/eval_jaxpr/while/body/eval_jaxpr/dot_general | solution.py:51
  130.8 6.0 %fusion.69 = f32[16,3,2048]{2,1,0:T(4,128)S(1)} fusion(f32[16,3,2048]{2,1,0:T(4,128)S(1)} %get-tuple-element.140, s32[]{:T(128)} %get-tuple-element.139, s32[2048]{0:T(1024)S(1)} %bitcast.199, f32[16,3,2048]{2,1,0:T(4,128)} %get-tuple-element.146), kind=kOutput, calls=%fused_computation.11.clone.1 | convolution fusion | flops 155189248 | bytes 74752 | tf_op jit(solution)/shard_map/while/body/eval_jaxpr/while/body/eval_jaxpr/dot_general | solution.py:51
  148.4 5.7 %all-to-all-start.2 = ((f32[32,1,576]{2,1,0:T(1,128)}), f32[32,1,576]{2,1,0:T(1,128)S(1)}, u32[]{:S(2)}, u32[]{:S(2)}) async-start(f32[32,1,576]{2,1,0:T(1,128)} %reshape.580), calls=%async_computation.2 | async-start | bytes 163840 | tf_op jit(solution)/shard_map/all_to_all | solution.py:147
  155.1 6.5 %all-to-all-done.2 = f32[32,1,576]{2,1,0:T(1,128)S(1)} async-done(((f32[32,1,576]{2,1,0:T(1,128)}), f32[32,1,576]{2,1,0:T(1,128)S(1)}, u32[]{:S(2)}, u32[]{:S(2)}) %all-to-all-start.2) | async-done | bytes 73760 | tf_op jit(solution)/shard_map/all_to_all | solution.py:147
  181.0 6.9 %all-to-all-done.3 = f32[32,16,6]{1,2,0:T(8,128)S(1)} async-done(((f32[32,16,6]{1,2,0:T(8,128)}), f32[32,16,6]{1,2,0:T(8,128)S(1)}, u32[]{:S(2)}, u32[]{:S(2)}) %all-to-all-start.3) | async-done | bytes 12320 | tf_op jit(solution)/shard_map/all_to_all | solution.py:148
  188.4 5.9 %all-reduce = f32[16,6]{1,0:T(8,128)S(1)} all-reduce(f32[16,6]{1,0:T(8,128)S(1)} %fusion.40), channel_id=3, replica_groups=mesh['scan'=8,'grp'=4] {'grp'}, use_global_device_ids=true, to_apply=%region_9.10.clone | all-reduce | flops 96 | bytes 768
  (140 shorter events, 52.8 us)
Async XLA Ops:
  7.2 16.4 %copy-start.1 = (f32[16,16,6,128]{3,1,2,0:T(8,128)S(1)}, f32[16,16,6,128]{3,1,2,0:T(8,128)}, u32[]{:S(2)}) copy-start(f32[16,16,6,128]{3,1,2,0:T(8,128)} %param.7) | copy-start | bytes 2359300
  15.2 14.6 %all-to-all-start = ((s32[32,16,2]{1,2,0:T(2,128)}), s32[32,16,2]{1,2,0:T(2,128)S(1)}, u32[]{:S(2)}, u32[]{:S(2)}) async-start(s32[32,16,2]{1,2,0:T(2,128)} %copy.143), calls=%async_computation | async-start | bytes 65536 | tf_op jit(solution)/shard_map/all_to_all | solution.py:129
  23.5 1.5 copy-start.3
  23.6 6.5 %copy-start = (s32[16]{0:T(128)S(1)}, s32[16]{0:T(128)}, u32[]{:S(2)}) copy-start(s32[16]{0:T(128)} %param.8) | copy-start | bytes 196
  38.0 3.0 %copy-start.4 = (f32[16,3,2048]{2,1,0:T(4,128)S(1)}, f32[16,3,2048]{2,1,0:T(4,128)}, u32[]{:S(2)}) copy-start(f32[16,3,2048]{2,1,0:T(4,128)} %custom-call.6) | copy-start | bytes 1179652
  38.0 99.7 %all-to-all-start.1 = ((f32[32,16,6,128]{3,1,2,0:T(8,128)}), f32[32,16,6,128]{3,1,2,0:T(8,128)S(1)}, u32[]{:S(2)}, u32[]{:S(2)}) async-start(f32[32,16,6,128]{3,1,2,0:T(8,128)} %pad_maximum_fusion), calls=%async_computation.1 | async-start | bytes 3145728 | tf_op jit(solution)/shard_map/all_to_all | solution.py:131
  142.7 0.8 copy-start.2
  142.9 0.7 copy-start.5
  142.9 0.8 copy-start.7
  142.9 0.8 copy-start.9
  148.4 13.2 %all-to-all-start.2 = ((f32[32,1,576]{2,1,0:T(1,128)}), f32[32,1,576]{2,1,0:T(1,128)S(1)}, u32[]{:S(2)}, u32[]{:S(2)}) async-start(f32[32,1,576]{2,1,0:T(1,128)} %reshape.580), calls=%async_computation.2 | async-start | bytes 163840 | tf_op jit(solution)/shard_map/all_to_all | solution.py:147
  154.0 40.9 %reduce-scatter.4.cloned.1.call-start = ((), (), s32[]{:S(2)}) async-start(), calls=%async_computation.5 | async-start | bytes 409600
  170.1 1.6 copy-start.6
  170.1 1.6 copy-start.8
  170.1 1.6 copy-start.10
  171.7 8.0 %copy-start.11 = (u32[32]{0:T(128)S(1)}, u32[32]{0:T(128)}, u32[]{:S(2)}) copy-start(u32[32]{0:T(128)} %constant.142) | copy-start | bytes 388
  177.1 10.8 %all-to-all-start.3 = ((f32[32,16,6]{1,2,0:T(8,128)}), f32[32,16,6]{1,2,0:T(8,128)S(1)}, u32[]{:S(2)}, u32[]{:S(2)}) async-start(f32[32,16,6]{1,2,0:T(8,128)} %copy.172), calls=%async_computation.3 | async-start | bytes 262144 | tf_op jit(solution)/shard_map/all_to_all | solution.py:148
Sparse Core Ops, SparseCore 0:
  171.8 17.4 reduce-scatter.3
where the time goes:
time: 206 us; the launch traced here: 204 us
  matrix products  103 us (50%)
  local copies, waits for them, and re-layouts  37.9 us (18%)
  starting transfers between devices  18.8 us (9%)
  waiting for transfers between devices  18.1 us (9%)
  between operations  15.2 us (7%)
  blocking collectives  5.95 us (3%)
  other arithmetic  4.39 us (2%)
    dot_general x16, matrix products, one_block(): jnp.dot(position, selector, precision=lax.Precision.HIGHEST, preferred_el...  95.4 us
    unnamed x36, local copies, waits for them, and re-layouts  8.17 us
    all_to_all x1, starting transfers between devices, local(): lax.all_to_all(request_ids, ('scan', 'grp'), split_axis=0, concat_axis=0,...  7.33 us
    all_to_all x1, waiting for transfers between devices, local(): lax.all_to_all(vector_buf, ('scan', 'grp'), split_axis=0, concat_axis=0,...  6.94 us
    all_to_all x1, waiting for transfers between devices, local(): lax.all_to_all(block_buf, ('scan', 'grp'), split_axis=0, concat_axis=0, t...  6.55 us
    unnamed x1, blocking collectives  5.95 us
    all_to_all x1, starting transfers between devices, local(): lax.all_to_all(block_buf, ('scan', 'grp'), split_axis=0, concat_axis=0, t...  5.66 us
    all_to_all x1, waiting for transfers between devices, local(): lax.all_to_all(request_ids, ('scan', 'grp'), split_axis=0, concat_axis=0,...  4.63 us
  transfers between devices with their start and end apart: 5, of which 3 were waited for; matrix products, arithmetic and copies ran while one was open for 52% of the time, Pallas kernels for 0%

commit v1 on v0

v1 whole, which is shorter than its diff:
```python
import jax
import jax.numpy as jnp
from jax import lax
from jax.experimental import pallas as pl
from jax.experimental.pallas import tpu as pltpu
from jax.sharding import PartitionSpec as P

LANES = 128
COORDS = 3
FIELDS = 6
PAIRS = [(i, j) for i in range(FIELDS) for j in range(i, FIELDS)]
MAT = len(PAIRS)
VALUES = MAT + FIELDS
ROW_FLAG = VALUES
ROW_MATE = VALUES + 1
WIDTH = 32
BOTH_LANES = (((1,), (1,)), ((), ()))
AXES = ("scan", "grp")


def div(x, n):
    if n & (n - 1) == 0:
        return lax.shift_right_logical(x, jnp.int32(n.bit_length() - 1))
    return x // n


def mod(x, n):
    if n & (n - 1) == 0:
        return x & (n - 1)
    return x % n


def iota(shape, dim):
    return lax.broadcasted_iota(jnp.int32, shape, dim)


def pieces(x, count):
    parts = []
    for _ in range(count - 1):
        part = x.astype(jnp.bfloat16)
        parts.append(part)
        x = x - part.astype(jnp.float32)
    parts.append(x.astype(jnp.bfloat16))
    return parts


def dot(a, b, dims=(((1,), (0,)), ((), ()))):
    return lax.dot_general(a, b, dims, preferred_element_type=jnp.float32)


def sizes(samples_shape, entries_shape, devices):
    scan_local, _, tiles, _ = samples_shape
    per_scan = entries_shape[1]
    entries = scan_local * per_scan
    cap = 2 * entries // devices
    return scan_local, tiles, per_scan, entries, cap, (COORDS + 1) * cap + 1


def send_kernel(devices, groups, group_ref, count_ref, samples_ref, scan_ref, tile_ref, src_ref, out_ref, data_ref):
    scan_local, tiles, per_scan, entries, cap, block = sizes(samples_ref.shape, scan_ref.shape, devices)
    group_points = tiles * LANES

    def one_scan(s, carry):
        first = group_ref[0] * group_points
        limit = count_ref[s] - first
        for h in range(per_scan // 8):
            ids = src_ref[s, pl.ds(h * 8, 8), :]
            lane = mod(ids, LANES)
            tile = div(ids, LANES)
            found = [jnp.zeros((8, LANES), jnp.float32) for _ in range(COORDS)]
            for t in range(tiles):
                here = tile == t
                for a in range(COORDS):
                    row = jnp.broadcast_to(samples_ref[s, a, t : t + 1, :], (8, LANES))
                    found[a] = jnp.where(here, jnp.take_along_axis(row, lane, axis=1), found[a])
            at = pl.multiple_of(s * per_scan + h * 8, 8)
            for a in range(COORDS):
                data_ref[a, pl.ds(at, 8), :] = found[a]
            data_ref[COORDS, pl.ds(at, 8), :] = (ids < limit).astype(jnp.float32)
        return carry

    lax.fori_loop(0, scan_local, one_scan, 0)

    scans = scan_ref[...]
    tile_ids = tile_ref[...]
    device = div(scans, scan_local) * groups + div(tile_ids, tiles)
    stacked = jnp.concatenate(
        [device.astype(jnp.float32), mod(scans, scan_local).astype(jnp.float32), mod(tile_ids, tiles).astype(jnp.float32)],
        axis=0,
    ).astype(jnp.bfloat16)
    spread = (mod(iota((per_scan, entries), 1), per_scan) == iota((per_scan, entries), 0)).astype(jnp.float32)
    wide = dot(stacked, spread.astype(jnp.bfloat16))
    own = div(iota((scan_local, entries), 1), per_scan) == iota((scan_local, entries), 0)
    device_row, mate_row, tile_row = [
        jnp.sum(jnp.where(own, wide[f * scan_local : (f + 1) * scan_local], 0.0), axis=0, keepdims=True)
        for f in range(3)
    ]
    rank_parts = []
    columns = []
    for h in range(entries // LANES):
        across = device_row[:, h * LANES : (h + 1) * LANES]
        columns.append(jnp.broadcast_to(across, (LANES, LANES)).T)
        total = jnp.zeros((1, LANES), jnp.float32)
        for g in range(h + 1):
            same = columns[g] == across
            if g == h:
                same = same & (iota((LANES, LANES), 0) < iota((LANES, LANES), 1))
            total = total + jnp.sum(same.astype(jnp.float32), axis=0, keepdims=True)
        rank_parts.append(total)
    rank_row = jnp.concatenate(rank_parts, axis=1)
    slot_row = (device_row * cap + rank_row).astype(jnp.int32)
    place = (iota((devices * cap, entries), 0) == slot_row).astype(jnp.float32).astype(jnp.bfloat16)
    for a in range(COORDS + 1):
        values = data_ref[a]
        if a < COORDS:
            parts = [dot(place, part) for part in pieces(values, 3)]
            moved = (parts[0] + parts[1]) + parts[2]
        else:
            moved = dot(place, values.astype(jnp.bfloat16))
        for d in range(devices):
            out_ref[pl.ds(d * block + a * cap, cap), :] = moved[d * cap : (d + 1) * cap]
    owner_row = (div(iota((1, entries), 1), per_scan) + 1).astype(jnp.float32)
    field = div(iota((LANES, entries), 0), cap)
    picked = jnp.where(field == 0, owner_row, jnp.where(field == 1, mate_row, tile_row))
    picked = jnp.where(
        (mod(iota((LANES, entries), 0), cap).astype(jnp.float32) == rank_row) & (field < 3), picked, 0.0
    ).astype(jnp.bfloat16)
    towards = (iota((devices, entries), 0).astype(jnp.float32) == device_row).astype(jnp.float32).astype(jnp.bfloat16)
    notes = dot(towards, picked, BOTH_LANES)
    for d in range(devices):
        out_ref[pl.ds(d * block + (COORDS + 1) * cap, 1), :] = notes[d : d + 1]


def pair_kernel(devices, group_ref, count_ref, samples_ref, recv_ref, flat_ref, pack_ref, point_ref, mate_ref, note_ref, wide_ref):
    scan_local, _, tiles, _ = samples_ref.shape
    slots = flat_ref.shape[1]
    cap = slots // devices
    block = (COORDS + 1) * cap + 1
    for d in range(devices):
        note_ref[pl.ds(d, 1), :] = recv_ref[pl.ds(d * block + (COORDS + 1) * cap, 1), :]
    notes = note_ref[...].astype(jnp.bfloat16)
    mine = div(iota((devices, slots), 1), cap) == iota((devices, slots), 0)
    rows = []
    for f in range(3):
        spread = (iota((LANES, slots), 0) == mod(iota((LANES, slots), 1), cap) + f * cap).astype(jnp.float32)
        rows.append(
            jnp.sum(jnp.where(mine, dot(notes, spread.astype(jnp.bfloat16)), 0.0), axis=0, keepdims=True)
        )
    flag_row, mate_row, tile_row = rows
    code_row = (mate_row * tiles + tile_row).astype(jnp.int32)
    table = scan_local * tiles
    chosen = (iota((table, slots), 0) == code_row).astype(jnp.float32).astype(jnp.bfloat16)
    base = group_ref[0] * tiles
    point_ids = (base + iota((tiles, LANES), 0)) * LANES + iota((tiles, LANES), 1)
    for a in range(FIELDS):
        values = []
        for b in range(scan_local):
            value = samples_ref[b, a]
            if a >= COORDS:
                value = jnp.where(point_ids < count_ref[b], value, 0.0)
            values.append(value)
        values = jnp.concatenate(values, axis=0)
        turned = jnp.concatenate([values[h : h + LANES].T for h in range(0, table, LANES)], axis=1)
        parts = [dot(part, chosen) for part in pieces(turned, 3)]
        mate_ref[a] = (parts[0] + parts[1]) + parts[2]
    per_chunk = LANES // cap
    for c in range(slots // LANES):
        for a in range(COORDS + 1):
            stack = [
                recv_ref[pl.ds(d * block + a * cap, cap), :] for d in range(c * per_chunk, (c + 1) * per_chunk)
            ]
            point_ref[a, :, c * LANES : (c + 1) * LANES] = jnp.concatenate(stack, axis=0).T
    for c in range(slots // LANES):
        lanes = slice(c * LANES, (c + 1) * LANES)

        def step(k, sums):
            at = pl.ds(pl.multiple_of(k * 8, 8), 8)
            px, py, pz, mask = [point_ref[a, at, lanes] for a in range(COORDS + 1)]
            qx, qy, qz, nx, ny, nz = [mate_ref[a, at, lanes] for a in range(FIELDS)]
            residual = nx * (px - qx) + ny * (py - qy) + nz * (pz - qz)
            weight = mask / (1.0 + residual * residual)
            jac = [py * nz - pz * ny, pz * nx - px * nz, px * ny - py * nx, nx, ny, nz]
            scaled = [weight * j for j in jac]
            terms = [scaled[i] * jac[j] for i, j in PAIRS] + [residual * s for s in scaled]
            return tuple(s + t for s, t in zip(sums, terms))

        zero = jnp.zeros((8, LANES), jnp.float32)
        sums = lax.fori_loop(0, LANES // 8, step, (zero,) * VALUES)
        lines = [jnp.sum(s, axis=0, keepdims=True) for s in sums]
        lines += [flag_row[:, lanes], mate_row[:, lanes]]
        lines += [jnp.zeros((1, LANES), jnp.float32)] * (WIDTH - len(lines))
        flat = jnp.concatenate(lines, axis=0)
        flat_ref[:, lanes] = flat
        tall = jnp.concatenate([flat, jnp.zeros((LANES - WIDTH, LANES), jnp.float32)], axis=0)
        wide_ref[pl.ds(c * LANES, LANES), :] = tall.T
    per_row = LANES // WIDTH
    packed = wide_ref[pl.ds(0, slots // per_row, stride=per_row), :]
    for k in range(1, per_row):
        packed = packed + pltpu.roll(wide_ref[pl.ds(k, slots // per_row, stride=per_row), :], k * WIDTH, 1)
    pack_ref[...] = packed


def layout(scan_local, groups, scan_total):
    columns = scan_total // groups
    pack = max(1, LANES // columns)
    per_block = -(-(MAT + 1) // pack)
    return columns, pack, per_block


def join_kernel(devices, groups, scan_local, place_ref, flat_ref, back_ref, out_ref):
    slots = flat_ref.shape[1]
    cap = slots // devices
    per_row = LANES // WIDTH
    stride = slots // per_row
    scan_total = scan_local * (devices // groups)
    columns, pack, per_block = layout(scan_local, groups, scan_total)
    turned = back_ref[...].T
    every = jnp.concatenate([turned[k * WIDTH : (k + 1) * WIDTH] for k in range(per_row)] + [flat_ref[...]], axis=1)
    total = 2 * slots
    at = iota((1, total), 1)
    mine = at < slots
    slot = jnp.where(mine, mod(at, stride) * per_row + div(at, stride), at - slots)
    peer = div(div(slot, cap), groups) * scan_local
    flag = every[ROW_FLAG : ROW_FLAG + 1].astype(jnp.int32) - 1
    mate = every[ROW_MATE : ROW_MATE + 1].astype(jnp.int32)
    row = jnp.where(mine, flag, mate)
    other = peer + jnp.where(mine, mate, flag)
    own = place_ref[0] * scan_local + row
    row_hot = iota((scan_local, total), 0) == row
    column = iota((scan_total, total), 0)
    mix = ((column == own).astype(jnp.float32) - (column == other).astype(jnp.float32)).astype(jnp.bfloat16)
    high = every.astype(jnp.bfloat16).astype(jnp.float32)
    hess = None
    for part in (high, every - high):
        spread = jnp.concatenate(
            [jnp.where(row_hot, part[q : q + 1], 0.0).astype(jnp.bfloat16) for q in range(MAT)], axis=0
        )
        piece = dot(spread, mix, BOTH_LANES)
        hess = piece if hess is None else hess + piece
    signed = jnp.where(mine, every, -every)
    lane = iota((scan_local, LANES), 1)
    home = MAT // per_block
    grad = jnp.zeros((scan_local, LANES), jnp.float32)
    for q in range(FIELDS):
        value = jnp.sum(jnp.where(row_hot, signed[MAT + q : MAT + q + 1], 0.0), axis=1, keepdims=True)
        grad = jnp.where(lane == home * columns + q, value, grad)
    rows = per_block * scan_local
    for c in range(groups):
        side, shift = divmod(c * columns, LANES)
        for r in range(per_block):
            tile = jnp.zeros((scan_local, LANES), jnp.float32)
            for k in range(pack):
                q = k * per_block + r
                if q < MAT:
                    value = hess[q * scan_local : (q + 1) * scan_local, side * LANES : (side + 1) * LANES]
                    turn = (k * columns - shift) % LANES
                    if turn:
                        value = pltpu.roll(value, turn, 1)
                elif q == MAT:
                    value = grad
                else:
                    continue
                if pack > 1:
                    value = jnp.where(div(lane, columns) == k, value, tile)
                tile = value
            out_ref[c, r * scan_local : (r + 1) * scan_local, :] = tile


def close_kernel(groups, group_ref, parts_ref, hess_ref, grad_ref, hold_ref):
    scan_local, columns = hess_ref.shape[1:]
    per_block = parts_ref.shape[1] // scan_local
    whole = parts_ref[0]
    for g in range(1, groups):
        whole = whole + parts_ref[g]
    for q in range(MAT + 1):
        k, r = divmod(q, per_block)
        tile = whole[r * scan_local : (r + 1) * scan_local, k * columns : (k + 1) * columns]
        if q < MAT:
            i, j = PAIRS[q]
            hess_ref[i * FIELDS + j] = tile
            if i != j:
                hess_ref[j * FIELDS + i] = tile
        else:
            hold_ref[:, 0:columns] = tile
    part = scan_local // groups
    grad_ref[...] = hold_ref[pl.ds(group_ref[0] * part, part), 0:FIELDS]


def call(kernel, out_shape, smem, vmem, scratch=()):
    return pl.pallas_call(
        kernel,
        out_shape=out_shape,
        in_specs=[pl.BlockSpec(memory_space=pltpu.SMEM)] * smem + [pl.BlockSpec(memory_space=pltpu.VMEM)] * vmem,
        scratch_shapes=list(scratch),
    )


def f32(*shape):
    return jax.ShapeDtypeStruct(shape, jnp.float32)


def exchange(x, axes):
    count, width = x.shape
    moved = lax.all_to_all(x.reshape(count, 1, width), axes, split_axis=0, concat_axis=0, tiled=True)
    return moved.reshape(count, width)


def local(samples, point_count, corr_scan, corr_tile, corr_src):
    devices = lax.axis_size(AXES)
    groups = lax.axis_size("grp")
    samples = samples.transpose(0, 2, 1, 3)
    scan_local, tiles, per_scan, entries, cap, block = sizes(samples.shape, corr_scan.shape, devices)
    slots = devices * cap
    scan_total = scan_local * (devices // groups)
    columns, pack, per_block = layout(scan_local, groups, scan_total)
    group = lax.axis_index("grp").astype(jnp.int32).reshape(1)
    scan = lax.axis_index("scan").astype(jnp.int32).reshape(1)
    bind = lambda kernel, *args: lambda *refs: kernel(*args, *refs)
    sent = call(
        bind(send_kernel, devices, groups),
        f32(devices * block, LANES),
        2,
        4,
        [pltpu.VMEM((COORDS + 1, entries, LANES), jnp.float32)],
    )(group, point_count, samples, corr_scan, corr_tile, corr_src)
    received = exchange(sent, AXES)
    flat, packed = call(
        bind(pair_kernel, devices),
        (f32(WIDTH, slots), f32(slots * WIDTH // LANES, LANES)),
        2,
        2,
        [
            pltpu.VMEM((COORDS + 1, LANES, slots), jnp.float32),
            pltpu.VMEM((FIELDS, LANES, slots), jnp.float32),
            pltpu.VMEM((devices, LANES), jnp.float32),
            pltpu.VMEM((slots, LANES), jnp.float32),
        ],
    )(group, point_count, samples, received)
    back = exchange(packed, AXES)
    shares = call(
        bind(join_kernel, devices, groups, scan_local), f32(groups, per_block * scan_local, LANES), 1, 2
    )(scan, flat, back)
    shares = lax.all_to_all(shares, "grp", split_axis=0, concat_axis=0, tiled=True)
    hess, grad = call(
        bind(close_kernel, groups),
        (f32(FIELDS * FIELDS, scan_local, columns), f32(scan_local // groups, FIELDS)),
        1,
        1,
        [pltpu.VMEM((scan_local, LANES), jnp.float32)],
    )(group, shares)
    return hess.reshape(FIELDS, FIELDS, scan_local, columns).transpose(2, 0, 1, 3), grad


def solution(mesh):
    placed = (
        P("scan", "grp", None, None),
        P("scan"),
        P("scan", "grp"),
        P("scan", "grp"),
        P("scan", "grp", None),
    )
    return jax.shard_map(
        local,
        mesh=mesh,
        in_specs=placed,
        out_specs=(P("scan", None, None, "grp"), P(AXES, None)),
        check_vma=False,
    )
```

time: 206 us -> 72.9 us (0.35)
  matrix products: 103 us -> 0 us
  blocking collectives: 5.95 us -> 45.2 us
  local copies, waits for them, and re-layouts: 37.9 us -> 0.62 us
  starting transfers between devices: 18.8 us -> 2.57 us
  Pallas kernels: 0 us -> 16.1 us
  between operations: 15.2 us -> 0.65 us
  waiting for transfers between devices: 18.1 us -> 7.4 us
  other arithmetic: 4.39 us -> 0 us
    dot_general x20 -> x0, matrix products: 103 us -> none  [the longest x16 95.4 us: one_block(): jnp.dot(position, selector, precision=lax.Precision.HIGHEST, preferred_el...]
    all_to_all x0 -> x2, blocking collectives: none -> 45.2 us  [the longest x1 35.8 us: exchange(): lax.all_to_all(x.reshape(count, 1, width), axes, split_axis=0, concat_axi...]
    pallas_call x0 -> x4, Pallas kernels: none -> 16.1 us  [the longest x1 6.07 us: local(): call(bind(send_kernel, devices, groups), f32(devices * block, LANES), 2,...]
    all_to_all x4 -> x1, starting transfers between devices: 18.6 us -> 2.57 us  [exchange(): lax.all_to_all(x.reshape(count, 1, width), axes, split_axis=0, concat_axi...]
    all_to_all x4 -> x1, waiting for transfers between devices: 18.1 us -> 7.4 us  [exchange(): lax.all_to_all(x.reshape(count, 1, width), axes, split_axis=0, concat_axi...]
    reshape x13 -> x0, local copies, waits for them, and re-layouts: 8.18 us -> none  [the longest x3 2.41 us: local(): target_scan = corr_scan.reshape(-1)]
    gather x4 -> x0, local copies, waits for them, and re-layouts: 7.65 us -> none  [the longest x2 3.43 us: masked_tiles(): limits = point_count[scan_local]]
    unnamed x36 -> x2, local copies, waits for them, and re-layouts: 8.17 us -> 0.62 us
  transfers between devices with their start and end apart: 5 -> 1, of which waited for: 3 -> 1; matrix products, arithmetic and copies ran while one was open for 52% -> 0% of each run, Pallas kernels for 0% -> 0%
where the time goes in v1:
time: 72.9 us; the launch traced here: 72.5 us
  blocking collectives  45.2 us (62%)
  Pallas kernels  16.1 us (22%)
  waiting for transfers between devices  7.4 us (10%)
  starting transfers between devices  2.57 us (4%)
    all_to_all x1, blocking collectives, exchange(): lax.all_to_all(x.reshape(count, 1, width), axes, split_axis=0, concat_axi...  35.8 us
    all_to_all x1, blocking collectives, local(): lax.all_to_all(shares, 'grp', split_axis=0, concat_axis=0, tiled=True)  9.35 us
    all_to_all x1, waiting for transfers between devices, exchange(): lax.all_to_all(x.reshape(count, 1, width), axes, split_axis=0, concat_axi...  7.4 us
    pallas_call x1, Pallas kernels, local(): call(bind(send_kernel, devices, groups), f32(devices * block, LANES), 2,...  6.07 us
    pallas_call x1, Pallas kernels, local(): call(bind(pair_kernel, devices), (f32(WIDTH, slots), f32(slots * WIDTH //...  5.95 us
    all_to_all x1, starting transfers between devices, exchange(): lax.all_to_all(x.reshape(count, 1, width), axes, split_axis=0, concat_axi...  2.57 us
    pallas_call x1, Pallas kernels, local(): call(bind(join_kernel, devices, groups, scan_local), f32(groups, per_bloc...  2.31 us
    pallas_call x1, Pallas kernels, local(): call(bind(close_kernel, groups), (f32(FIELDS * FIELDS, scan_local, column...  1.75 us
  transfers between devices with their start and end apart: 1, of which 1 were waited for; matrix products, arithmetic and copies ran while one was open for 0% of the time, Pallas kernels for 0%

profile of v1, /device:TPU:0, one launch (start us, length us, event | category | flops | bytes accessed | tf_op | source)
XLA Modules:
  0.0 72.5 jit_solution(18365657751564225583)
XLA Ops:
  0.6 6.1 %shard_map.68 = f32[2080,128]{1,0:T(8,128)} custom-call(s32[1]{0:T(128)} %bitcast.refs_0_, s32[16]{0:T(128)} %refs_1_.3, f32[16,6,16,128]{3,2,1,0:T(8,128)} %bitcast.16, s32[16,16]{1,0:T(8,128)} %refs_3_.1, s32[16,16]{1,0:T(8,128)} %refs_4_.1, s32[16,16,128]{2,1,0:T(8,128)} %refs_5_.1), custom_call_target="tpu_custom_call" | custom-call | tf_op jit(solution)/shard_map/pallas_call | solution.py:319
  6.7 35.8 %all_to_all.15 = f32[2080,1,128]{2,1,0:T(1,128)} all-to-all(f32[2080,1,128]{2,1,0:T(1,128)} %bitcast.15), channel_id=1, replica_groups=mesh['scan'=8,'grp'=4] {'scan','grp'}, dimensions={0} | all-to-all | bytes 2129920 | tf_op jit(solution)/shard_map/all_to_all | solution.py:304
  42.5 5.9 %shard_map.69 = (f32[32,512]{1,0:T(8,128)}, f32[128,128]{1,0:T(8,128)}) custom-call(s32[1]{0:T(128)} %bitcast.refs_0_, s32[16]{0:T(128)} %refs_1_.3, f32[16,6,16,128]{3,2,1,0:T(8,128)} %bitcast.17, f32[2080,128]{1,0:T(8,128)} %bitcast.14), custom_call_target="tpu_custom_call" | custom-call | tf_op jit(solution)/shard_map/pallas_call | solution.py:327
  48.5 2.6 %all-to-all-start.1 = ((f32[128,1,128]{2,1,0:T(1,128)}), f32[128,1,128]{2,1,0:T(1,128)S(1)}, u32[]{:S(2)}, u32[]{:S(2)}) async-start(f32[128,1,128]{2,1,0:T(1,128)} %bitcast.19), calls=%async_computation.1 | async-start | bytes 131072 | tf_op jit(solution)/shard_map/all_to_all | solution.py:304
  51.0 7.4 %all-to-all-done.1 = f32[128,1,128]{2,1,0:T(1,128)S(1)} async-done(((f32[128,1,128]{2,1,0:T(1,128)}), f32[128,1,128]{2,1,0:T(1,128)S(1)}, u32[]{:S(2)}, u32[]{:S(2)}) %all-to-all-start.1) | async-done | bytes 65568 | tf_op jit(solution)/shard_map/all_to_all | solution.py:304
  58.4 0.0 copy-start
  58.4 0.6 copy-done
  59.1 2.3 %shard_map.70 = f32[4,96,128]{2,1,0:T(8,128)} custom-call(s32[1]{0:T(128)} %bitcast.1.refs_0_, f32[32,512]{1,0:T(8,128)} %get-tuple-element.6.refs_1_, f32[128,128]{1,0:T(8,128)} %bitcast.18), custom_call_target="tpu_custom_call" | custom-call | tf_op jit(solution)/shard_map/pallas_call | solution.py:340
  61.4 9.4 %all_to_all.16.refs_1_ = f32[4,96,128]{2,1,0:T(8,128)} all-to-all(f32[4,96,128]{2,1,0:T(8,128)} %shard_map.70), channel_id=1, replica_groups=mesh['scan'=8,'grp'=4] {'grp'}, dimensions={0} | all-to-all | bytes 393216 | tf_op jit(solution)/shard_map/all_to_all | solution.py:343
  70.7 1.7 %shard_map.71 = (f32[36,16,32]{2,1,0:T(8,128)}, f32[4,6]{1,0:T(4,128)}) custom-call(s32[1]{0:T(128)} %bitcast.refs_0_, f32[4,96,128]{2,1,0:T(8,128)} %all_to_all.16.refs_1_), custom_call_target="tpu_custom_call" | custom-call | tf_op jit(solution)/shard_map/pallas_call | solution.py:344
Async XLA Ops:
  48.5 10.0 %all-to-all-start.1 = ((f32[128,1,128]{2,1,0:T(1,128)}), f32[128,1,128]{2,1,0:T(1,128)S(1)}, u32[]{:S(2)}, u32[]{:S(2)}) async-start(f32[128,1,128]{2,1,0:T(1,128)} %bitcast.19), calls=%async_computation.1 | async-start | bytes 131072 | tf_op jit(solution)/shard_map/all_to_all | solution.py:304
  58.4 0.6 copy-start

commit v2 on v1

--- a/solution.py
+++ b/solution.py
@@ -10,9 +10,9 @@
 FIELDS = 6
 PAIRS = [(i, j) for i in range(FIELDS) for j in range(i, FIELDS)]
 MAT = len(PAIRS)
-VALUES = MAT + FIELDS
-ROW_FLAG = VALUES
-ROW_MATE = VALUES + 1
+ROW_FLAG = MAT
+ROW_MATE = MAT + 1
+HEAD = MAT + 3
 WIDTH = 32
 BOTH_LANES = (((1,), (1,)), ((), ()))
 AXES = ("scan", "grp")
@@ -131,7 +131,21 @@
         out_ref[pl.ds(d * block + (COORDS + 1) * cap, 1), :] = notes[d : d + 1]
 
 
-def pair_kernel(devices, group_ref, count_ref, samples_ref, recv_ref, flat_ref, pack_ref, point_ref, mate_ref, note_ref, wide_ref):
+def turn(x, amount):
+    amount = amount % LANES
+    return pltpu.roll(x, amount, 1) if amount else x
+
+
+def back_layout(scan_local, groups, cap):
+    span = groups * cap
+    return span, HEAD * span // LANES, WIDTH * scan_local // LANES
+
+
+def partner(index, k, groups):
+    return index ^ k if groups & (groups - 1) == 0 else (index + k) % groups
+
+
+def pair_kernel(devices, groups, group_ref, count_ref, samples_ref, recv_ref, flat_ref, back_ref, point_ref, mate_ref, note_ref):
     scan_local, _, tiles, _ = samples_ref.shape
     slots = flat_ref.shape[1]
     cap = slots // devices
@@ -185,19 +199,37 @@
             return tuple(s + t for s, t in zip(sums, terms))
 
         zero = jnp.zeros((8, LANES), jnp.float32)
-        sums = lax.fori_loop(0, LANES // 8, step, (zero,) * VALUES)
+        sums = lax.fori_loop(0, LANES // 8, step, (zero,) * (MAT + FIELDS))
         lines = [jnp.sum(s, axis=0, keepdims=True) for s in sums]
-        lines += [flag_row[:, lanes], mate_row[:, lanes]]
-        lines += [jnp.zeros((1, LANES), jnp.float32)] * (WIDTH - len(lines))
-        flat = jnp.concatenate(lines, axis=0)
-        flat_ref[:, lanes] = flat
-        tall = jnp.concatenate([flat, jnp.zeros((LANES - WIDTH, LANES), jnp.float32)], axis=0)
-        wide_ref[pl.ds(c * LANES, LANES), :] = tall.T
-    per_row = LANES // WIDTH
-    packed = wide_ref[pl.ds(0, slots // per_row, stride=per_row), :]
-    for k in range(1, per_row):
-        packed = packed + pltpu.roll(wide_ref[pl.ds(k, slots // per_row, stride=per_row), :], k * WIDTH, 1)
-    pack_ref[...] = packed
+        blank = jnp.zeros((1, LANES), jnp.float32)
+        lines[MAT:MAT] = [flag_row[:, lanes], mate_row[:, lanes], blank]
+        lines += [blank] * (WIDTH - len(lines))
+        flat_ref[:, lanes] = jnp.concatenate(lines, axis=0)
+    scans = devices // groups
+    span, slot_rows, sum_rows = back_layout(scan_local, groups, cap)
+    source = div(div(iota((1, slots), 1), cap), groups) * scan_local + flag_row.astype(jnp.int32) - 1
+    source = jnp.where(flag_row > 0.0, source, -1)
+    source_hot = (iota((scans * scan_local, slots), 0) == source).astype(jnp.float32).astype(jnp.bfloat16)
+    parts = [dot(part, source_hot, BOTH_LANES) for part in pieces(flat_ref[...], 3)]
+    sums = (parts[0] + parts[1]) + parts[2]
+    slot_lane = div(iota((slot_rows, LANES), 1), span)
+    sum_lane = div(iota((sum_rows, LANES), 1), scan_local)
+    for scan in range(scans):
+        c, start = divmod(scan * span, LANES)
+        body = None
+        for i in range(LANES // span):
+            piece = flat_ref[i * slot_rows : (i + 1) * slot_rows, c * LANES : (c + 1) * LANES]
+            piece = turn(piece, i * span - start)
+            body = piece if i == 0 else jnp.where(slot_lane == i, piece, body)
+        c, start = divmod(scan * scan_local, LANES)
+        tail = None
+        for i in range(WIDTH // sum_rows):
+            piece = turn(sums[i * sum_rows : (i + 1) * sum_rows, c * LANES : (c + 1) * LANES], i * scan_local - start)
+            tail = piece if i == 0 else jnp.where(sum_lane == i, piece, tail)
+        for c in range(groups):
+            at = (scan * groups + c) * (slot_rows + sum_rows)
+            back_ref[at : at + slot_rows, :] = body
+            back_ref[at + slot_rows : at + slot_rows + sum_rows, :] = tail
 
 
 def layout(scan_local, groups, scan_total):
@@ -207,44 +239,34 @@
     return columns, pack, per_block
 
 
-def join_kernel(devices, groups, scan_local, place_ref, flat_ref, back_ref, out_ref):
+def block_rows(every, row_hot, count):
+    high = every.astype(jnp.bfloat16).astype(jnp.float32)
+    for part in (high, every - high):
+        yield jnp.concatenate(
+            [jnp.where(row_hot, part[q : q + 1], 0.0).astype(jnp.bfloat16) for q in range(count)], axis=0
+        )
+
+
+def held_kernel(devices, groups, scan_local, place_ref, flat_ref, *refs):
+    out_refs, stage_ref = refs[:-1], refs[-1]
     slots = flat_ref.shape[1]
     cap = slots // devices
-    per_row = LANES // WIDTH
-    stride = slots // per_row
     scan_total = scan_local * (devices // groups)
     columns, pack, per_block = layout(scan_local, groups, scan_total)
-    turned = back_ref[...].T
-    every = jnp.concatenate([turned[k * WIDTH : (k + 1) * WIDTH] for k in range(per_row)] + [flat_ref[...]], axis=1)
-    total = 2 * slots
-    at = iota((1, total), 1)
-    mine = at < slots
-    slot = jnp.where(mine, mod(at, stride) * per_row + div(at, stride), at - slots)
-    peer = div(div(slot, cap), groups) * scan_local
-    flag = every[ROW_FLAG : ROW_FLAG + 1].astype(jnp.int32) - 1
-    mate = every[ROW_MATE : ROW_MATE + 1].astype(jnp.int32)
-    row = jnp.where(mine, flag, mate)
-    other = peer + jnp.where(mine, mate, flag)
+    every = flat_ref[...]
+    row = every[ROW_MATE : ROW_MATE + 1].astype(jnp.int32)
+    other = div(div(iota((1, slots), 1), cap), groups) * scan_local + every[ROW_FLAG : ROW_FLAG + 1].astype(jnp.int32) - 1
     own = place_ref[0] * scan_local + row
-    row_hot = iota((scan_local, total), 0) == row
-    column = iota((scan_total, total), 0)
+    row_hot = iota((scan_local, slots), 0) == row
+    column = iota((scan_total, slots), 0)
     mix = ((column == own).astype(jnp.float32) - (column == other).astype(jnp.float32)).astype(jnp.bfloat16)
-    high = every.astype(jnp.bfloat16).astype(jnp.float32)
-    hess = None
-    for part in (high, every - high):
-        spread = jnp.concatenate(
-            [jnp.where(row_hot, part[q : q + 1], 0.0).astype(jnp.bfloat16) for q in range(MAT)], axis=0
-        )
-        piece = dot(spread, mix, BOTH_LANES)
-        hess = piece if hess is None else hess + piece
-    signed = jnp.where(mine, every, -every)
+    hess = sum(dot(rows, mix, BOTH_LANES) for rows in block_rows(every, row_hot, MAT))
     lane = iota((scan_local, LANES), 1)
     home = MAT // per_block
     grad = jnp.zeros((scan_local, LANES), jnp.float32)
     for q in range(FIELDS):
-        value = jnp.sum(jnp.where(row_hot, signed[MAT + q : MAT + q + 1], 0.0), axis=1, keepdims=True)
-        grad = jnp.where(lane == home * columns + q, value, grad)
-    rows = per_block * scan_local
+        value = jnp.sum(jnp.where(row_hot, every[HEAD + q : HEAD + q + 1], 0.0), axis=1, keepdims=True)
+        grad = jnp.where(lane == home * columns + q, -value, grad)
     for c in range(groups):
         side, shift = divmod(c * columns, LANES)
         for r in range(per_block):
@@ -253,37 +275,74 @@
                 q = k * per_block + r
                 if q < MAT:
                     value = hess[q * scan_local : (q + 1) * scan_local, side * LANES : (side + 1) * LANES]
-                    turn = (k * columns - shift) % LANES
-                    if turn:
-                        value = pltpu.roll(value, turn, 1)
+                    value = turn(value, k * columns - shift)
                 elif q == MAT:
                     value = grad
                 else:
                     continue
-                if pack > 1:
-                    value = jnp.where(div(lane, columns) == k, value, tile)
-                tile = value
-            out_ref[c, r * scan_local : (r + 1) * scan_local, :] = tile
-
-
-def close_kernel(groups, group_ref, parts_ref, hess_ref, grad_ref, hold_ref):
+                tile = jnp.where(div(lane, columns) == k, value, tile) if pack > 1 else value
+            stage_ref[c, r * scan_local : (r + 1) * scan_local, :] = tile
+    for k, out_ref in enumerate(out_refs):
+        out_ref[...] = stage_ref[partner(place_ref[1], k, groups)]
+
+
+def close_kernel(devices, groups, cap, place_ref, back_ref, *refs):
+    part_refs, (hess_ref, grad_ref, every_ref, hold_ref) = refs[:groups], refs[groups:]
     scan_local, columns = hess_ref.shape[1:]
-    per_block = parts_ref.shape[1] // scan_local
-    whole = parts_ref[0]
-    for g in range(1, groups):
-        whole = whole + parts_ref[g]
-    for q in range(MAT + 1):
+    per_block = part_refs[0].shape[0] // scan_local
+    span, slot_rows, sum_rows = back_layout(scan_local, groups, cap)
+    block = slot_rows + sum_rows
+    senders = devices // groups
+    first = place_ref[1] * (senders * block)
+    lane_block = div(iota((slot_rows, LANES), 1), span)
+    per_chunk = LANES // span
+    for chunk in range(senders // per_chunk):
+        found = [back_ref[pl.ds(first + (chunk * per_chunk + u) * block, slot_rows), :] for u in range(per_chunk)]
+        for i in range(LANES // span):
+            tile = None
+            for u in range(per_chunk):
+                piece = turn(found[u], (u - i) * span)
+                tile = piece if u == 0 else jnp.where(lane_block == u, piece, tile)
+            every_ref[i * slot_rows : (i + 1) * slot_rows, chunk * LANES : (chunk + 1) * LANES] = tile
+    every = every_ref[...]
+    total = every.shape[1]
+    row = every[ROW_FLAG : ROW_FLAG + 1].astype(jnp.int32) - 1
+    mate = every[ROW_MATE : ROW_MATE + 1].astype(jnp.int32)
+    column = div(div(iota((1, total), 1), span), groups) * scan_local + mate
+    row_hot = iota((scan_local, total), 0) == row
+    mix = (iota((columns, total), 0) == column).astype(jnp.float32).astype(jnp.bfloat16)
+    cross = sum(dot(rows, mix, BOTH_LANES) for rows in block_rows(every, row_hot, MAT))
+    sums = back_ref[slot_rows:block, :]
+    for d in range(1, devices):
+        sums = sums + back_ref[d * block + slot_rows : (d + 1) * block, :]
+    line = iota((scan_local, LANES), 0)
+    lane = iota((scan_local, LANES), 1)
+
+    def by_row(q):
+        i, r = divmod(q, sum_rows)
+        return jnp.sum(jnp.where(lane == line + i * scan_local, sums[r : r + 1], 0.0), axis=1, keepdims=True)
+
+    whole = part_refs[0][...]
+    for part_ref in part_refs[1:]:
+        whole = whole + part_ref[...]
+    offset = place_ref[0] * scan_local - place_ref[1] * columns
+    diagonal = iota((scan_local, columns), 1) == iota((scan_local, columns), 0) + offset
+    for q in range(MAT):
         k, r = divmod(q, per_block)
         tile = whole[r * scan_local : (r + 1) * scan_local, k * columns : (k + 1) * columns]
-        if q < MAT:
-            i, j = PAIRS[q]
-            hess_ref[i * FIELDS + j] = tile
-            if i != j:
-                hess_ref[j * FIELDS + i] = tile
-        else:
-            hold_ref[:, 0:columns] = tile
+        tile = tile - cross[q * scan_local : (q + 1) * scan_local]
+        tile = tile + jnp.where(diagonal, by_row(q), 0.0)
+        i, j = PAIRS[q]
+        hess_ref[i * FIELDS + j] = tile
+        if i != j:
+            hess_ref[j * FIELDS + i] = tile
+    k, r = divmod(MAT, per_block)
+    grad = turn(whole[r * scan_local : (r + 1) * scan_local], -k * columns)
+    for q in range(FIELDS):
+        grad = grad + jnp.where(lane == q, by_row(HEAD + q), 0.0)
+    hold_ref[...] = grad
     part = scan_local // groups
-    grad_ref[...] = hold_ref[pl.ds(group_ref[0] * part, part), 0:FIELDS]
+    grad_ref[...] = hold_ref[pl.ds(place_ref[1] * part, part), 0:FIELDS]
 
 
 def call(kernel, out_shape, smem, vmem, scratch=()):
@@ -313,9 +372,14 @@
     slots = devices * cap
     scan_total = scan_local * (devices // groups)
     columns, pack, per_block = layout(scan_local, groups, scan_total)
-    group = lax.axis_index("grp").astype(jnp.int32).reshape(1)
-    scan = lax.axis_index("scan").astype(jnp.int32).reshape(1)
-    bind = lambda kernel, *args: lambda *refs: kernel(*args, *refs)
+    group = lax.axis_index("grp").astype(jnp.int32)
+    place = jnp.stack([lax.axis_index("scan").astype(jnp.int32), group])
+    group = group.reshape(1)
+    _, slot_rows, sum_rows = back_layout(scan_local, groups, cap)
+
+    def bind(kernel, *args):
+        return lambda *refs: kernel(*args, *refs)
+
     sent = call(
         bind(send_kernel, devices, groups),
         f32(devices * block, LANES),
@@ -324,30 +388,39 @@
         [pltpu.VMEM((COORDS + 1, entries, LANES), jnp.float32)],
     )(group, point_count, samples, corr_scan, corr_tile, corr_src)
     received = exchange(sent, AXES)
-    flat, packed = call(
-        bind(pair_kernel, devices),
-        (f32(WIDTH, slots), f32(slots * WIDTH // LANES, LANES)),
+    flat, back = call(
+        bind(pair_kernel, devices, groups),
+        (f32(WIDTH, slots), f32(devices * (slot_rows + sum_rows), LANES)),
         2,
         2,
         [
             pltpu.VMEM((COORDS + 1, LANES, slots), jnp.float32),
             pltpu.VMEM((FIELDS, LANES, slots), jnp.float32),
             pltpu.VMEM((devices, LANES), jnp.float32),
-            pltpu.VMEM((slots, LANES), jnp.float32),
         ],
     )(group, point_count, samples, received)
-    back = exchange(packed, AXES)
+    back = exchange(back, AXES)
+    share = f32(per_block * scan_local, LANES)
     shares = call(
-        bind(join_kernel, devices, groups, scan_local), f32(groups, per_block * scan_local, LANES), 1, 2
-    )(scan, flat, back)
-    shares = lax.all_to_all(shares, "grp", split_axis=0, concat_axis=0, tiled=True)
+        bind(held_kernel, devices, groups, scan_local),
+        (share,) * groups,
+        1,
+        1,
+        [pltpu.VMEM((groups,) + share.shape, jnp.float32)],
+    )(place, flat)
+    shares = [shares[0]] + [
+        lax.ppermute(shares[k], "grp", [(g, partner(g, k, groups)) for g in range(groups)]) for k in range(1, groups)
+    ]
     hess, grad = call(
-        bind(close_kernel, groups),
+        bind(close_kernel, devices, groups, cap),
         (f32(FIELDS * FIELDS, scan_local, columns), f32(scan_local // groups, FIELDS)),
         1,
-        1,
-        [pltpu.VMEM((scan_local, LANES), jnp.float32)],
-    )(group, shares)
+        1 + groups,
+        [
+            pltpu.VMEM((HEAD, (devices // groups) * groups * cap), jnp.float32),
+            pltpu.VMEM((scan_local, LANES), jnp.float32),
+        ],
+    )(place, back, *shares)
     return hess.reshape(FIELDS, FIELDS, scan_local, columns).transpose(2, 0, 1, 3), grad
 
 

time: 72.9 us -> 65.7 us (0.901)
  blocking collectives: 45.2 us -> 35.8 us
  starting transfers between devices: 2.57 us -> 4.45 us
  waiting for transfers between devices: 7.4 us -> 6.09 us
  Pallas kernels: 16.1 us -> 17 us
    all_to_all x1 -> x0, blocking collectives: 9.35 us -> none  [local(): lax.all_to_all(shares, 'grp', split_axis=0, concat_axis=0, tiled=True)]
    all_to_all x1, waiting for transfers between devices: 7.4 us -> 1.79 us  [exchange(): lax.all_to_all(x.reshape(count, 1, width), axes, split_axis=0, concat_axi...]
    ppermute x0 -> x3, waiting for transfers between devices: none -> 4.31 us  [local(): lax.ppermute(shares[k], 'grp', [(g, partner(g, k, groups)) for g in range...]
    ppermute x0 -> x3, starting transfers between devices: none -> 1.86 us  [local(): lax.ppermute(shares[k], 'grp', [(g, partner(g, k, groups)) for g in range...]
    pallas_call x3, Pallas kernels: 10 us -> 11 us  [the longest x1 5.95 us: local(): call(bind(pair_kernel, devices, groups), (f32(WIDTH, slots), f32(devices...]
  transfers between devices with their start and end apart: 1 -> 4, of which waited for: 1 -> 3; matrix products, arithmetic and copies ran while one was open for 0% -> 1% of each run, Pallas kernels for 0% -> 3%
where the time goes in v2:
time: 65.7 us; the launch traced here: 65.3 us
  blocking collectives  35.8 us (54%)
  Pallas kernels  17 us (26%)
  waiting for transfers between devices  6.09 us (9%)
  starting transfers between devices  4.45 us (7%)
  local copies, waits for them, and re-layouts  0.71 us (1%)
  between operations  0.66 us (1%)
    all_to_all x1, blocking collectives, exchange(): lax.all_to_all(x.reshape(count, 1, width), axes, split_axis=0, concat_axi...  35.8 us
    pallas_call x1, Pallas kernels, local(): call(bind(send_kernel, devices, groups), f32(devices * block, LANES), 2,...  6.03 us
    pallas_call x1, Pallas kernels, local(): call(bind(pair_kernel, devices, groups), (f32(WIDTH, slots), f32(devices...  5.95 us
    ppermute x3, waiting for transfers between devices, local(): lax.ppermute(shares[k], 'grp', [(g, partner(g, k, groups)) for g in range...  4.31 us
    pallas_call x1, Pallas kernels, local(): call(bind(close_kernel, devices, groups, cap), (f32(FIELDS * FIELDS, scan...  3.05 us
    all_to_all x1, starting transfers between devices, exchange(): lax.all_to_all(x.reshape(count, 1, width), axes, split_axis=0, concat_axi...  2.59 us
    pallas_call x1, Pallas kernels, local(): call(bind(held_kernel, devices, groups, scan_local), (share,) * groups, 1...  2.01 us
    ppermute x3, starting transfers between devices, local(): lax.ppermute(shares[k], 'grp', [(g, partner(g, k, groups)) for g in range...  1.86 us
  transfers between devices with their start and end apart: 4, of which 3 were waited for; matrix products, arithmetic and copies ran while one was open for 1% of the time, Pallas kernels for 3%

profile of v2, /device:TPU:0, one launch (start us, length us, event | category | flops | bytes accessed | tf_op | source)
XLA Modules:
  0.0 65.3 jit_solution(15171783096261882311)
XLA Ops:
  0.6 6.0 %shard_map.68 = f32[2080,128]{1,0:T(8,128)} custom-call(s32[1]{0:T(128)} %bitcast.1.refs_0_, s32[16]{0:T(128)} %refs_1_.3, f32[16,6,16,128]{3,2,1,0:T(8,128)} %bitcast.16, s32[16,16]{1,0:T(8,128)} %refs_3_.1, s32[16,16]{1,0:T(8,128)} %refs_4_.1, s32[16,16,128]{2,1,0:T(8,128)} %refs_5_.1), custom_call_target="tpu_custom_call" | custom-call | tf_op jit(solution)/shard_map/pallas_call | solution.py:383
  6.7 35.8 %all_to_all.10 = f32[2080,1,128]{2,1,0:T(1,128)} all-to-all(f32[2080,1,128]{2,1,0:T(1,128)} %bitcast.15), channel_id=1, replica_groups=mesh['scan'=8,'grp'=4] {'scan','grp'}, dimensions={0} | all-to-all | bytes 2129920 | tf_op jit(solution)/shard_map/all_to_all | solution.py:363
  42.5 6.0 %shard_map.69 = (f32[32,512]{1,0:T(8,128)}, f32[512,128]{1,0:T(8,128)}) custom-call(s32[1]{0:T(128)} %bitcast.1.refs_0_, s32[16]{0:T(128)} %refs_1_.3, f32[16,6,16,128]{3,2,1,0:T(8,128)} %bitcast.17, f32[2080,128]{1,0:T(8,128)} %bitcast.14), custom_call_target="tpu_custom_call" | custom-call | tf_op jit(solution)/shard_map/pallas_call | solution.py:391
  48.4 2.6 %all-to-all-start.1 = ((f32[512,1,128]{2,1,0:T(1,128)}), f32[512,1,128]{2,1,0:T(1,128)S(1)}, u32[]{:S(2)}, u32[]{:S(2)}) async-start(f32[512,1,128]{2,1,0:T(1,128)} %bitcast.19), calls=%async_computation.1 | async-start | bytes 524288 | tf_op jit(solution)/shard_map/all_to_all | solution.py:363
  51.0 0.6 pad_add_fusion.refs_0_
  51.6 2.0 %shard_map.70 = (f32[96,128]{1,0:T(8,128)}, f32[96,128]{1,0:T(8,128)}, f32[96,128]{1,0:T(8,128)}, f32[96,128]{1,0:T(8,128)}) custom-call(s32[2]{0:T(128)} %pad_add_fusion.refs_0_, f32[32,512]{1,0:T(8,128)} %get-tuple-element.11.refs_1_), custom_call_target="tpu_custom_call" | custom-call | tf_op jit(solution)/shard_map/pallas_call | solution.py:404
  53.6 0.1 collective-permute-start
  53.7 1.7 %collective-permute-start.1 = (f32[96,128]{1,0:T(8,128)}, f32[96,128]{1,0:T(8,128)S(1)}, u32[]{:S(2)}, u32[]{:S(2)}) collective-permute-start(f32[96,128]{1,0:T(8,128)} %get-tuple-element.14), channel_id=1, source_target_pairs={{0,2},{1,3},{2,0},{3,1},{4,6},{5,7},{6,4},{7,5},{8,10},{9,11},{10,... | collective-permute-start | bytes 147464 | tf_op jit(solution)/shard_map/ppermute | solution.py:412
  55.4 0.1 collective-permute-start.2
  55.5 0.0 collective-permute-done.refs_3_
  55.5 0.0 copy-start.1
  55.5 3.0 %collective-permute-done.1.refs_4_ = f32[96,128]{1,0:T(8,128)S(1)} collective-permute-done((f32[96,128]{1,0:T(8,128)}, f32[96,128]{1,0:T(8,128)S(1)}, u32[]{:S(2)}, u32[]{:S(2)}) %collective-permute-start.1) | collective-permute-done | bytes 49184 | tf_op jit(solution)/shard_map/ppermute | solution.py:412
  58.5 0.0 copy-start.2
  58.5 1.3 %collective-permute-done.2.refs_5_ = f32[96,128]{1,0:T(8,128)S(1)} collective-permute-done((f32[96,128]{1,0:T(8,128)}, f32[96,128]{1,0:T(8,128)S(1)}, u32[]{:S(2)}, u32[]{:S(2)}) %collective-permute-start.2) | collective-permute-done | bytes 49184 | tf_op jit(solution)/shard_map/ppermute | solution.py:412
  59.8 0.0 copy-start.3
  59.8 1.8 %all-to-all-done.1 = f32[512,1,128]{2,1,0:T(1,128)S(1)} async-done(((f32[512,1,128]{2,1,0:T(1,128)}), f32[512,1,128]{2,1,0:T(1,128)S(1)}, u32[]{:S(2)}, u32[]{:S(2)}) %all-to-all-start.1) | async-done | bytes 262176 | tf_op jit(solution)/shard_map/all_to_all | solution.py:363
  61.6 0.0 copy-start
  61.6 0.0 copy-done.1
  61.6 0.0 copy-done.2
  61.6 0.0 copy-done.3
  61.6 0.7 %copy-done = f32[512,1,128]{2,1,0:T(1,128)} copy-done((f32[512,1,128]{2,1,0:T(1,128)}, f32[512,1,128]{2,1,0:T(1,128)S(1)}, u32[]{:S(2)}) %copy-start) | copy-done | bytes 262168
  62.3 3.0 %shard_map.71 = (f32[36,16,32]{2,1,0:T(8,128)}, f32[4,6]{1,0:T(4,128)}) custom-call(s32[2]{0:T(128)} %pad_add_fusion.refs_0_, f32[512,128]{1,0:T(8,128)} %bitcast.18, f32[96,128]{1,0:T(8,128)} %get-tuple-element.12.refs_2_, f32[96,128]{1,0:T(8,128)} %copy-done.1, f32[96,128]{1,0:T(8,128)} %copy-done.2, f32[96,128]{1,0:T(8,128)} %copy-done.3), custom_call_target="tpu_custom_call" | custom-call | tf_op jit(solution)/shard_map/pallas_call | solution.py:414
Async XLA Ops:
  48.4 13.2 %all-to-all-start.1 = ((f32[512,1,128]{2,1,0:T(1,128)}), f32[512,1,128]{2,1,0:T(1,128)S(1)}, u32[]{:S(2)}, u32[]{:S(2)}) async-start(f32[512,1,128]{2,1,0:T(1,128)} %bitcast.19), calls=%async_computation.1 | async-start | bytes 524288 | tf_op jit(solution)/shard_map/all_to_all | solution.py:363
  53.6 1.9 %collective-permute-start = (f32[96,128]{1,0:T(8,128)}, f32[96,128]{1,0:T(8,128)S(1)}, u32[]{:S(2)}, u32[]{:S(2)}) collective-permute-start(f32[96,128]{1,0:T(8,128)} %get-tuple-element.13), channel_id=1, source_target_pairs={{0,1},{1,0},{2,3},{3,2},{4,5},{5,4},{6,7},{7,6},{8,9},{9,8},{10,11... | collective-permute-start | bytes 147464 | tf_op jit(solution)/shard_map/ppermute | solution.py:412
  53.7 4.7 %collective-permute-start.1 = (f32[96,128]{1,0:T(8,128)}, f32[96,128]{1,0:T(8,128)S(1)}, u32[]{:S(2)}, u32[]{:S(2)}) collective-permute-start(f32[96,128]{1,0:T(8,128)} %get-tuple-element.14), channel_id=1, source_target_pairs={{0,2},{1,3},{2,0},{3,1},{4,6},{5,7},{6,4},{7,5},{8,10},{9,11},{10,... | collective-permute-start | bytes 147464 | tf_op jit(solution)/shard_map/ppermute | solution.py:412
  55.4 4.4 %collective-permute-start.2 = (f32[96,128]{1,0:T(8,128)}, f32[96,128]{1,0:T(8,128)S(1)}, u32[]{:S(2)}, u32[]{:S(2)}) collective-permute-start(f32[96,128]{1,0:T(8,128)} %get-tuple-element.15), channel_id=1, source_target_pairs={{0,3},{1,2},{2,1},{3,0},{4,7},{5,6},{6,5},{7,4},{8,11},{9,10},{10,... | collective-permute-start | bytes 147464 | tf_op jit(solution)/shard_map/ppermute | solution.py:412
  55.5 6.1 %copy-start.1 = (f32[96,128]{1,0:T(8,128)}, f32[96,128]{1,0:T(8,128)S(1)}, u32[]{:S(2)}) copy-start(f32[96,128]{1,0:T(8,128)S(1)} %collective-permute-done.refs_3_) | copy-start | bytes 147460
  58.5 3.1 %copy-start.2 = (f32[96,128]{1,0:T(8,128)}, f32[96,128]{1,0:T(8,128)S(1)}, u32[]{:S(2)}) copy-start(f32[96,128]{1,0:T(8,128)S(1)} %collective-permute-done.1.refs_4_) | copy-start | bytes 147460
  59.8 1.8 %copy-start.3 = (f32[96,128]{1,0:T(8,128)}, f32[96,128]{1,0:T(8,128)S(1)}, u32[]{:S(2)}) copy-start(f32[96,128]{1,0:T(8,128)S(1)} %collective-permute-done.2.refs_5_) | copy-start | bytes 147460
  61.6 0.7 %copy-start = (f32[512,1,128]{2,1,0:T(1,128)}, f32[512,1,128]{2,1,0:T(1,128)S(1)}, u32[]{:S(2)}) copy-start(f32[512,1,128]{2,1,0:T(1,128)S(1)} %all-to-all-done.1) | copy-start | bytes 786436

commit v3 on v2

--- a/solution.py
+++ b/solution.py
@@ -346,16 +346,26 @@
 
 
 def call(kernel, out_shape, smem, vmem, scratch=()):
-    return pl.pallas_call(
+    body = pl.pallas_call(
         kernel,
         out_shape=out_shape,
         in_specs=[pl.BlockSpec(memory_space=pltpu.SMEM)] * smem + [pl.BlockSpec(memory_space=pltpu.VMEM)] * vmem,
         scratch_shapes=list(scratch),
     )
 
+    def run(*args):
+        args = args[:smem] + tuple(pltpu.with_memory_space_constraint(x, pltpu.VMEM) for x in args[smem:])
+        return body(*args)
+
+    return run
+
 
 def f32(*shape):
     return jax.ShapeDtypeStruct(shape, jnp.float32)
+
+
+def near(*shape):
+    return pltpu.VMEM(shape, jnp.float32)
 
 
 def exchange(x, axes):
@@ -382,7 +392,7 @@
 
     sent = call(
         bind(send_kernel, devices, groups),
-        f32(devices * block, LANES),
+        near(devices * block, LANES),
         2,
         4,
         [pltpu.VMEM((COORDS + 1, entries, LANES), jnp.float32)],
@@ -390,7 +400,7 @@
     received = exchange(sent, AXES)
     flat, back = call(
         bind(pair_kernel, devices, groups),
-        (f32(WIDTH, slots), f32(devices * (slot_rows + sum_rows), LANES)),
+        (near(WIDTH, slots), near(devices * (slot_rows + sum_rows), LANES)),
         2,
         2,
         [
@@ -400,7 +410,7 @@
         ],
     )(group, point_count, samples, received)
     back = exchange(back, AXES)
-    share = f32(per_block * scan_local, LANES)
+    share = near(per_block * scan_local, LANES)
     shares = call(
         bind(held_kernel, devices, groups, scan_local),
         (share,) * groups,

time: 65.7 us -> 65.5 us (level)
  Pallas kernels: 17 us -> 13.5 us
  local copies, waits for them, and re-layouts: 0.71 us -> 3.42 us
  waiting for transfers between devices: 6.09 us -> 6.88 us
    pallas_call x4, Pallas kernels: 17 us -> 13.5 us  [run(): return body(*args)]
    unnamed x8, local copies, waits for them, and re-layouts: 0.71 us -> 3.42 us
    all_to_all x1, waiting for transfers between devices: 1.79 us -> 2.58 us  [exchange(): lax.all_to_all(x.reshape(count, 1, width), axes, split_axis=0, concat_axi...]
  transfers between devices with their start and end apart: 4 -> 4, of which waited for: 3 -> 3; matrix products, arithmetic and copies ran while one was open for 1% -> 1% of each run, Pallas kernels for 3% -> 2%
where the time goes in v3:
time: 65.5 us; the launch traced here: 65.1 us
  blocking collectives  35.5 us (54%)
  Pallas kernels  13.5 us (21%)
  waiting for transfers between devices  6.88 us (11%)
  starting transfers between devices  4.51 us (7%)
  local copies, waits for them, and re-layouts  3.42 us (5%)
  between operations  0.68 us (1%)
    all_to_all x1, blocking collectives, exchange(): lax.all_to_all(x.reshape(count, 1, width), axes, split_axis=0, concat_axi...  35.5 us
    pallas_call x4, Pallas kernels, run(): return body(*args)  13.5 us
    ppermute x3, waiting for transfers between devices, local(): lax.ppermute(shares[k], 'grp', [(g, partner(g, k, groups)) for g in range...  4.29 us
    unnamed x8, local copies, waits for them, and re-layouts  3.42 us
    all_to_all x1, starting transfers between devices, exchange(): lax.all_to_all(x.reshape(count, 1, width), axes, split_axis=0, concat_axi...  2.59 us
    all_to_all x1, waiting for transfers between devices, exchange(): lax.all_to_all(x.reshape(count, 1, width), axes, split_axis=0, concat_axi...  2.58 us
    ppermute x3, starting transfers between devices, local(): lax.ppermute(shares[k], 'grp', [(g, partner(g, k, groups)) for g in range...  1.93 us
  transfers between devices with their start and end apart: 4, of which 3 were waited for; matrix products, arithmetic and copies ran while one was open for 1% of the time, Pallas kernels for 2%

profile of v3, /device:TPU:0, one launch (start us, length us, event | category | flops | bytes accessed | tf_op | source)
XLA Modules:
  0.0 65.1 jit_solution(1260531314704205021)
XLA Ops:
  0.6 0.0 copy-start
  0.6 1.1 %copy-done = f32[16,16,6,128]{3,1,2,0:T(8,128)S(1)} copy-done((f32[16,16,6,128]{3,1,2,0:T(8,128)S(1)}, f32[16,16,6,128]{3,1,2,0:T(8,128)}, u32[]{:S(2)}) %copy-start) | copy-done | bytes 786456
  1.8 0.0 copy-start.1
  1.8 0.9 %copy-done.1 = s32[16,16,128]{2,1,0:T(8,128)S(1)} copy-done((s32[16,16,128]{2,1,0:T(8,128)S(1)}, s32[16,16,128]{2,1,0:T(8,128)}, u32[]{:S(2)}) %copy-start.1) | copy-done | bytes 131096
  2.7 0.0 copy-start.2
  2.7 0.7 %copy-done.2 = s32[16,16]{1,0:T(8,128)S(1)} copy-done((s32[16,16]{1,0:T(8,128)S(1)}, s32[16,16]{1,0:T(8,128)}, u32[]{:S(2)}) %copy-start.2) | copy-done | bytes 1048
  3.4 0.0 copy-start.3
  3.4 0.7 %copy-done.3 = s32[16,16]{1,0:T(8,128)S(1)} copy-done((s32[16,16]{1,0:T(8,128)S(1)}, s32[16,16]{1,0:T(8,128)}, u32[]{:S(2)}) %copy-start.3) | copy-done | bytes 1048
  4.1 4.5 %shard_map.68 = f32[2080,128]{1,0:T(8,128)S(1)} custom-call(s32[1]{0:T(128)} %bitcast.1.refs_0_, s32[16]{0:T(128)} %refs_1_.3, f32[16,6,16,128]{3,2,1,0:T(8,128)S(1)} %bitcast.16, s32[16,16]{1,0:T(8,128)S(1)} %copy-done.2, s32[16,16]{1,0:T(8,128)S(1)} %copy-done.3, s32[16,16,128]{2,1,0:T(8,128)S(1)} %copy-done.1), custom_call_target="tpu_custom_call" | custom-call | tf_op jit(solution)/shard_map/pallas_call | solution.py:358
  8.6 35.5 %all_to_all.10 = f32[2080,1,128]{2,1,0:T(1,128)S(1)} all-to-all(f32[2080,1,128]{2,1,0:T(1,128)S(1)} %bitcast.15), channel_id=1, replica_groups=mesh['scan'=8,'grp'=4] {'scan','grp'}, dimensions={0} | all-to-all | bytes 2129920 | tf_op jit(solution)/shard_map/all_to_all | solution.py:373
  44.1 5.2 %shard_map.69 = (f32[32,512]{1,0:T(8,128)S(1)}, f32[512,128]{1,0:T(8,128)}) custom-call(s32[1]{0:T(128)} %bitcast.1.refs_0_, s32[16]{0:T(128)} %refs_1_.3, f32[16,6,16,128]{3,2,1,0:T(8,128)S(1)} %bitcast.17, f32[2080,128]{1,0:T(8,128)S(1)} %bitcast.14), custom_call_target="tpu_custom_call" | custom-call | tf_op jit(solution)/shard_map/pallas_call | solution.py:358
  49.2 2.6 %all-to-all-start.1 = ((f32[512,1,128]{2,1,0:T(1,128)}), f32[512,1,128]{2,1,0:T(1,128)S(1)}, u32[]{:S(2)}, u32[]{:S(2)}) async-start(f32[512,1,128]{2,1,0:T(1,128)} %bitcast.7), calls=%async_computation.1 | async-start | bytes 524288 | tf_op jit(solution)/shard_map/all_to_all | solution.py:373
  51.8 0.6 pad_add_fusion.refs_0_
  52.4 1.1 %shard_map.70 = (f32[96,128]{1,0:T(8,128)S(1)}, f32[96,128]{1,0:T(8,128)S(1)}, f32[96,128]{1,0:T(8,128)S(1)}, f32[96,128]{1,0:T(8,128)S(1)}) custom-call(s32[2]{0:T(128)} %pad_add_fusion.refs_0_, f32[32,512]{1,0:T(8,128)S(1)} %get-tuple-element.11.refs_1_), custom_call_target="tpu_custom_call" | custom-call | tf_op jit(solution)/shard_map/pallas_call | solution.py:358
  53.6 0.2 collective-permute-start
  53.8 1.7 %collective-permute-start.1 = (f32[96,128]{1,0:T(8,128)S(1)}, f32[96,128]{1,0:T(8,128)S(1)}, u32[]{:S(2)}, u32[]{:S(2)}) collective-permute-start(f32[96,128]{1,0:T(8,128)S(1)} %get-tuple-element.14), channel_id=1, source_target_pairs={{0,2},{1,3},{2,0},{3,1},{4,6},{5,7},{6,4},{7,5},{8,10},{9,11},{10,... | collective-permute-start | bytes 147464 | tf_op jit(solution)/shard_map/ppermute | solution.py:422
  55.4 0.1 collective-permute-start.2
  55.5 0.0 collective-permute-done.refs_3_
  55.5 3.4 %collective-permute-done.1.refs_4_ = f32[96,128]{1,0:T(8,128)S(1)} collective-permute-done((f32[96,128]{1,0:T(8,128)S(1)}, f32[96,128]{1,0:T(8,128)S(1)}, u32[]{:S(2)}, u32[]{:S(2)}) %collective-permute-start.1) | collective-permute-done | bytes 49184 | tf_op jit(solution)/shard_map/ppermute | solution.py:422
  58.9 0.9 %collective-permute-done.2.refs_5_ = f32[96,128]{1,0:T(8,128)S(1)} collective-permute-done((f32[96,128]{1,0:T(8,128)S(1)}, f32[96,128]{1,0:T(8,128)S(1)}, u32[]{:S(2)}, u32[]{:S(2)}) %collective-permute-start.2) | collective-permute-done | bytes 49184 | tf_op jit(solution)/shard_map/ppermute | solution.py:422
  59.8 2.6 %all-to-all-done.1 = f32[512,1,128]{2,1,0:T(1,128)S(1)} async-done(((f32[512,1,128]{2,1,0:T(1,128)}), f32[512,1,128]{2,1,0:T(1,128)S(1)}, u32[]{:S(2)}, u32[]{:S(2)}) %all-to-all-start.1) | async-done | bytes 262176 | tf_op jit(solution)/shard_map/all_to_all | solution.py:373
  62.4 2.7 %shard_map.71 = (f32[36,16,32]{2,1,0:T(8,128)}, f32[4,6]{1,0:T(4,128)}) custom-call(s32[2]{0:T(128)} %pad_add_fusion.refs_0_, f32[512,128]{1,0:T(8,128)S(1)} %bitcast.18, f32[96,128]{1,0:T(8,128)S(1)} %get-tuple-element.12.refs_2_, f32[96,128]{1,0:T(8,128)S(1)} %collective-permute-done.refs_3_, f32[96,128]{1,0:T(8,128)S(1)} %collective-permute-done.1.refs_4_, ...), custom_call_target="tpu_custom_call" | custom-call | tf_op jit(solution)/shard_map/pallas_call | solution.py:358
Async XLA Ops:
  0.6 1.1 %copy-start = (f32[16,16,6,128]{3,1,2,0:T(8,128)S(1)}, f32[16,16,6,128]{3,1,2,0:T(8,128)}, u32[]{:S(2)}) copy-start(f32[16,16,6,128]{3,1,2,0:T(8,128)} %param.5) | copy-start | bytes 2359300
  1.8 0.9 %copy-start.1 = (s32[16,16,128]{2,1,0:T(8,128)S(1)}, s32[16,16,128]{2,1,0:T(8,128)}, u32[]{:S(2)}) copy-start(s32[16,16,128]{2,1,0:T(8,128)} %refs_5_.1) | copy-start | bytes 393220
  2.7 0.7 %copy-start.2 = (s32[16,16]{1,0:T(8,128)S(1)}, s32[16,16]{1,0:T(8,128)}, u32[]{:S(2)}) copy-start(s32[16,16]{1,0:T(8,128)} %refs_3_.1) | copy-start | bytes 3076
  3.4 0.7 %copy-start.3 = (s32[16,16]{1,0:T(8,128)S(1)}, s32[16,16]{1,0:T(8,128)}, u32[]{:S(2)}) copy-start(s32[16,16]{1,0:T(8,128)} %refs_4_.1) | copy-start | bytes 3076
  49.2 13.2 %all-to-all-start.1 = ((f32[512,1,128]{2,1,0:T(1,128)}), f32[512,1,128]{2,1,0:T(1,128)S(1)}, u32[]{:S(2)}, u32[]{:S(2)}) async-start(f32[512,1,128]{2,1,0:T(1,128)} %bitcast.7), calls=%async_computation.1 | async-start | bytes 524288 | tf_op jit(solution)/shard_map/all_to_all | solution.py:373
  53.6 1.9 %collective-permute-start = (f32[96,128]{1,0:T(8,128)S(1)}, f32[96,128]{1,0:T(8,128)S(1)}, u32[]{:S(2)}, u32[]{:S(2)}) collective-permute-start(f32[96,128]{1,0:T(8,128)S(1)} %get-tuple-element.13), channel_id=1, source_target_pairs={{0,1},{1,0},{2,3},{3,2},{4,5},{5,4},{6,7},{7,6},{8,9},{9,8},{10,11... | collective-permute-start | bytes 147464 | tf_op jit(solution)/shard_map/ppermute | solution.py:422
  53.8 5.1 %collective-permute-start.1 = (f32[96,128]{1,0:T(8,128)S(1)}, f32[96,128]{1,0:T(8,128)S(1)}, u32[]{:S(2)}, u32[]{:S(2)}) collective-permute-start(f32[96,128]{1,0:T(8,128)S(1)} %get-tuple-element.14), channel_id=1, source_target_pairs={{0,2},{1,3},{2,0},{3,1},{4,6},{5,7},{6,4},{7,5},{8,10},{9,11},{10,... | collective-permute-start | bytes 147464 | tf_op jit(solution)/shard_map/ppermute | solution.py:422
  55.4 4.4 %collective-permute-start.2 = (f32[96,128]{1,0:T(8,128)S(1)}, f32[96,128]{1,0:T(8,128)S(1)}, u32[]{:S(2)}, u32[]{:S(2)}) collective-permute-start(f32[96,128]{1,0:T(8,128)S(1)} %get-tuple-element.15), channel_id=1, source_target_pairs={{0,3},{1,2},{2,1},{3,0},{4,7},{5,6},{6,5},{7,4},{8,11},{9,10},{10,... | collective-permute-start | bytes 147464 | tf_op jit(solution)/shard_map/ppermute | solution.py:422

commit v4 on v3

--- a/solution.py
+++ b/solution.py
@@ -56,30 +56,31 @@
     return scan_local, tiles, per_scan, entries, cap, (COORDS + 1) * cap + 1
 
 
-def send_kernel(devices, groups, group_ref, count_ref, samples_ref, scan_ref, tile_ref, src_ref, out_ref, data_ref):
+def send_kernel(
+    devices,
+    groups,
+    group_ref,
+    count_ref,
+    samples_hbm,
+    scan_hbm,
+    tile_hbm,
+    src_hbm,
+    out_ref,
+    samples_ref,
+    scan_ref,
+    tile_ref,
+    src_ref,
+    data_ref,
+    sems,
+):
     scan_local, tiles, per_scan, entries, cap, block = sizes(samples_ref.shape, scan_ref.shape, devices)
     group_points = tiles * LANES
-
-    def one_scan(s, carry):
-        first = group_ref[0] * group_points
-        limit = count_ref[s] - first
-        for h in range(per_scan // 8):
-            ids = src_ref[s, pl.ds(h * 8, 8), :]
-            lane = mod(ids, LANES)
-            tile = div(ids, LANES)
-            found = [jnp.zeros((8, LANES), jnp.float32) for _ in range(COORDS)]
-            for t in range(tiles):
-                here = tile == t
-                for a in range(COORDS):
-                    row = jnp.broadcast_to(samples_ref[s, a, t : t + 1, :], (8, LANES))
-                    found[a] = jnp.where(here, jnp.take_along_axis(row, lane, axis=1), found[a])
-            at = pl.multiple_of(s * per_scan + h * 8, 8)
-            for a in range(COORDS):
-                data_ref[a, pl.ds(at, 8), :] = found[a]
-            data_ref[COORDS, pl.ds(at, 8), :] = (ids < limit).astype(jnp.float32)
-        return carry
-
-    lax.fori_loop(0, scan_local, one_scan, 0)
+    pairs = ((scan_hbm, scan_ref), (tile_hbm, tile_ref), (src_hbm, src_ref), (samples_hbm, samples_ref))
+    loads = [pltpu.make_async_copy(far, here, sems.at[k]) for k, (far, here) in enumerate(pairs)]
+    for load in loads:
+        load.start()
+    for load in loads[:2]:
+        load.wait()
 
     scans = scan_ref[...]
     tile_ids = tile_ref[...]
@@ -110,15 +111,6 @@
     rank_row = jnp.concatenate(rank_parts, axis=1)
     slot_row = (device_row * cap + rank_row).astype(jnp.int32)
     place = (iota((devices * cap, entries), 0) == slot_row).astype(jnp.float32).astype(jnp.bfloat16)
-    for a in range(COORDS + 1):
-        values = data_ref[a]
-        if a < COORDS:
-            parts = [dot(place, part) for part in pieces(values, 3)]
-            moved = (parts[0] + parts[1]) + parts[2]
-        else:
-            moved = dot(place, values.astype(jnp.bfloat16))
-        for d in range(devices):
-            out_ref[pl.ds(d * block + a * cap, cap), :] = moved[d * cap : (d + 1) * cap]
     owner_row = (div(iota((1, entries), 1), per_scan) + 1).astype(jnp.float32)
     field = div(iota((LANES, entries), 0), cap)
     picked = jnp.where(field == 0, owner_row, jnp.where(field == 1, mate_row, tile_row))
@@ -129,6 +121,39 @@
     notes = dot(towards, picked, BOTH_LANES)
     for d in range(devices):
         out_ref[pl.ds(d * block + (COORDS + 1) * cap, 1), :] = notes[d : d + 1]
+
+    for load in loads[2:]:
+        load.wait()
+
+    def one_scan(s, carry):
+        limit = count_ref[s] - group_ref[0] * group_points
+        for h in range(per_scan // 8):
+            ids = src_ref[s, pl.ds(h * 8, 8), :]
+            lane = mod(ids, LANES)
+            tile = div(ids, LANES)
+            found = [jnp.zeros((8, LANES), jnp.float32) for _ in range(COORDS)]
+            for t in range(tiles):
+                here = tile == t
+                for a in range(COORDS):
+                    row = jnp.broadcast_to(samples_ref[s, a, t : t + 1, :], (8, LANES))
+                    found[a] = jnp.where(here, jnp.take_along_axis(row, lane, axis=1), found[a])
+            at = pl.multiple_of(s * per_scan + h * 8, 8)
+            for a in range(COORDS):
+                data_ref[a, pl.ds(at, 8), :] = found[a]
+            data_ref[COORDS, pl.ds(at, 8), :] = (ids < limit).astype(jnp.float32)
+        return carry
+
+    lax.fori_loop(0, scan_local, one_scan, 0, unroll=4)
+
+    for a in range(COORDS + 1):
+        values = data_ref[a]
+        if a < COORDS:
+            parts = [dot(place, part) for part in pieces(values, 3)]
+            moved = (parts[0] + parts[1]) + parts[2]
+        else:
+            moved = dot(place, values.astype(jnp.bfloat16))
+        for d in range(devices):
+            out_ref[pl.ds(d * block + a * cap, cap), :] = moved[d * cap : (d + 1) * cap]
 
 
 def turn(x, amount):
@@ -199,7 +224,7 @@
             return tuple(s + t for s, t in zip(sums, terms))
 
         zero = jnp.zeros((8, LANES), jnp.float32)
-        sums = lax.fori_loop(0, LANES // 8, step, (zero,) * (MAT + FIELDS))
+        sums = lax.fori_loop(0, LANES // 8, step, (zero,) * (MAT + FIELDS), unroll=4)
         lines = [jnp.sum(s, axis=0, keepdims=True) for s in sums]
         blank = jnp.zeros((1, LANES), jnp.float32)
         lines[MAT:MAT] = [flag_row[:, lanes], mate_row[:, lanes], blank]
@@ -390,12 +415,17 @@
     def bind(kernel, *args):
         return lambda *refs: kernel(*args, *refs)
 
-    sent = call(
+    sent, samples = pl.pallas_call(
         bind(send_kernel, devices, groups),
-        near(devices * block, LANES),
-        2,
-        4,
-        [pltpu.VMEM((COORDS + 1, entries, LANES), jnp.float32)],
+        out_shape=(near(devices * block, LANES), near(*samples.shape)),
+        in_specs=[pl.BlockSpec(memory_space=pltpu.SMEM)] * 2 + [pl.BlockSpec(memory_space=pl.ANY)] * 4,
+        scratch_shapes=[
+            pltpu.VMEM(corr_scan.shape, jnp.int32),
+            pltpu.VMEM(corr_tile.shape, jnp.int32),
+            pltpu.VMEM(corr_src.shape, jnp.int32),
+            pltpu.VMEM((COORDS + 1, entries, LANES), jnp.float32),
+            pltpu.SemaphoreType.DMA((4,)),
+        ],
     )(group, point_count, samples, corr_scan, corr_tile, corr_src)
     received = exchange(sent, AXES)
     flat, back = call(

time: 65.5 us -> 61.1 us (0.933)
  local copies, waits for them, and re-layouts: 3.42 us -> 0 us
  Pallas kernels: 13.5 us -> 12.7 us
    pallas_call x4 -> x3, Pallas kernels: 13.5 us -> 7.86 us  [run(): return body(*args)]
    pallas_call x0 -> x1, Pallas kernels: none -> 4.79 us  [local(): pl.pallas_call(bind(send_kernel, devices, groups), out_shape=(near(device...]
    unnamed x8 -> x0, local copies, waits for them, and re-layouts: 3.42 us -> none
where the time goes in v4:
time: 61.1 us; the launch traced here: 60.8 us
  blocking collectives  35.5 us (58%)
  Pallas kernels  12.7 us (21%)
  waiting for transfers between devices  6.85 us (11%)
  starting transfers between devices  4.51 us (7%)
  between operations  0.67 us (1%)
  other arithmetic  0.64 us (1%)
    all_to_all x1, blocking collectives, exchange(): lax.all_to_all(x.reshape(count, 1, width), axes, split_axis=0, concat_axi...  35.5 us
    pallas_call x3, Pallas kernels, run(): return body(*args)  7.86 us
    pallas_call x1, Pallas kernels, local(): pl.pallas_call(bind(send_kernel, devices, groups), out_shape=(near(device...  4.79 us
    ppermute x3, waiting for transfers between devices, local(): lax.ppermute(shares[k], 'grp', [(g, partner(g, k, groups)) for g in range...  4.29 us
    all_to_all x1, starting transfers between devices, exchange(): lax.all_to_all(x.reshape(count, 1, width), axes, split_axis=0, concat_axi...  2.59 us
    all_to_all x1, waiting for transfers between devices, exchange(): lax.all_to_all(x.reshape(count, 1, width), axes, split_axis=0, concat_axi...  2.56 us
    ppermute x3, starting transfers between devices, local(): lax.ppermute(shares[k], 'grp', [(g, partner(g, k, groups)) for g in range...  1.93 us
  transfers between devices with their start and end apart: 4, of which 3 were waited for; matrix products, arithmetic and copies ran while one was open for 1% of the time, Pallas kernels for 2%

profile of v4, /device:TPU:0, one launch (start us, length us, event | category | flops | bytes accessed | tf_op | source)
XLA Modules:
  0.0 60.8 jit_solution(9859329213985974926)
XLA Ops:
  0.6 4.8 %shard_map.68 = (f32[2080,128]{1,0:T(8,128)S(1)}, f32[16,6,16,128]{3,2,1,0:T(8,128)S(1)}) custom-call(s32[1]{0:T(128)} %bitcast.1.refs_0_, s32[16]{0:T(128)} %refs_1_.3, f32[16,6,16,128]{3,2,1,0:T(8,128)} %bitcast.17, s32[16,16]{1,0:T(8,128)} %refs_3_.1, s32[16,16]{1,0:T(8,128)} %refs_4_.1, s32[16,16,128]{2,1,0:T(8,128)} %refs_5_.1), custom_call_target="tpu_custom_call" | custom-call | tf_op jit(solution)/shard_map/pallas_call | solution.py:418
  5.4 35.5 %all_to_all.10 = f32[2080,1,128]{2,1,0:T(1,128)S(1)} all-to-all(f32[2080,1,128]{2,1,0:T(1,128)S(1)} %bitcast.15), channel_id=1, replica_groups=mesh['scan'=8,'grp'=4] {'scan','grp'}, dimensions={0} | all-to-all | bytes 2129920 | tf_op jit(solution)/shard_map/all_to_all | solution.py:398
  40.9 4.0 %shard_map.69 = (f32[32,512]{1,0:T(8,128)S(1)}, f32[512,128]{1,0:T(8,128)}) custom-call(s32[1]{0:T(128)} %bitcast.1.refs_0_, s32[16]{0:T(128)} %refs_1_.3, f32[16,6,16,128]{3,2,1,0:T(8,128)S(1)} %get-tuple-element.12.refs_2_, f32[2080,128]{1,0:T(8,128)S(1)} %bitcast.14), custom_call_target="tpu_custom_call" | custom-call | tf_op jit(solution)/shard_map/pallas_call | solution.py:383
  45.0 2.6 %all-to-all-start.1 = ((f32[512,1,128]{2,1,0:T(1,128)}), f32[512,1,128]{2,1,0:T(1,128)S(1)}, u32[]{:S(2)}, u32[]{:S(2)}) async-start(f32[512,1,128]{2,1,0:T(1,128)} %bitcast.7), calls=%async_computation.1 | async-start | bytes 524288 | tf_op jit(solution)/shard_map/all_to_all | solution.py:398
  47.5 0.6 %pad_add_fusion.refs_0_ = s32[2]{0:T(128)} fusion(s32[1]{0:T(128)} %bitcast.1.refs_0_, s32[1]{0:T(128)} %bitcast), kind=kLoop, calls=%fused_computation | loop fusion | flops 2 | bytes 16 | tf_op jit(solution)/shard_map/stack | solution.py:411
  48.2 1.1 %shard_map.70 = (f32[96,128]{1,0:T(8,128)S(1)}, f32[96,128]{1,0:T(8,128)S(1)}, f32[96,128]{1,0:T(8,128)S(1)}, f32[96,128]{1,0:T(8,128)S(1)}) custom-call(s32[2]{0:T(128)} %pad_add_fusion.refs_0_, f32[32,512]{1,0:T(8,128)S(1)} %get-tuple-element.15.refs_1_), custom_call_target="tpu_custom_call" | custom-call | tf_op jit(solution)/shard_map/pallas_call | solution.py:383
  49.3 0.2 collective-permute-start
  49.5 1.6 %collective-permute-start.1 = (f32[96,128]{1,0:T(8,128)S(1)}, f32[96,128]{1,0:T(8,128)S(1)}, u32[]{:S(2)}, u32[]{:S(2)}) collective-permute-start(f32[96,128]{1,0:T(8,128)S(1)} %get-tuple-element.18), channel_id=1, source_target_pairs={{0,2},{1,3},{2,0},{3,1},{4,6},{5,7},{6,4},{7,5},{8,10},{9,11},{10,... | collective-permute-start | bytes 147464 | tf_op jit(solution)/shard_map/ppermute | solution.py:452
  51.2 0.1 collective-permute-start.2
  51.3 0.0 collective-permute-done.refs_3_
  51.3 3.3 %collective-permute-done.1.refs_4_ = f32[96,128]{1,0:T(8,128)S(1)} collective-permute-done((f32[96,128]{1,0:T(8,128)S(1)}, f32[96,128]{1,0:T(8,128)S(1)}, u32[]{:S(2)}, u32[]{:S(2)}) %collective-permute-start.1) | collective-permute-done | bytes 49184 | tf_op jit(solution)/shard_map/ppermute | solution.py:452
  54.6 1.0 %collective-permute-done.2.refs_5_ = f32[96,128]{1,0:T(8,128)S(1)} collective-permute-done((f32[96,128]{1,0:T(8,128)S(1)}, f32[96,128]{1,0:T(8,128)S(1)}, u32[]{:S(2)}, u32[]{:S(2)}) %collective-permute-start.2) | collective-permute-done | bytes 49184 | tf_op jit(solution)/shard_map/ppermute | solution.py:452
  55.6 2.6 %all-to-all-done.1 = f32[512,1,128]{2,1,0:T(1,128)S(1)} async-done(((f32[512,1,128]{2,1,0:T(1,128)}), f32[512,1,128]{2,1,0:T(1,128)S(1)}, u32[]{:S(2)}, u32[]{:S(2)}) %all-to-all-start.1) | async-done | bytes 262176 | tf_op jit(solution)/shard_map/all_to_all | solution.py:398
  58.1 2.7 %shard_map.71 = (f32[36,16,32]{2,1,0:T(8,128)}, f32[4,6]{1,0:T(4,128)}) custom-call(s32[2]{0:T(128)} %pad_add_fusion.refs_0_, f32[512,128]{1,0:T(8,128)S(1)} %bitcast.16, f32[96,128]{1,0:T(8,128)S(1)} %get-tuple-element.16.refs_2_, f32[96,128]{1,0:T(8,128)S(1)} %collective-permute-done.refs_3_, f32[96,128]{1,0:T(8,128)S(1)} %collective-permute-done.1.refs_4_, ...), custom_call_target="tpu_custom_call" | custom-call | tf_op jit(solution)/shard_map/pallas_call | solution.py:383
Async XLA Ops:
  45.0 13.2 %all-to-all-start.1 = ((f32[512,1,128]{2,1,0:T(1,128)}), f32[512,1,128]{2,1,0:T(1,128)S(1)}, u32[]{:S(2)}, u32[]{:S(2)}) async-start(f32[512,1,128]{2,1,0:T(1,128)} %bitcast.7), calls=%async_computation.1 | async-start | bytes 524288 | tf_op jit(solution)/shard_map/all_to_all | solution.py:398
  49.3 1.9 %collective-permute-start = (f32[96,128]{1,0:T(8,128)S(1)}, f32[96,128]{1,0:T(8,128)S(1)}, u32[]{:S(2)}, u32[]{:S(2)}) collective-permute-start(f32[96,128]{1,0:T(8,128)S(1)} %get-tuple-element.17), channel_id=1, source_target_pairs={{0,1},{1,0},{2,3},{3,2},{4,5},{5,4},{6,7},{7,6},{8,9},{9,8},{10,11... | collective-permute-start | bytes 147464 | tf_op jit(solution)/shard_map/ppermute | solution.py:452
  49.5 5.1 %collective-permute-start.1 = (f32[96,128]{1,0:T(8,128)S(1)}, f32[96,128]{1,0:T(8,128)S(1)}, u32[]{:S(2)}, u32[]{:S(2)}) collective-permute-start(f32[96,128]{1,0:T(8,128)S(1)} %get-tuple-element.18), channel_id=1, source_target_pairs={{0,2},{1,3},{2,0},{3,1},{4,6},{5,7},{6,4},{7,5},{8,10},{9,11},{10,... | collective-permute-start | bytes 147464 | tf_op jit(solution)/shard_map/ppermute | solution.py:452
  51.2 4.4 %collective-permute-start.2 = (f32[96,128]{1,0:T(8,128)S(1)}, f32[96,128]{1,0:T(8,128)S(1)}, u32[]{:S(2)}, u32[]{:S(2)}) collective-permute-start(f32[96,128]{1,0:T(8,128)S(1)} %get-tuple-element.19), channel_id=1, source_target_pairs={{0,3},{1,2},{2,1},{3,0},{4,7},{5,6},{6,5},{7,4},{8,11},{9,10},{10,... | collective-permute-start | bytes 147464 | tf_op jit(solution)/shard_map/ppermute | solution.py:452

commit v5 on v4

--- a/solution.py
+++ b/solution.py
@@ -14,6 +14,7 @@
 ROW_MATE = MAT + 1
 HEAD = MAT + 3
 WIDTH = 32
+FAR = 2.0**100
 BOTH_LANES = (((1,), (1,)), ((), ()))
 AXES = ("scan", "grp")
 
@@ -53,7 +54,7 @@
     per_scan = entries_shape[1]
     entries = scan_local * per_scan
     cap = 2 * entries // devices
-    return scan_local, tiles, per_scan, entries, cap, (COORDS + 1) * cap + 1
+    return scan_local, tiles, per_scan, entries, cap, COORDS * cap + 1
 
 
 def send_kernel(
@@ -120,7 +121,7 @@
     towards = (iota((devices, entries), 0).astype(jnp.float32) == device_row).astype(jnp.float32).astype(jnp.bfloat16)
     notes = dot(towards, picked, BOTH_LANES)
     for d in range(devices):
-        out_ref[pl.ds(d * block + (COORDS + 1) * cap, 1), :] = notes[d : d + 1]
+        out_ref[pl.ds(d * block + COORDS * cap, 1), :] = notes[d : d + 1]
 
     for load in loads[2:]:
         load.wait()
@@ -137,21 +138,17 @@
                 for a in range(COORDS):
                     row = jnp.broadcast_to(samples_ref[s, a, t : t + 1, :], (8, LANES))
                     found[a] = jnp.where(here, jnp.take_along_axis(row, lane, axis=1), found[a])
+            found[0] = jnp.where(ids < limit, found[0], FAR)
             at = pl.multiple_of(s * per_scan + h * 8, 8)
             for a in range(COORDS):
                 data_ref[a, pl.ds(at, 8), :] = found[a]
-            data_ref[COORDS, pl.ds(at, 8), :] = (ids < limit).astype(jnp.float32)
         return carry
 
     lax.fori_loop(0, scan_local, one_scan, 0, unroll=4)
 
-    for a in range(COORDS + 1):
-        values = data_ref[a]
-        if a < COORDS:
-            parts = [dot(place, part) for part in pieces(values, 3)]
-            moved = (parts[0] + parts[1]) + parts[2]
-        else:
-            moved = dot(place, values.astype(jnp.bfloat16))
+    for a in range(COORDS):
+        parts = [dot(place, part) for part in pieces(data_ref[a], 3)]
+        moved = (parts[0] + parts[1]) + parts[2]
         for d in range(devices):
             out_ref[pl.ds(d * block + a * cap, cap), :] = moved[d * cap : (d + 1) * cap]
 
@@ -174,9 +171,9 @@
     scan_local, _, tiles, _ = samples_ref.shape
     slots = flat_ref.shape[1]
     cap = slots // devices
-    block = (COORDS + 1) * cap + 1
+    block = COORDS * cap + 1
     for d in range(devices):
-        note_ref[pl.ds(d, 1), :] = recv_ref[pl.ds(d * block + (COORDS + 1) * cap, 1), :]
+        note_ref[pl.ds(d, 1), :] = recv_ref[pl.ds(d * block + COORDS * cap, 1), :]
     notes = note_ref[...].astype(jnp.bfloat16)
     mine = div(iota((devices, slots), 1), cap) == iota((devices, slots), 0)
     rows = []
@@ -204,7 +201,7 @@
         mate_ref[a] = (parts[0] + parts[1]) + parts[2]
     per_chunk = LANES // cap
     for c in range(slots // LANES):
-        for a in range(COORDS + 1):
+        for a in range(COORDS):
             stack = [
                 recv_ref[pl.ds(d * block + a * cap, cap), :] for d in range(c * per_chunk, (c + 1) * per_chunk)
             ]
@@ -214,10 +211,12 @@
 
         def step(k, sums):
             at = pl.ds(pl.multiple_of(k * 8, 8), 8)
-            px, py, pz, mask = [point_ref[a, at, lanes] for a in range(COORDS + 1)]
+            px, py, pz = [point_ref[a, at, lanes] for a in range(COORDS)]
+            present = px < FAR
+            px = jnp.where(present, px, 0.0)
             qx, qy, qz, nx, ny, nz = [mate_ref[a, at, lanes] for a in range(FIELDS)]
             residual = nx * (px - qx) + ny * (py - qy) + nz * (pz - qz)
-            weight = mask / (1.0 + residual * residual)
+            weight = jnp.where(present, 1.0 / (1.0 + residual * residual), 0.0)
             jac = [py * nz - pz * ny, pz * nx - px * nz, px * ny - py * nx, nx, ny, nz]
             scaled = [weight * j for j in jac]
             terms = [scaled[i] * jac[j] for i, j in PAIRS] + [residual * s for s in scaled]
@@ -225,7 +224,8 @@
 
         zero = jnp.zeros((8, LANES), jnp.float32)
         sums = lax.fori_loop(0, LANES // 8, step, (zero,) * (MAT + FIELDS), unroll=4)
-        lines = [jnp.sum(s, axis=0, keepdims=True) for s in sums]
+        filled = flag_row[:, lanes] > 0.0
+        lines = [jnp.where(filled, jnp.sum(s, axis=0, keepdims=True), 0.0) for s in sums]
         blank = jnp.zeros((1, LANES), jnp.float32)
         lines[MAT:MAT] = [flag_row[:, lanes], mate_row[:, lanes], blank]
         lines += [blank] * (WIDTH - len(lines))
@@ -423,7 +423,7 @@
             pltpu.VMEM(corr_scan.shape, jnp.int32),
             pltpu.VMEM(corr_tile.shape, jnp.int32),
             pltpu.VMEM(corr_src.shape, jnp.int32),
-            pltpu.VMEM((COORDS + 1, entries, LANES), jnp.float32),
+            pltpu.VMEM((COORDS, entries, LANES), jnp.float32),
             pltpu.SemaphoreType.DMA((4,)),
         ],
     )(group, point_count, samples, corr_scan, corr_tile, corr_src)
@@ -434,7 +434,7 @@
         2,
         2,
         [
-            pltpu.VMEM((COORDS + 1, LANES, slots), jnp.float32),
+            pltpu.VMEM((COORDS, LANES, slots), jnp.float32),
             pltpu.VMEM((FIELDS, LANES, slots), jnp.float32),
             pltpu.VMEM((devices, LANES), jnp.float32),
         ],

time: 61.1 us -> 54.7 us (0.90)
  blocking collectives: 35.5 us -> 28.1 us
  starting transfers between devices: 4.51 us -> 5.58 us
    all_to_all x1, blocking collectives: 35.5 us -> 28.1 us  [exchange(): lax.all_to_all(x.reshape(count, 1, width), axes, split_axis=0, concat_axi...]
    all_to_all x1, starting transfers between devices: 2.59 us -> 3.62 us  [exchange(): lax.all_to_all(x.reshape(count, 1, width), axes, split_axis=0, concat_axi...]
where the time goes in v5:
time: 54.7 us; the launch traced here: 54.4 us
  blocking collectives  28.1 us (51%)
  Pallas kernels  12.6 us (23%)
  waiting for transfers between devices  6.82 us (12%)
  starting transfers between devices  5.58 us (10%)
  between operations  0.67 us (1%)
  other arithmetic  0.64 us (1%)
    all_to_all x1, blocking collectives, exchange(): lax.all_to_all(x.reshape(count, 1, width), axes, split_axis=0, concat_axi...  28.1 us
    pallas_call x3, Pallas kernels, run(): return body(*args)  7.9 us
    pallas_call x1, Pallas kernels, local(): pl.pallas_call(bind(send_kernel, devices, groups), out_shape=(near(device...  4.72 us
    ppermute x3, waiting for transfers between devices, local(): lax.ppermute(shares[k], 'grp', [(g, partner(g, k, groups)) for g in range...  4.3 us
    all_to_all x1, starting transfers between devices, exchange(): lax.all_to_all(x.reshape(count, 1, width), axes, split_axis=0, concat_axi...  3.62 us
    all_to_all x1, waiting for transfers between devices, exchange(): lax.all_to_all(x.reshape(count, 1, width), axes, split_axis=0, concat_axi...  2.52 us
    ppermute x3, starting transfers between devices, local(): lax.ppermute(shares[k], 'grp', [(g, partner(g, k, groups)) for g in range...  1.96 us
  transfers between devices with their start and end apart: 4, of which 3 were waited for; matrix products, arithmetic and copies ran while one was open for 1% of the time, Pallas kernels for 2%

profile of v5, /device:TPU:0, one launch (start us, length us, event | category | flops | bytes accessed | tf_op | source)
XLA Modules:
  0.0 54.4 jit_solution(10093062566134629124)
XLA Ops:
  0.6 4.7 %shard_map.68 = (f32[1568,128]{1,0:T(8,128)S(1)}, f32[16,6,16,128]{3,2,1,0:T(8,128)S(1)}) custom-call(s32[1]{0:T(128)} %bitcast.1.refs_0_, s32[16]{0:T(128)} %refs_1_.3, f32[16,6,16,128]{3,2,1,0:T(8,128)} %bitcast.17, s32[16,16]{1,0:T(8,128)} %refs_3_.1, s32[16,16]{1,0:T(8,128)} %refs_4_.1, s32[16,16,128]{2,1,0:T(8,128)} %refs_5_.1), custom_call_target="tpu_custom_call" | custom-call | tf_op jit(solution)/shard_map/pallas_call | solution.py:418
  5.4 28.1 %all_to_all.10 = f32[1568,1,128]{2,1,0:T(1,128)S(1)} all-to-all(f32[1568,1,128]{2,1,0:T(1,128)S(1)} %bitcast.16), channel_id=1, replica_groups=mesh['scan'=8,'grp'=4] {'scan','grp'}, dimensions={0} | all-to-all | bytes 1605632 | tf_op jit(solution)/shard_map/all_to_all | solution.py:398
  33.4 4.1 %shard_map.69 = (f32[32,512]{1,0:T(8,128)S(1)}, f32[512,128]{1,0:T(8,128)}) custom-call(s32[1]{0:T(128)} %bitcast.1.refs_0_, s32[16]{0:T(128)} %refs_1_.3, f32[16,6,16,128]{3,2,1,0:T(8,128)S(1)} %get-tuple-element.12.refs_2_, f32[1568,128]{1,0:T(8,128)S(1)} %bitcast.14), custom_call_target="tpu_custom_call" | custom-call | tf_op jit(solution)/shard_map/pallas_call | solution.py:383
  37.5 3.6 %all-to-all-start.1 = ((f32[512,1,128]{2,1,0:T(1,128)}), f32[512,1,128]{2,1,0:T(1,128)S(1)}, u32[]{:S(2)}, u32[]{:S(2)}) async-start(f32[512,1,128]{2,1,0:T(1,128)} %bitcast.7), calls=%async_computation.1 | async-start | bytes 524288 | tf_op jit(solution)/shard_map/all_to_all | solution.py:398
  41.1 0.6 %pad_add_fusion.refs_0_ = s32[2]{0:T(128)} fusion(s32[1]{0:T(128)} %bitcast.1.refs_0_, s32[1]{0:T(128)} %bitcast), kind=kLoop, calls=%fused_computation | loop fusion | flops 2 | bytes 16 | tf_op jit(solution)/shard_map/stack | solution.py:411
  41.8 1.1 %shard_map.70 = (f32[96,128]{1,0:T(8,128)S(1)}, f32[96,128]{1,0:T(8,128)S(1)}, f32[96,128]{1,0:T(8,128)S(1)}, f32[96,128]{1,0:T(8,128)S(1)}) custom-call(s32[2]{0:T(128)} %pad_add_fusion.refs_0_, f32[32,512]{1,0:T(8,128)S(1)} %get-tuple-element.15.refs_1_), custom_call_target="tpu_custom_call" | custom-call | tf_op jit(solution)/shard_map/pallas_call | solution.py:383
  42.9 0.3 collective-permute-start
  43.2 1.6 %collective-permute-start.1 = (f32[96,128]{1,0:T(8,128)S(1)}, f32[96,128]{1,0:T(8,128)S(1)}, u32[]{:S(2)}, u32[]{:S(2)}) collective-permute-start(f32[96,128]{1,0:T(8,128)S(1)} %get-tuple-element.18), channel_id=1, source_target_pairs={{0,2},{1,3},{2,0},{3,1},{4,6},{5,7},{6,4},{7,5},{8,10},{9,11},{10,... | collective-permute-start | bytes 147464 | tf_op jit(solution)/shard_map/ppermute | solution.py:452
  44.9 0.0 collective-permute-start.2
  44.9 0.0 collective-permute-done.refs_3_
  44.9 3.2 %collective-permute-done.1.refs_4_ = f32[96,128]{1,0:T(8,128)S(1)} collective-permute-done((f32[96,128]{1,0:T(8,128)S(1)}, f32[96,128]{1,0:T(8,128)S(1)}, u32[]{:S(2)}, u32[]{:S(2)}) %collective-permute-start.1) | collective-permute-done | bytes 49184 | tf_op jit(solution)/shard_map/ppermute | solution.py:452
  48.1 1.1 %collective-permute-done.2.refs_5_ = f32[96,128]{1,0:T(8,128)S(1)} collective-permute-done((f32[96,128]{1,0:T(8,128)S(1)}, f32[96,128]{1,0:T(8,128)S(1)}, u32[]{:S(2)}, u32[]{:S(2)}) %collective-permute-start.2) | collective-permute-done | bytes 49184 | tf_op jit(solution)/shard_map/ppermute | solution.py:452
  49.2 2.5 %all-to-all-done.1 = f32[512,1,128]{2,1,0:T(1,128)S(1)} async-done(((f32[512,1,128]{2,1,0:T(1,128)}), f32[512,1,128]{2,1,0:T(1,128)S(1)}, u32[]{:S(2)}, u32[]{:S(2)}) %all-to-all-start.1) | async-done | bytes 262176 | tf_op jit(solution)/shard_map/all_to_all | solution.py:398
  51.7 2.7 %shard_map.71 = (f32[36,16,32]{2,1,0:T(8,128)}, f32[4,6]{1,0:T(4,128)}) custom-call(s32[2]{0:T(128)} %pad_add_fusion.refs_0_, f32[512,128]{1,0:T(8,128)S(1)} %bitcast.15, f32[96,128]{1,0:T(8,128)S(1)} %get-tuple-element.16.refs_2_, f32[96,128]{1,0:T(8,128)S(1)} %collective-permute-done.refs_3_, f32[96,128]{1,0:T(8,128)S(1)} %collective-permute-done.1.refs_4_, ...), custom_call_target="tpu_custom_call" | custom-call | tf_op jit(solution)/shard_map/pallas_call | solution.py:383
Async XLA Ops:
  37.5 14.2 %all-to-all-start.1 = ((f32[512,1,128]{2,1,0:T(1,128)}), f32[512,1,128]{2,1,0:T(1,128)S(1)}, u32[]{:S(2)}, u32[]{:S(2)}) async-start(f32[512,1,128]{2,1,0:T(1,128)} %bitcast.7), calls=%async_computation.1 | async-start | bytes 524288 | tf_op jit(solution)/shard_map/all_to_all | solution.py:398
  42.9 2.0 %collective-permute-start = (f32[96,128]{1,0:T(8,128)S(1)}, f32[96,128]{1,0:T(8,128)S(1)}, u32[]{:S(2)}, u32[]{:S(2)}) collective-permute-start(f32[96,128]{1,0:T(8,128)S(1)} %get-tuple-element.17), channel_id=1, source_target_pairs={{0,1},{1,0},{2,3},{3,2},{4,5},{5,4},{6,7},{7,6},{8,9},{9,8},{10,11... | collective-permute-start | bytes 147464 | tf_op jit(solution)/shard_map/ppermute | solution.py:452
  43.2 4.9 %collective-permute-start.1 = (f32[96,128]{1,0:T(8,128)S(1)}, f32[96,128]{1,0:T(8,128)S(1)}, u32[]{:S(2)}, u32[]{:S(2)}) collective-permute-start(f32[96,128]{1,0:T(8,128)S(1)} %get-tuple-element.18), channel_id=1, source_target_pairs={{0,2},{1,3},{2,0},{3,1},{4,6},{5,7},{6,4},{7,5},{8,10},{9,11},{10,... | collective-permute-start | bytes 147464 | tf_op jit(solution)/shard_map/ppermute | solution.py:452
  44.9 4.3 %collective-permute-start.2 = (f32[96,128]{1,0:T(8,128)S(1)}, f32[96,128]{1,0:T(8,128)S(1)}, u32[]{:S(2)}, u32[]{:S(2)}) collective-permute-start(f32[96,128]{1,0:T(8,128)S(1)} %get-tuple-element.19), channel_id=1, source_target_pairs={{0,3},{1,2},{2,1},{3,0},{4,7},{5,6},{6,5},{7,4},{8,11},{9,10},{10,... | collective-permute-start | bytes 147464 | tf_op jit(solution)/shard_map/ppermute | solution.py:452

commit v6 on v5

--- a/solution.py
+++ b/solution.py
@@ -61,13 +61,14 @@
     devices,
     groups,
     group_ref,
-    count_ref,
+    count_hbm,
     samples_hbm,
     scan_hbm,
     tile_hbm,
     src_hbm,
     out_ref,
     samples_ref,
+    count_ref,
     scan_ref,
     tile_ref,
     src_ref,
@@ -76,7 +77,13 @@
 ):
     scan_local, tiles, per_scan, entries, cap, block = sizes(samples_ref.shape, scan_ref.shape, devices)
     group_points = tiles * LANES
-    pairs = ((scan_hbm, scan_ref), (tile_hbm, tile_ref), (src_hbm, src_ref), (samples_hbm, samples_ref))
+    pairs = (
+        (scan_hbm, scan_ref),
+        (tile_hbm, tile_ref),
+        (count_hbm, count_ref),
+        (src_hbm, src_ref),
+        (samples_hbm, samples_ref),
+    )
     loads = [pltpu.make_async_copy(far, here, sems.at[k]) for k, (far, here) in enumerate(pairs)]
     for load in loads:
         load.start()
@@ -142,6 +149,9 @@
             at = pl.multiple_of(s * per_scan + h * 8, 8)
             for a in range(COORDS):
                 data_ref[a, pl.ds(at, 8), :] = found[a]
+        present = iota((tiles, LANES), 0) * LANES + iota((tiles, LANES), 1) < limit
+        for a in range(COORDS, FIELDS):
+            samples_ref[s, a] = jnp.where(present, samples_ref[s, a], 0.0)
         return carry
 
     lax.fori_loop(0, scan_local, one_scan, 0, unroll=4)
@@ -167,7 +177,7 @@
     return index ^ k if groups & (groups - 1) == 0 else (index + k) % groups
 
 
-def pair_kernel(devices, groups, group_ref, count_ref, samples_ref, recv_ref, flat_ref, back_ref, point_ref, mate_ref, note_ref):
+def pair_kernel(devices, groups, samples_ref, recv_ref, flat_ref, back_ref, point_ref, mate_ref, note_ref):
     scan_local, _, tiles, _ = samples_ref.shape
     slots = flat_ref.shape[1]
     cap = slots // devices
@@ -186,16 +196,8 @@
     code_row = (mate_row * tiles + tile_row).astype(jnp.int32)
     table = scan_local * tiles
     chosen = (iota((table, slots), 0) == code_row).astype(jnp.float32).astype(jnp.bfloat16)
-    base = group_ref[0] * tiles
-    point_ids = (base + iota((tiles, LANES), 0)) * LANES + iota((tiles, LANES), 1)
     for a in range(FIELDS):
-        values = []
-        for b in range(scan_local):
-            value = samples_ref[b, a]
-            if a >= COORDS:
-                value = jnp.where(point_ids < count_ref[b], value, 0.0)
-            values.append(value)
-        values = jnp.concatenate(values, axis=0)
+        values = jnp.concatenate([samples_ref[b, a] for b in range(scan_local)], axis=0)
         turned = jnp.concatenate([values[h : h + LANES].T for h in range(0, table, LANES)], axis=1)
         parts = [dot(part, chosen) for part in pieces(turned, 3)]
         mate_ref[a] = (parts[0] + parts[1]) + parts[2]
@@ -272,7 +274,7 @@
         )
 
 
-def held_kernel(devices, groups, scan_local, place_ref, flat_ref, *refs):
+def held_kernel(devices, groups, scan_local, scan_ref, group_ref, flat_ref, *refs):
     out_refs, stage_ref = refs[:-1], refs[-1]
     slots = flat_ref.shape[1]
     cap = slots // devices
@@ -281,7 +283,7 @@
     every = flat_ref[...]
     row = every[ROW_MATE : ROW_MATE + 1].astype(jnp.int32)
     other = div(div(iota((1, slots), 1), cap), groups) * scan_local + every[ROW_FLAG : ROW_FLAG + 1].astype(jnp.int32) - 1
-    own = place_ref[0] * scan_local + row
+    own = scan_ref[0] * scan_local + row
     row_hot = iota((scan_local, slots), 0) == row
     column = iota((scan_total, slots), 0)
     mix = ((column == own).astype(jnp.float32) - (column == other).astype(jnp.float32)).astype(jnp.bfloat16)
@@ -308,17 +310,17 @@
                 tile = jnp.where(div(lane, columns) == k, value, tile) if pack > 1 else value
             stage_ref[c, r * scan_local : (r + 1) * scan_local, :] = tile
     for k, out_ref in enumerate(out_refs):
-        out_ref[...] = stage_ref[partner(place_ref[1], k, groups)]
-
-
-def close_kernel(devices, groups, cap, place_ref, back_ref, *refs):
+        out_ref[...] = stage_ref[partner(group_ref[0], k, groups)]
+
+
+def close_kernel(devices, groups, cap, scan_ref, group_ref, back_ref, *refs):
     part_refs, (hess_ref, grad_ref, every_ref, hold_ref) = refs[:groups], refs[groups:]
     scan_local, columns = hess_ref.shape[1:]
     per_block = part_refs[0].shape[0] // scan_local
     span, slot_rows, sum_rows = back_layout(scan_local, groups, cap)
     block = slot_rows + sum_rows
     senders = devices // groups
-    first = place_ref[1] * (senders * block)
+    first = group_ref[0] * (senders * block)
     lane_block = div(iota((slot_rows, LANES), 1), span)
     per_chunk = LANES // span
     for chunk in range(senders // per_chunk):
@@ -350,7 +352,7 @@
     whole = part_refs[0][...]
     for part_ref in part_refs[1:]:
         whole = whole + part_ref[...]
-    offset = place_ref[0] * scan_local - place_ref[1] * columns
+    offset = scan_ref[0] * scan_local - group_ref[0] * columns
     diagonal = iota((scan_local, columns), 1) == iota((scan_local, columns), 0) + offset
     for q in range(MAT):
         k, r = divmod(q, per_block)
@@ -367,7 +369,7 @@
         grad = grad + jnp.where(lane == q, by_row(HEAD + q), 0.0)
     hold_ref[...] = grad
     part = scan_local // groups
-    grad_ref[...] = hold_ref[pl.ds(place_ref[1] * part, part), 0:FIELDS]
+    grad_ref[...] = hold_ref[pl.ds(group_ref[0] * part, part), 0:FIELDS]
 
 
 def call(kernel, out_shape, smem, vmem, scratch=()):
@@ -407,9 +409,8 @@
     slots = devices * cap
     scan_total = scan_local * (devices // groups)
     columns, pack, per_block = layout(scan_local, groups, scan_total)
-    group = lax.axis_index("grp").astype(jnp.int32)
-    place = jnp.stack([lax.axis_index("scan").astype(jnp.int32), group])
-    group = group.reshape(1)
+    group = lax.axis_index("grp").astype(jnp.int32).reshape(1)
+    scan = lax.axis_index("scan").astype(jnp.int32).reshape(1)
     _, slot_rows, sum_rows = back_layout(scan_local, groups, cap)
 
     def bind(kernel, *args):
@@ -418,49 +419,50 @@
     sent, samples = pl.pallas_call(
         bind(send_kernel, devices, groups),
         out_shape=(near(devices * block, LANES), near(*samples.shape)),
-        in_specs=[pl.BlockSpec(memory_space=pltpu.SMEM)] * 2 + [pl.BlockSpec(memory_space=pl.ANY)] * 4,
+        in_specs=[pl.BlockSpec(memory_space=pltpu.SMEM)] + [pl.BlockSpec(memory_space=pl.ANY)] * 5,
         scratch_shapes=[
+            pltpu.SMEM(point_count.shape, jnp.int32),
             pltpu.VMEM(corr_scan.shape, jnp.int32),
             pltpu.VMEM(corr_tile.shape, jnp.int32),
             pltpu.VMEM(corr_src.shape, jnp.int32),
             pltpu.VMEM((COORDS, entries, LANES), jnp.float32),
-            pltpu.SemaphoreType.DMA((4,)),
+            pltpu.SemaphoreType.DMA((5,)),
         ],
     )(group, point_count, samples, corr_scan, corr_tile, corr_src)
     received = exchange(sent, AXES)
     flat, back = call(
         bind(pair_kernel, devices, groups),
         (near(WIDTH, slots), near(devices * (slot_rows + sum_rows), LANES)),
-        2,
+        0,
         2,
         [
             pltpu.VMEM((COORDS, LANES, slots), jnp.float32),
             pltpu.VMEM((FIELDS, LANES, slots), jnp.float32),
             pltpu.VMEM((devices, LANES), jnp.float32),
         ],
-    )(group, point_count, samples, received)
+    )(samples, received)
     back = exchange(back, AXES)
     share = near(per_block * scan_local, LANES)
     shares = call(
         bind(held_kernel, devices, groups, scan_local),
         (share,) * groups,
-        1,
+        2,
         1,
         [pltpu.VMEM((groups,) + share.shape, jnp.float32)],
-    )(place, flat)
+    )(scan, group, flat)
     shares = [shares[0]] + [
         lax.ppermute(shares[k], "grp", [(g, partner(g, k, groups)) for g in range(groups)]) for k in range(1, groups)
     ]
     hess, grad = call(
         bind(close_kernel, devices, groups, cap),
         (f32(FIELDS * FIELDS, scan_local, columns), f32(scan_local // groups, FIELDS)),
-        1,
+        2,
         1 + groups,
         [
             pltpu.VMEM((HEAD, (devices // groups) * groups * cap), jnp.float32),
             pltpu.VMEM((scan_local, LANES), jnp.float32),
         ],
-    )(place, back, *shares)
+    )(scan, group, back, *shares)
     return hess.reshape(FIELDS, FIELDS, scan_local, columns).transpose(2, 0, 1, 3), grad
 
 

time: 54.7 us -> 52.7 us (0.963)
  Pallas kernels: 12.6 us -> 10 us
  waiting for transfers between devices: 6.82 us -> 8.11 us
  other arithmetic: 0.64 us -> 0 us
    pallas_call x3, Pallas kernels: 7.9 us -> 5.95 us  [run(): return body(*args)]
    all_to_all x1, waiting for transfers between devices: 2.52 us -> 3.46 us  [exchange(): lax.all_to_all(x.reshape(count, 1, width), axes, split_axis=0, concat_axi...]
    pallas_call x1, Pallas kernels: 4.72 us -> 4.07 us  [local(): pl.pallas_call(bind(send_kernel, devices, groups), out_shape=(near(device...]
    another operation x1 -> x0, other arithmetic: 0.64 us -> none  [local(): place = jnp.stack([lax.axis_index('scan').astype(jnp.int32), group])]
  transfers between devices with their start and end apart: 4 -> 4, of which waited for: 3 -> 3; matrix products, arithmetic and copies ran while one was open for 1% -> 0% of each run, Pallas kernels for 2% -> 1%
where the time goes in v6:
time: 52.7 us; the launch traced here: 52.5 us
  blocking collectives  28.1 us (53%)
  Pallas kernels  10 us (19%)
  waiting for transfers between devices  8.11 us (15%)
  starting transfers between devices  5.57 us (11%)
  between operations  0.67 us (1%)
    all_to_all x1, blocking collectives, exchange(): lax.all_to_all(x.reshape(count, 1, width), axes, split_axis=0, concat_axi...  28.1 us
    pallas_call x3, Pallas kernels, run(): return body(*args)  5.95 us
    ppermute x3, waiting for transfers between devices, local(): lax.ppermute(shares[k], 'grp', [(g, partner(g, k, groups)) for g in range...  4.65 us
    pallas_call x1, Pallas kernels, local(): pl.pallas_call(bind(send_kernel, devices, groups), out_shape=(near(device...  4.07 us
    all_to_all x1, starting transfers between devices, exchange(): lax.all_to_all(x.reshape(count, 1, width), axes, split_axis=0, concat_axi...  3.62 us
    all_to_all x1, waiting for transfers between devices, exchange(): lax.all_to_all(x.reshape(count, 1, width), axes, split_axis=0, concat_axi...  3.46 us
    ppermute x3, starting transfers between devices, local(): lax.ppermute(shares[k], 'grp', [(g, partner(g, k, groups)) for g in range...  1.95 us
  transfers between devices with their start and end apart: 4, of which 3 were waited for; matrix products, arithmetic and copies ran while one was open for 0% of the time, Pallas kernels for 1%

profile of v6, /device:TPU:0, one launch (start us, length us, event | category | flops | bytes accessed | tf_op | source)
XLA Modules:
  0.0 52.5 jit_solution(1145802189381367829)
XLA Ops:
  0.6 4.1 %shard_map.68 = (f32[1568,128]{1,0:T(8,128)S(1)}, f32[16,6,16,128]{3,2,1,0:T(8,128)S(1)}) custom-call(s32[1]{0:T(128)} %bitcast.1.refs_0_.refs_1_, s32[16]{0:T(128)} %refs_1_.1, f32[16,6,16,128]{3,2,1,0:T(8,128)} %bitcast.17, s32[16,16]{1,0:T(8,128)} %refs_3_.1, s32[16,16]{1,0:T(8,128)} %refs_4_.1, s32[16,16,128]{2,1,0:T(8,128)} %refs_5_.1), custom_call_target="tpu_custom_call" | custom-call | tf_op jit(solution)/shard_map/pallas_call | solution.py:419
  4.7 28.1 %all_to_all.10 = f32[1568,1,128]{2,1,0:T(1,128)S(1)} all-to-all(f32[1568,1,128]{2,1,0:T(1,128)S(1)} %bitcast.16), channel_id=1, replica_groups=mesh['scan'=8,'grp'=4] {'scan','grp'}, dimensions={0} | all-to-all | bytes 1605632 | tf_op jit(solution)/shard_map/all_to_all | solution.py:400
  32.8 3.4 %shard_map.69 = (f32[32,512]{1,0:T(8,128)S(1)}, f32[512,128]{1,0:T(8,128)}) custom-call(f32[16,6,16,128]{3,2,1,0:T(8,128)S(1)} %get-tuple-element.12.refs_0_, f32[1568,128]{1,0:T(8,128)S(1)} %bitcast.14), custom_call_target="tpu_custom_call" | custom-call | tf_op jit(solution)/shard_map/pallas_call | solution.py:385
  36.2 3.6 %all-to-all-start.1 = ((f32[512,1,128]{2,1,0:T(1,128)}), f32[512,1,128]{2,1,0:T(1,128)S(1)}, u32[]{:S(2)}, u32[]{:S(2)}) async-start(f32[512,1,128]{2,1,0:T(1,128)} %bitcast.7), calls=%async_computation.1 | async-start | bytes 524288 | tf_op jit(solution)/shard_map/all_to_all | solution.py:400
  39.8 0.5 shard_map.70
  40.3 0.3 collective-permute-start
  40.6 1.6 %collective-permute-start.1 = (f32[96,128]{1,0:T(8,128)S(1)}, f32[96,128]{1,0:T(8,128)S(1)}, u32[]{:S(2)}, u32[]{:S(2)}) collective-permute-start(f32[96,128]{1,0:T(8,128)S(1)} %get-tuple-element.18), channel_id=1, source_target_pairs={{0,2},{1,3},{2,0},{3,1},{4,6},{5,7},{6,4},{7,5},{8,10},{9,11},{10,... | collective-permute-start | bytes 147464 | tf_op jit(solution)/shard_map/ppermute | solution.py:454
  42.3 0.0 collective-permute-start.2
  42.3 0.0 collective-permute-done.refs_4_
  42.3 3.6 %collective-permute-done.1.refs_5_ = f32[96,128]{1,0:T(8,128)S(1)} collective-permute-done((f32[96,128]{1,0:T(8,128)S(1)}, f32[96,128]{1,0:T(8,128)S(1)}, u32[]{:S(2)}, u32[]{:S(2)}) %collective-permute-start.1) | collective-permute-done | bytes 49184 | tf_op jit(solution)/shard_map/ppermute | solution.py:454
  45.9 1.0 %collective-permute-done.2.refs_6_ = f32[96,128]{1,0:T(8,128)S(1)} collective-permute-done((f32[96,128]{1,0:T(8,128)S(1)}, f32[96,128]{1,0:T(8,128)S(1)}, u32[]{:S(2)}, u32[]{:S(2)}) %collective-permute-start.2) | collective-permute-done | bytes 49184 | tf_op jit(solution)/shard_map/ppermute | solution.py:454
  46.9 3.5 %all-to-all-done.1 = f32[512,1,128]{2,1,0:T(1,128)S(1)} async-done(((f32[512,1,128]{2,1,0:T(1,128)}), f32[512,1,128]{2,1,0:T(1,128)S(1)}, u32[]{:S(2)}, u32[]{:S(2)}) %all-to-all-start.1) | async-done | bytes 262176 | tf_op jit(solution)/shard_map/all_to_all | solution.py:400
  50.4 2.1 %shard_map.71 = (f32[36,16,32]{2,1,0:T(8,128)}, f32[4,6]{1,0:T(4,128)}) custom-call(s32[1]{0:T(128)} %bitcast.refs_0_, s32[1]{0:T(128)} %bitcast.1.refs_0_.refs_1_, f32[512,128]{1,0:T(8,128)S(1)} %bitcast.15, f32[96,128]{1,0:T(8,128)S(1)} %get-tuple-element.16.refs_3_, f32[96,128]{1,0:T(8,128)S(1)} %collective-permute-done.refs_4_, ...), custom_call_target="tpu_custom_call" | custom-call | tf_op jit(solution)/shard_map/pallas_call | solution.py:385
Async XLA Ops:
  36.2 14.2 %all-to-all-start.1 = ((f32[512,1,128]{2,1,0:T(1,128)}), f32[512,1,128]{2,1,0:T(1,128)S(1)}, u32[]{:S(2)}, u32[]{:S(2)}) async-start(f32[512,1,128]{2,1,0:T(1,128)} %bitcast.7), calls=%async_computation.1 | async-start | bytes 524288 | tf_op jit(solution)/shard_map/all_to_all | solution.py:400
  40.3 2.0 %collective-permute-start = (f32[96,128]{1,0:T(8,128)S(1)}, f32[96,128]{1,0:T(8,128)S(1)}, u32[]{:S(2)}, u32[]{:S(2)}) collective-permute-start(f32[96,128]{1,0:T(8,128)S(1)} %get-tuple-element.17), channel_id=1, source_target_pairs={{0,1},{1,0},{2,3},{3,2},{4,5},{5,4},{6,7},{7,6},{8,9},{9,8},{10,11... | collective-permute-start | bytes 147464 | tf_op jit(solution)/shard_map/ppermute | solution.py:454
  40.6 5.3 %collective-permute-start.1 = (f32[96,128]{1,0:T(8,128)S(1)}, f32[96,128]{1,0:T(8,128)S(1)}, u32[]{:S(2)}, u32[]{:S(2)}) collective-permute-start(f32[96,128]{1,0:T(8,128)S(1)} %get-tuple-element.18), channel_id=1, source_target_pairs={{0,2},{1,3},{2,0},{3,1},{4,6},{5,7},{6,4},{7,5},{8,10},{9,11},{10,... | collective-permute-start | bytes 147464 | tf_op jit(solution)/shard_map/ppermute | solution.py:454
  42.3 4.7 %collective-permute-start.2 = (f32[96,128]{1,0:T(8,128)S(1)}, f32[96,128]{1,0:T(8,128)S(1)}, u32[]{:S(2)}, u32[]{:S(2)}) collective-permute-start(f32[96,128]{1,0:T(8,128)S(1)} %get-tuple-element.19), channel_id=1, source_target_pairs={{0,3},{1,2},{2,1},{3,0},{4,7},{5,6},{6,5},{7,4},{8,11},{9,10},{10,... | collective-permute-start | bytes 147464 | tf_op jit(solution)/shard_map/ppermute | solution.py:454

commit v7 on v6

--- a/solution.py
+++ b/solution.py
@@ -60,6 +60,7 @@
 def send_kernel(
     devices,
     groups,
+    place_ref,
     group_ref,
     count_hbm,
     samples_hbm,
@@ -154,7 +155,7 @@
             samples_ref[s, a] = jnp.where(present, samples_ref[s, a], 0.0)
         return carry
 
-    lax.fori_loop(0, scan_local, one_scan, 0, unroll=4)
+    lax.fori_loop(0, scan_local, one_scan, 0, unroll=8)
 
     for a in range(COORDS):
         parts = [dot(place, part) for part in pieces(data_ref[a], 3)]
@@ -170,18 +171,26 @@
 
 def back_layout(scan_local, groups, cap):
     span = groups * cap
-    return span, HEAD * span // LANES, WIDTH * scan_local // LANES
+    slot_rows = HEAD * span // LANES
+    sum_rows = WIDTH * scan_local // LANES
+    if FIELDS * (scan_local // groups) <= span:
+        turns, grad_row = divmod(HEAD - 1, slot_rows)
+        grad_lane, used = turns * span, slot_rows
+    else:
+        grad_row, grad_lane, used = slot_rows, 0, slot_rows + 1
+    return span, slot_rows, sum_rows, grad_row, grad_lane, max(used, sum_rows)
 
 
 def partner(index, k, groups):
     return index ^ k if groups & (groups - 1) == 0 else (index + k) % groups
 
 
-def pair_kernel(devices, groups, samples_ref, recv_ref, flat_ref, back_ref, point_ref, mate_ref, note_ref):
+def pair_kernel(devices, groups, place_ref, samples_ref, recv_ref, flat_ref, back_ref, point_ref, mate_ref, note_ref):
     scan_local, _, tiles, _ = samples_ref.shape
     slots = flat_ref.shape[1]
     cap = slots // devices
     block = COORDS * cap + 1
+    scans = devices // groups
     for d in range(devices):
         note_ref[pl.ds(d, 1), :] = recv_ref[pl.ds(d * block + COORDS * cap, 1), :]
     notes = note_ref[...].astype(jnp.bfloat16)
@@ -225,7 +234,7 @@
             return tuple(s + t for s, t in zip(sums, terms))
 
         zero = jnp.zeros((8, LANES), jnp.float32)
-        sums = lax.fori_loop(0, LANES // 8, step, (zero,) * (MAT + FIELDS), unroll=4)
+        sums = lax.fori_loop(0, LANES // 8, step, (zero,) * (MAT + FIELDS), unroll=16)
         filled = flag_row[:, lanes] > 0.0
         lines = [jnp.where(filled, jnp.sum(s, axis=0, keepdims=True), 0.0) for s in sums]
         blank = jnp.zeros((1, LANES), jnp.float32)
@@ -233,14 +242,29 @@
         lines += [blank] * (WIDTH - len(lines))
         flat_ref[:, lanes] = jnp.concatenate(lines, axis=0)
     scans = devices // groups
-    span, slot_rows, sum_rows = back_layout(scan_local, groups, cap)
-    source = div(div(iota((1, slots), 1), cap), groups) * scan_local + flag_row.astype(jnp.int32) - 1
-    source = jnp.where(flag_row > 0.0, source, -1)
+    span, slot_rows, sum_rows, grad_row, grad_lane, rows = back_layout(scan_local, groups, cap)
+    columns = scans * scan_local // groups
+    near_group = div(place_ref[0] * scan_local, columns)
+    peer = div(div(iota((1, slots), 1), cap), groups)
+    member = flag_row.astype(jnp.int32) - 1
+    source = jnp.where(member >= 0, peer * scan_local + member, -1)
     source_hot = (iota((scans * scan_local, slots), 0) == source).astype(jnp.float32).astype(jnp.bfloat16)
     parts = [dot(part, source_hot, BOTH_LANES) for part in pieces(flat_ref[...], 3)]
     sums = (parts[0] + parts[1]) + parts[2]
+    share = scan_local // groups
+    few = iota((FIELDS * share, slots), 0)
+    chosen = jnp.concatenate(
+        [jnp.broadcast_to(flat_ref[HEAD + q : HEAD + q + 1, :], (share, slots)) for q in range(FIELDS)], axis=0
+    )
+    chosen = jnp.where(member == near_group * share + mod(few, share), chosen, 0.0)
+    blank = [jnp.zeros((n, slots), jnp.float32) for n in (grad_lane, LANES - grad_lane - FIELDS * share)]
+    chosen = jnp.concatenate([blank[0], chosen, blank[1]] if grad_lane else [chosen, blank[1]], axis=0)
+    peer_hot = (iota((scans, slots), 0) == peer).astype(jnp.float32).astype(jnp.bfloat16)
+    parts = [dot(peer_hot, part, BOTH_LANES) for part in pieces(chosen, 3)]
+    grads = (parts[0] + parts[1]) + parts[2]
     slot_lane = div(iota((slot_rows, LANES), 1), span)
     sum_lane = div(iota((sum_rows, LANES), 1), scan_local)
+    tails = []
     for scan in range(scans):
         c, start = divmod(scan * span, LANES)
         body = None
@@ -248,15 +272,32 @@
             piece = flat_ref[i * slot_rows : (i + 1) * slot_rows, c * LANES : (c + 1) * LANES]
             piece = turn(piece, i * span - start)
             body = piece if i == 0 else jnp.where(slot_lane == i, piece, body)
+        if grad_row < slot_rows:
+            body = jnp.where(
+                (iota((slot_rows, LANES), 0) == grad_row) & (iota((slot_rows, LANES), 1) >= grad_lane),
+                grads[scan : scan + 1],
+                body,
+            )
         c, start = divmod(scan * scan_local, LANES)
         tail = None
         for i in range(WIDTH // sum_rows):
             piece = turn(sums[i * sum_rows : (i + 1) * sum_rows, c * LANES : (c + 1) * LANES], i * scan_local - start)
             tail = piece if i == 0 else jnp.where(sum_lane == i, piece, tail)
+        tails.append(tail)
         for c in range(groups):
-            at = (scan * groups + c) * (slot_rows + sum_rows)
+            at = (scan * groups + c) * rows
             back_ref[at : at + slot_rows, :] = body
-            back_ref[at + slot_rows : at + slot_rows + sum_rows, :] = tail
+            if rows > slot_rows:
+                back_ref[at + slot_rows : at + rows, :] = jnp.broadcast_to(
+                    grads[scan : scan + 1], (rows - slot_rows, LANES)
+                )
+    for c in range(groups):
+
+        @pl.when(near_group != c)
+        def _():
+            for scan in range(scans):
+                at = (scan * groups + c) * rows
+                back_ref[at : at + sum_rows, :] = tails[scan]
 
 
 def layout(scan_local, groups, scan_total):
@@ -317,8 +358,7 @@
     part_refs, (hess_ref, grad_ref, every_ref, hold_ref) = refs[:groups], refs[groups:]
     scan_local, columns = hess_ref.shape[1:]
     per_block = part_refs[0].shape[0] // scan_local
-    span, slot_rows, sum_rows = back_layout(scan_local, groups, cap)
-    block = slot_rows + sum_rows
+    span, slot_rows, sum_rows, grad_row, grad_lane, block = back_layout(scan_local, groups, cap)
     senders = devices // groups
     first = group_ref[0] * (senders * block)
     lane_block = div(iota((slot_rows, LANES), 1), span)
@@ -337,11 +377,20 @@
     mate = every[ROW_MATE : ROW_MATE + 1].astype(jnp.int32)
     column = div(div(iota((1, total), 1), span), groups) * scan_local + mate
     row_hot = iota((scan_local, total), 0) == row
-    mix = (iota((columns, total), 0) == column).astype(jnp.float32).astype(jnp.bfloat16)
+    offset = scan_ref[0] * scan_local - group_ref[0] * columns
+    line = iota((columns, total), 0)
+    mix = (line == row + offset).astype(jnp.float32) - (line == column).astype(jnp.float32)
+    mix = mix.astype(jnp.bfloat16)
     cross = sum(dot(rows, mix, BOTH_LANES) for rows in block_rows(every, row_hot, MAT))
-    sums = back_ref[slot_rows:block, :]
-    for d in range(1, devices):
-        sums = sums + back_ref[d * block + slot_rows : (d + 1) * block, :]
+    sums = jnp.zeros((sum_rows, LANES), jnp.float32)
+    for c in range(groups):
+        part = back_ref[c * senders * block : c * senders * block + sum_rows, :]
+        for d in range(c * senders + 1, (c + 1) * senders):
+            part = part + back_ref[d * block : d * block + sum_rows, :]
+        sums = sums + jnp.where(group_ref[0] != c, part, 0.0)
+    near = back_ref[pl.ds(first + grad_row, 1), :]
+    for u in range(1, senders):
+        near = near + back_ref[pl.ds(first + u * block + grad_row, 1), :]
     line = iota((scan_local, LANES), 0)
     lane = iota((scan_local, LANES), 1)
 
@@ -352,12 +401,11 @@
     whole = part_refs[0][...]
     for part_ref in part_refs[1:]:
         whole = whole + part_ref[...]
-    offset = scan_ref[0] * scan_local - group_ref[0] * columns
     diagonal = iota((scan_local, columns), 1) == iota((scan_local, columns), 0) + offset
     for q in range(MAT):
         k, r = divmod(q, per_block)
         tile = whole[r * scan_local : (r + 1) * scan_local, k * columns : (k + 1) * columns]
-        tile = tile - cross[q * scan_local : (q + 1) * scan_local]
+        tile = tile + cross[q * scan_local : (q + 1) * scan_local]
         tile = tile + jnp.where(diagonal, by_row(q), 0.0)
         i, j = PAIRS[q]
         hess_ref[i * FIELDS + j] = tile
@@ -369,7 +417,13 @@
         grad = grad + jnp.where(lane == q, by_row(HEAD + q), 0.0)
     hold_ref[...] = grad
     part = scan_local // groups
-    grad_ref[...] = hold_ref[pl.ds(group_ref[0] * part, part), 0:FIELDS]
+    own = jnp.zeros((part, LANES), jnp.float32)
+    for q in range(FIELDS):
+        spot = grad_lane + q * part + iota((part, LANES), 0) == iota((part, LANES), 1)
+        value = jnp.sum(jnp.where(spot, near, 0.0), axis=1, keepdims=True)
+        own = jnp.where(iota((part, LANES), 1) == q, value, own)
+    hold = hold_ref[pl.ds(group_ref[0] * part, part), :] + own
+    grad_ref[...] = hold[:, 0:FIELDS]
 
 
 def call(kernel, out_shape, smem, vmem, scratch=()):
@@ -411,7 +465,7 @@
     columns, pack, per_block = layout(scan_local, groups, scan_total)
     group = lax.axis_index("grp").astype(jnp.int32).reshape(1)
     scan = lax.axis_index("scan").astype(jnp.int32).reshape(1)
-    _, slot_rows, sum_rows = back_layout(scan_local, groups, cap)
+    back_rows = back_layout(scan_local, groups, cap)[-1]
 
     def bind(kernel, *args):
         return lambda *refs: kernel(*args, *refs)
@@ -419,7 +473,7 @@
     sent, samples = pl.pallas_call(
         bind(send_kernel, devices, groups),
         out_shape=(near(devices * block, LANES), near(*samples.shape)),
-        in_specs=[pl.BlockSpec(memory_space=pltpu.SMEM)] + [pl.BlockSpec(memory_space=pl.ANY)] * 5,
+        in_specs=[pl.BlockSpec(memory_space=pltpu.SMEM)] * 2 + [pl.BlockSpec(memory_space=pl.ANY)] * 5,
         scratch_shapes=[
             pltpu.SMEM(point_count.shape, jnp.int32),
             pltpu.VMEM(corr_scan.shape, jnp.int32),
@@ -428,19 +482,19 @@
             pltpu.VMEM((COORDS, entries, LANES), jnp.float32),
             pltpu.SemaphoreType.DMA((5,)),
         ],
-    )(group, point_count, samples, corr_scan, corr_tile, corr_src)
+    )(scan, group, point_count, samples, corr_scan, corr_tile, corr_src)
     received = exchange(sent, AXES)
     flat, back = call(
         bind(pair_kernel, devices, groups),
-        (near(WIDTH, slots), near(devices * (slot_rows + sum_rows), LANES)),
-        0,
+        (near(WIDTH, slots), near(devices * back_rows, LANES)),
+        1,
         2,
         [
             pltpu.VMEM((COORDS, LANES, slots), jnp.float32),
             pltpu.VMEM((FIELDS, LANES, slots), jnp.float32),
             pltpu.VMEM((devices, LANES), jnp.float32),
         ],
-    )(samples, received)
+    )(scan, samples, received)
     back = exchange(back, AXES)
     share = near(per_block * scan_local, LANES)
     shares = call(

time: 52.7 us -> 50.7 us (0.962)
  waiting for transfers between devices: 8.11 us -> 6.49 us
    all_to_all x1, waiting for transfers between devices: 3.46 us -> 2.01 us  [exchange(): lax.all_to_all(x.reshape(count, 1, width), axes, split_axis=0, concat_axi...]
where the time goes in v7:
time: 50.7 us; the launch traced here: 50.4 us
  blocking collectives  28.1 us (55%)
  Pallas kernels  9.62 us (19%)
  waiting for transfers between devices  6.49 us (13%)
  starting transfers between devices  5.57 us (11%)
  between operations  0.67 us (1%)
    all_to_all x1, blocking collectives, exchange(): lax.all_to_all(x.reshape(count, 1, width), axes, split_axis=0, concat_axi...  28.1 us
    pallas_call x3, Pallas kernels, run(): return body(*args)  5.69 us
    ppermute x3, waiting for transfers between devices, local(): lax.ppermute(shares[k], 'grp', [(g, partner(g, k, groups)) for g in range...  4.48 us
    pallas_call x1, Pallas kernels, local(): pl.pallas_call(bind(send_kernel, devices, groups), out_shape=(near(device...  3.94 us
    all_to_all x1, starting transfers between devices, exchange(): lax.all_to_all(x.reshape(count, 1, width), axes, split_axis=0, concat_axi...  3.62 us
    all_to_all x1, waiting for transfers between devices, exchange(): lax.all_to_all(x.reshape(count, 1, width), axes, split_axis=0, concat_axi...  2.01 us
    ppermute x3, starting transfers between devices, local(): lax.ppermute(shares[k], 'grp', [(g, partner(g, k, groups)) for g in range...  1.95 us
  transfers between devices with their start and end apart: 4, of which 3 were waited for; matrix products, arithmetic and copies ran while one was open for 0% of the time, Pallas kernels for 1%

profile of v7, /device:TPU:0, one launch (start us, length us, event | category | flops | bytes accessed | tf_op | source)
XLA Modules:
  0.0 50.4 jit_solution(223936192484870841)
XLA Ops:
  0.6 3.9 %shard_map.68 = (f32[1568,128]{1,0:T(8,128)S(1)}, f32[16,6,16,128]{3,2,1,0:T(8,128)S(1)}) custom-call(s32[1]{0:T(128)} %bitcast.refs_0_, s32[1]{0:T(128)} %bitcast.1.refs_1_, s32[16]{0:T(128)} %refs_2_.1, f32[16,6,16,128]{3,2,1,0:T(8,128)} %bitcast.17, s32[16,16]{1,0:T(8,128)} %refs_4_.1, s32[16,16]{1,0:T(8,128)} %refs_5_.1, s32[16,16,128]{2,1,0:T(8,128)} %refs_6_.1), custom_call_target="tpu_custom_call" | custom-call | tf_op jit(solution)/shard_map/pallas_call | solution.py:473
  4.6 28.1 %all_to_all.10 = f32[1568,1,128]{2,1,0:T(1,128)S(1)} all-to-all(f32[1568,1,128]{2,1,0:T(1,128)S(1)} %bitcast.15), channel_id=1, replica_groups=mesh['scan'=8,'grp'=4] {'scan','grp'}, dimensions={0} | all-to-all | bytes 1605632 | tf_op jit(solution)/shard_map/all_to_all | solution.py:454
  32.7 2.9 %shard_map.69 = (f32[32,512]{1,0:T(8,128)S(1)}, f32[384,128]{1,0:T(8,128)}) custom-call(s32[1]{0:T(128)} %bitcast.refs_0_, f32[16,6,16,128]{3,2,1,0:T(8,128)S(1)} %get-tuple-element.12.refs_1_, f32[1568,128]{1,0:T(8,128)S(1)} %bitcast.14), custom_call_target="tpu_custom_call" | custom-call | tf_op jit(solution)/shard_map/pallas_call | solution.py:439
  35.6 3.6 %all-to-all-start.1 = ((f32[384,1,128]{2,1,0:T(1,128)}), f32[384,1,128]{2,1,0:T(1,128)S(1)}, u32[]{:S(2)}, u32[]{:S(2)}) async-start(f32[384,1,128]{2,1,0:T(1,128)} %bitcast.7), calls=%async_computation.1 | async-start | bytes 393216 | tf_op jit(solution)/shard_map/all_to_all | solution.py:454
  39.2 0.5 shard_map.70
  39.7 0.3 collective-permute-start
  40.0 1.6 %collective-permute-start.1 = (f32[96,128]{1,0:T(8,128)S(1)}, f32[96,128]{1,0:T(8,128)S(1)}, u32[]{:S(2)}, u32[]{:S(2)}) collective-permute-start(f32[96,128]{1,0:T(8,128)S(1)} %get-tuple-element.18), channel_id=1, source_target_pairs={{0,2},{1,3},{2,0},{3,1},{4,6},{5,7},{6,4},{7,5},{8,10},{9,11},{10,... | collective-permute-start | bytes 147464 | tf_op jit(solution)/shard_map/ppermute | solution.py:508
  41.6 0.0 collective-permute-start.2
  41.7 0.0 collective-permute-done.refs_4_
  41.7 3.0 %collective-permute-done.1.refs_5_ = f32[96,128]{1,0:T(8,128)S(1)} collective-permute-done((f32[96,128]{1,0:T(8,128)S(1)}, f32[96,128]{1,0:T(8,128)S(1)}, u32[]{:S(2)}, u32[]{:S(2)}) %collective-permute-start.1) | collective-permute-done | bytes 49184 | tf_op jit(solution)/shard_map/ppermute | solution.py:508
  44.6 1.5 %collective-permute-done.2.refs_6_ = f32[96,128]{1,0:T(8,128)S(1)} collective-permute-done((f32[96,128]{1,0:T(8,128)S(1)}, f32[96,128]{1,0:T(8,128)S(1)}, u32[]{:S(2)}, u32[]{:S(2)}) %collective-permute-start.2) | collective-permute-done | bytes 49184 | tf_op jit(solution)/shard_map/ppermute | solution.py:508
  46.1 2.0 %all-to-all-done.1 = f32[384,1,128]{2,1,0:T(1,128)S(1)} async-done(((f32[384,1,128]{2,1,0:T(1,128)}), f32[384,1,128]{2,1,0:T(1,128)S(1)}, u32[]{:S(2)}, u32[]{:S(2)}) %all-to-all-start.1) | async-done | bytes 196640 | tf_op jit(solution)/shard_map/all_to_all | solution.py:454
  48.1 2.3 %shard_map.71 = (f32[36,16,32]{2,1,0:T(8,128)}, f32[4,6]{1,0:T(4,128)}) custom-call(s32[1]{0:T(128)} %bitcast.refs_0_, s32[1]{0:T(128)} %bitcast.1.refs_1_, f32[384,128]{1,0:T(8,128)S(1)} %bitcast.16, f32[96,128]{1,0:T(8,128)S(1)} %get-tuple-element.16.refs_3_, f32[96,128]{1,0:T(8,128)S(1)} %collective-permute-done.refs_4_, ...), custom_call_target="tpu_custom_call" | custom-call | tf_op jit(solution)/shard_map/pallas_call | solution.py:439
Async XLA Ops:
  35.6 12.6 %all-to-all-start.1 = ((f32[384,1,128]{2,1,0:T(1,128)}), f32[384,1,128]{2,1,0:T(1,128)S(1)}, u32[]{:S(2)}, u32[]{:S(2)}) async-start(f32[384,1,128]{2,1,0:T(1,128)} %bitcast.7), calls=%async_computation.1 | async-start | bytes 393216 | tf_op jit(solution)/shard_map/all_to_all | solution.py:454
  39.7 2.0 %collective-permute-start = (f32[96,128]{1,0:T(8,128)S(1)}, f32[96,128]{1,0:T(8,128)S(1)}, u32[]{:S(2)}, u32[]{:S(2)}) collective-permute-start(f32[96,128]{1,0:T(8,128)S(1)} %get-tuple-element.17), channel_id=1, source_target_pairs={{0,1},{1,0},{2,3},{3,2},{4,5},{5,4},{6,7},{7,6},{8,9},{9,8},{10,11... | collective-permute-start | bytes 147464 | tf_op jit(solution)/shard_map/ppermute | solution.py:508
  40.0 4.6 %collective-permute-start.1 = (f32[96,128]{1,0:T(8,128)S(1)}, f32[96,128]{1,0:T(8,128)S(1)}, u32[]{:S(2)}, u32[]{:S(2)}) collective-permute-start(f32[96,128]{1,0:T(8,128)S(1)} %get-tuple-element.18), channel_id=1, source_target_pairs={{0,2},{1,3},{2,0},{3,1},{4,6},{5,7},{6,4},{7,5},{8,10},{9,11},{10,... | collective-permute-start | bytes 147464 | tf_op jit(solution)/shard_map/ppermute | solution.py:508
  41.6 4.5 %collective-permute-start.2 = (f32[96,128]{1,0:T(8,128)S(1)}, f32[96,128]{1,0:T(8,128)S(1)}, u32[]{:S(2)}, u32[]{:S(2)}) collective-permute-start(f32[96,128]{1,0:T(8,128)S(1)} %get-tuple-element.19), channel_id=1, source_target_pairs={{0,3},{1,2},{2,1},{3,0},{4,7},{5,6},{6,5},{7,4},{8,11},{9,10},{10,... | collective-permute-start | bytes 147464 | tf_op jit(solution)/shard_map/ppermute | solution.py:508

commit v8 on v7

--- a/solution.py
+++ b/solution.py
@@ -157,11 +157,11 @@
 
     lax.fori_loop(0, scan_local, one_scan, 0, unroll=8)
 
+    thirds = [jnp.concatenate(part, axis=1) for part in zip(*[pieces(data_ref[a], 3) for a in range(COORDS)])]
+    moved = dot(jnp.concatenate([place] * 3, axis=1), jnp.concatenate(thirds, axis=0))
     for a in range(COORDS):
-        parts = [dot(place, part) for part in pieces(data_ref[a], 3)]
-        moved = (parts[0] + parts[1]) + parts[2]
         for d in range(devices):
-            out_ref[pl.ds(d * block + a * cap, cap), :] = moved[d * cap : (d + 1) * cap]
+            out_ref[pl.ds(d * block + a * cap, cap), :] = moved[d * cap : (d + 1) * cap, a * LANES : (a + 1) * LANES]
 
 
 def turn(x, amount):
@@ -185,7 +185,7 @@
     return index ^ k if groups & (groups - 1) == 0 else (index + k) % groups
 
 
-def pair_kernel(devices, groups, place_ref, samples_ref, recv_ref, flat_ref, back_ref, point_ref, mate_ref, note_ref):
+def pair_kernel(devices, groups, place_ref, samples_ref, recv_ref, flat_ref, back_hbm, back_ref, point_ref, mate_ref, note_ref, sems):
     scan_local, _, tiles, _ = samples_ref.shape
     slots = flat_ref.shape[1]
     cap = slots // devices
@@ -217,6 +217,15 @@
                 recv_ref[pl.ds(d * block + a * cap, cap), :] for d in range(c * per_chunk, (c + 1) * per_chunk)
             ]
             point_ref[a, :, c * LANES : (c + 1) * LANES] = jnp.concatenate(stack, axis=0).T
+    span, slot_rows, sum_rows, grad_row, grad_lane, rows = back_layout(scan_local, groups, cap)
+    near_group = div(place_ref[0] * scan_local, scans * scan_local // groups)
+    share = scan_local // groups
+    slot_lane = div(iota((slot_rows, LANES), 1), span)
+    sum_lane = div(iota((sum_rows, LANES), 1), scan_local)
+    grad_spot = (iota((slot_rows, LANES), 0) == grad_row) & (iota((slot_rows, LANES), 1) >= grad_lane)
+    peer = div(iota((1, LANES), 1), span)
+    per_line = LANES // span
+    stores = []
     for c in range(slots // LANES):
         lanes = slice(c * LANES, (c + 1) * LANES)
 
@@ -240,64 +249,47 @@
         blank = jnp.zeros((1, LANES), jnp.float32)
         lines[MAT:MAT] = [flag_row[:, lanes], mate_row[:, lanes], blank]
         lines += [blank] * (WIDTH - len(lines))
-        flat_ref[:, lanes] = jnp.concatenate(lines, axis=0)
-    scans = devices // groups
-    span, slot_rows, sum_rows, grad_row, grad_lane, rows = back_layout(scan_local, groups, cap)
-    columns = scans * scan_local // groups
-    near_group = div(place_ref[0] * scan_local, columns)
-    peer = div(div(iota((1, slots), 1), cap), groups)
-    member = flag_row.astype(jnp.int32) - 1
-    source = jnp.where(member >= 0, peer * scan_local + member, -1)
-    source_hot = (iota((scans * scan_local, slots), 0) == source).astype(jnp.float32).astype(jnp.bfloat16)
-    parts = [dot(part, source_hot, BOTH_LANES) for part in pieces(flat_ref[...], 3)]
-    sums = (parts[0] + parts[1]) + parts[2]
-    share = scan_local // groups
-    few = iota((FIELDS * share, slots), 0)
-    chosen = jnp.concatenate(
-        [jnp.broadcast_to(flat_ref[HEAD + q : HEAD + q + 1, :], (share, slots)) for q in range(FIELDS)], axis=0
-    )
-    chosen = jnp.where(member == near_group * share + mod(few, share), chosen, 0.0)
-    blank = [jnp.zeros((n, slots), jnp.float32) for n in (grad_lane, LANES - grad_lane - FIELDS * share)]
-    chosen = jnp.concatenate([blank[0], chosen, blank[1]] if grad_lane else [chosen, blank[1]], axis=0)
-    peer_hot = (iota((scans, slots), 0) == peer).astype(jnp.float32).astype(jnp.bfloat16)
-    parts = [dot(peer_hot, part, BOTH_LANES) for part in pieces(chosen, 3)]
-    grads = (parts[0] + parts[1]) + parts[2]
-    slot_lane = div(iota((slot_rows, LANES), 1), span)
-    sum_lane = div(iota((sum_rows, LANES), 1), scan_local)
-    tails = []
-    for scan in range(scans):
-        c, start = divmod(scan * span, LANES)
-        body = None
-        for i in range(LANES // span):
-            piece = flat_ref[i * slot_rows : (i + 1) * slot_rows, c * LANES : (c + 1) * LANES]
-            piece = turn(piece, i * span - start)
-            body = piece if i == 0 else jnp.where(slot_lane == i, piece, body)
-        if grad_row < slot_rows:
-            body = jnp.where(
-                (iota((slot_rows, LANES), 0) == grad_row) & (iota((slot_rows, LANES), 1) >= grad_lane),
-                grads[scan : scan + 1],
-                body,
-            )
-        c, start = divmod(scan * scan_local, LANES)
-        tail = None
-        for i in range(WIDTH // sum_rows):
-            piece = turn(sums[i * sum_rows : (i + 1) * sum_rows, c * LANES : (c + 1) * LANES], i * scan_local - start)
-            tail = piece if i == 0 else jnp.where(sum_lane == i, piece, tail)
-        tails.append(tail)
-        for c in range(groups):
-            at = (scan * groups + c) * rows
-            back_ref[at : at + slot_rows, :] = body
-            if rows > slot_rows:
-                back_ref[at + slot_rows : at + rows, :] = jnp.broadcast_to(
-                    grads[scan : scan + 1], (rows - slot_rows, LANES)
-                )
-    for c in range(groups):
-
-        @pl.when(near_group != c)
-        def _():
-            for scan in range(scans):
-                at = (scan * groups + c) * rows
-                back_ref[at : at + sum_rows, :] = tails[scan]
+        flat = jnp.concatenate(lines, axis=0)
+        flat_ref[:, lanes] = flat
+        member = flag_row[:, lanes].astype(jnp.int32) - 1
+        source = jnp.where(member >= 0, peer * scan_local + member, -1)
+        source_hot = (iota((LANES, LANES), 0) == source).astype(jnp.float32).astype(jnp.bfloat16)
+        totals = dot(
+            jnp.concatenate(pieces(flat, 3), axis=1), jnp.concatenate([source_hot] * 3, axis=1), BOTH_LANES
+        )
+        chosen = jnp.concatenate(
+            [jnp.broadcast_to(flat[HEAD + q : HEAD + q + 1, :], (share, LANES)) for q in range(FIELDS)], axis=0
+        )
+        chosen = jnp.where(member == near_group * share + mod(iota(chosen.shape, 0), share), chosen, 0.0)
+        below = jnp.zeros((LANES - grad_lane - FIELDS * share, LANES), jnp.float32)
+        above = [jnp.zeros((grad_lane, LANES), jnp.float32)] if grad_lane else []
+        chosen = jnp.concatenate(above + [chosen, below], axis=0)
+        peer_hot = (iota((8, LANES), 0) == peer).astype(jnp.float32).astype(jnp.bfloat16)
+        grads = dot(
+            jnp.concatenate([peer_hot] * 3, axis=1), jnp.concatenate(pieces(chosen, 3), axis=1), BOTH_LANES
+        )
+        for u in range(per_line):
+            body = None
+            for i in range(per_line):
+                piece = turn(flat[i * slot_rows : (i + 1) * slot_rows], (i - u) * span)
+                body = piece if i == 0 else jnp.where(slot_lane == i, piece, body)
+            if grad_row < slot_rows:
+                body = jnp.where(grad_spot, grads[u : u + 1], body)
+            else:
+                body = jnp.concatenate([body, grads[u : u + 1]], axis=0)
+            tail = None
+            for i in range(WIDTH // sum_rows):
+                piece = turn(totals[i * sum_rows : (i + 1) * sum_rows], (i - u) * scan_local)
+                tail = piece if i == 0 else jnp.where(sum_lane == i, piece, tail)
+            for g in range(groups):
+                at = ((c * per_line + u) * groups + g) * rows
+                back_ref[at : at + body.shape[0], :] = body
+                back_ref[at : at + sum_rows, :] = jnp.where(near_group != g, tail, body[0:sum_rows])
+        at = pl.ds(c * per_line * groups * rows, per_line * groups * rows)
+        stores.append(pltpu.make_async_copy(back_ref.at[at], back_hbm.at[at], sems.at[c]))
+        stores[-1].start()
+    for store in stores:
+        store.wait()
 
 
 def layout(scan_local, groups, scan_total):
@@ -381,7 +373,8 @@
     line = iota((columns, total), 0)
     mix = (line == row + offset).astype(jnp.float32) - (line == column).astype(jnp.float32)
     mix = mix.astype(jnp.bfloat16)
-    cross = sum(dot(rows, mix, BOTH_LANES) for rows in block_rows(every, row_hot, MAT))
+    rows = jnp.concatenate(list(block_rows(every, row_hot, MAT)), axis=1)
+    cross = dot(rows, jnp.concatenate([mix, mix], axis=1), BOTH_LANES)
     sums = jnp.zeros((sum_rows, LANES), jnp.float32)
     for c in range(groups):
         part = back_ref[c * senders * block : c * senders * block + sum_rows, :]
@@ -402,11 +395,14 @@
     for part_ref in part_refs[1:]:
         whole = whole + part_ref[...]
     diagonal = iota((scan_local, columns), 1) == iota((scan_local, columns), 0) + offset
+    shifted = pltpu.roll(sums, mod(offset + LANES * (devices // groups), LANES), 1)
+    facing = [turn(shifted, -n * scan_local) for n in range(WIDTH // sum_rows)]
     for q in range(MAT):
         k, r = divmod(q, per_block)
         tile = whole[r * scan_local : (r + 1) * scan_local, k * columns : (k + 1) * columns]
         tile = tile + cross[q * scan_local : (q + 1) * scan_local]
-        tile = tile + jnp.where(diagonal, by_row(q), 0.0)
+        n, r = divmod(q, sum_rows)
+        tile = tile + jnp.where(diagonal, facing[n][r : r + 1, 0:columns], 0.0)
         i, j = PAIRS[q]
         hess_ref[i * FIELDS + j] = tile
         if i != j:
@@ -426,12 +422,13 @@
     grad_ref[...] = hold[:, 0:FIELDS]
 
 
-def call(kernel, out_shape, smem, vmem, scratch=()):
+def call(kernel, out_shape, smem, vmem, scratch=(), out_specs=None):
     body = pl.pallas_call(
         kernel,
         out_shape=out_shape,
         in_specs=[pl.BlockSpec(memory_space=pltpu.SMEM)] * smem + [pl.BlockSpec(memory_space=pltpu.VMEM)] * vmem,
         scratch_shapes=list(scratch),
+        **({} if out_specs is None else {"out_specs": out_specs}),
     )
 
     def run(*args):
@@ -486,14 +483,17 @@
     received = exchange(sent, AXES)
     flat, back = call(
         bind(pair_kernel, devices, groups),
-        (near(WIDTH, slots), near(devices * back_rows, LANES)),
+        (near(WIDTH, slots), f32(devices * back_rows, LANES)),
         1,
         2,
         [
+            pltpu.VMEM((devices * back_rows, LANES), jnp.float32),
             pltpu.VMEM((COORDS, LANES, slots), jnp.float32),
             pltpu.VMEM((FIELDS, LANES, slots), jnp.float32),
             pltpu.VMEM((devices, LANES), jnp.float32),
+            pltpu.SemaphoreType.DMA((slots // LANES,)),
         ],
+        (pl.BlockSpec(memory_space=pltpu.VMEM), pl.BlockSpec(memory_space=pl.ANY)),
     )(scan, samples, received)
     back = exchange(back, AXES)
     share = near(per_block * scan_local, LANES)

time: 50.7 us -> 49.3 us (0.972)
  Pallas kernels: 9.62 us -> 8.21 us
    pallas_call x3, Pallas kernels: 5.69 us -> 4.48 us  [run(): return body(*args)]
where the time goes in v8:
time: 49.3 us; the launch traced here: 49 us
  blocking collectives  28.1 us (57%)
  Pallas kernels  8.21 us (17%)
  waiting for transfers between devices  6.49 us (13%)
  starting transfers between devices  5.58 us (11%)
  between operations  0.67 us (1%)
    all_to_all x1, blocking collectives, exchange(): lax.all_to_all(x.reshape(count, 1, width), axes, split_axis=0, concat_axi...  28.1 us
    ppermute x3, waiting for transfers between devices, local(): lax.ppermute(shares[k], 'grp', [(g, partner(g, k, groups)) for g in range...  4.49 us
    pallas_call x3, Pallas kernels, run(): return body(*args)  4.48 us
    pallas_call x1, Pallas kernels, local(): pl.pallas_call(bind(send_kernel, devices, groups), out_shape=(near(device...  3.73 us
    all_to_all x1, starting transfers between devices, exchange(): lax.all_to_all(x.reshape(count, 1, width), axes, split_axis=0, concat_axi...  3.63 us
    all_to_all x1, waiting for transfers between devices, exchange(): lax.all_to_all(x.reshape(count, 1, width), axes, split_axis=0, concat_axi...  2 us
    ppermute x3, starting transfers between devices, local(): lax.ppermute(shares[k], 'grp', [(g, partner(g, k, groups)) for g in range...  1.96 us
  transfers between devices with their start and end apart: 4, of which 3 were waited for; matrix products, arithmetic and copies ran while one was open for 0% of the time, Pallas kernels for 1%

profile of v8, /device:TPU:0, one launch (start us, length us, event | category | flops | bytes accessed | tf_op | source)
XLA Modules:
  0.0 49.0 jit_solution(961632479849755917)
XLA Ops:
  0.6 3.7 %shard_map.68 = (f32[1568,128]{1,0:T(8,128)S(1)}, f32[16,6,16,128]{3,2,1,0:T(8,128)S(1)}) custom-call(s32[1]{0:T(128)} %bitcast.refs_0_, s32[1]{0:T(128)} %bitcast.1.refs_1_, s32[16]{0:T(128)} %refs_2_.1, f32[16,6,16,128]{3,2,1,0:T(8,128)} %bitcast.17, s32[16,16]{1,0:T(8,128)} %refs_4_.1, s32[16,16]{1,0:T(8,128)} %refs_5_.1, s32[16,16,128]{2,1,0:T(8,128)} %refs_6_.1), custom_call_target="tpu_custom_call" | custom-call | tf_op jit(solution)/shard_map/pallas_call | solution.py:470
  4.4 28.1 %all_to_all.10 = f32[1568,1,128]{2,1,0:T(1,128)S(1)} all-to-all(f32[1568,1,128]{2,1,0:T(1,128)S(1)} %bitcast.15), channel_id=1, replica_groups=mesh['scan'=8,'grp'=4] {'scan','grp'}, dimensions={0} | all-to-all | bytes 1605632 | tf_op jit(solution)/shard_map/all_to_all | solution.py:451
  32.4 2.7 %shard_map.69 = (f32[32,512]{1,0:T(8,128)S(1)}, f32[384,128]{1,0:T(8,128)}) custom-call(s32[1]{0:T(128)} %bitcast.refs_0_, f32[16,6,16,128]{3,2,1,0:T(8,128)S(1)} %get-tuple-element.12.refs_1_, f32[1568,128]{1,0:T(8,128)S(1)} %bitcast.14), custom_call_target="tpu_custom_call" | custom-call | tf_op jit(solution)/shard_map/pallas_call | solution.py:436
  35.2 3.6 %all-to-all-start.1 = ((f32[384,1,128]{2,1,0:T(1,128)}), f32[384,1,128]{2,1,0:T(1,128)S(1)}, u32[]{:S(2)}, u32[]{:S(2)}) async-start(f32[384,1,128]{2,1,0:T(1,128)} %bitcast.18), calls=%async_computation.1 | async-start | bytes 393216 | tf_op jit(solution)/shard_map/all_to_all | solution.py:451
  38.8 0.5 %shard_map.70 = (f32[96,128]{1,0:T(8,128)S(1)}, f32[96,128]{1,0:T(8,128)S(1)}, f32[96,128]{1,0:T(8,128)S(1)}, f32[96,128]{1,0:T(8,128)S(1)}) custom-call(s32[1]{0:T(128)} %bitcast.refs_0_, s32[1]{0:T(128)} %bitcast.1.refs_1_, f32[32,512]{1,0:T(8,128)S(1)} %get-tuple-element.15.refs_2_), custom_call_target="tpu_custom_call" | custom-call | tf_op jit(solution)/shard_map/pallas_call | solution.py:436
  39.3 0.3 collective-permute-start
  39.6 1.6 %collective-permute-start.1 = (f32[96,128]{1,0:T(8,128)S(1)}, f32[96,128]{1,0:T(8,128)S(1)}, u32[]{:S(2)}, u32[]{:S(2)}) collective-permute-start(f32[96,128]{1,0:T(8,128)S(1)} %get-tuple-element.18), channel_id=1, source_target_pairs={{0,2},{1,3},{2,0},{3,1},{4,6},{5,7},{6,4},{7,5},{8,10},{9,11},{10,... | collective-permute-start | bytes 147464 | tf_op jit(solution)/shard_map/ppermute | solution.py:508
  41.3 0.0 collective-permute-start.2
  41.3 0.0 collective-permute-done.refs_4_
  41.3 2.9 %collective-permute-done.1.refs_5_ = f32[96,128]{1,0:T(8,128)S(1)} collective-permute-done((f32[96,128]{1,0:T(8,128)S(1)}, f32[96,128]{1,0:T(8,128)S(1)}, u32[]{:S(2)}, u32[]{:S(2)}) %collective-permute-start.1) | collective-permute-done | bytes 49184 | tf_op jit(solution)/shard_map/ppermute | solution.py:508
  44.2 1.5 %collective-permute-done.2.refs_6_ = f32[96,128]{1,0:T(8,128)S(1)} collective-permute-done((f32[96,128]{1,0:T(8,128)S(1)}, f32[96,128]{1,0:T(8,128)S(1)}, u32[]{:S(2)}, u32[]{:S(2)}) %collective-permute-start.2) | collective-permute-done | bytes 49184 | tf_op jit(solution)/shard_map/ppermute | solution.py:508
  45.8 2.0 %all-to-all-done.1 = f32[384,1,128]{2,1,0:T(1,128)S(1)} async-done(((f32[384,1,128]{2,1,0:T(1,128)}), f32[384,1,128]{2,1,0:T(1,128)S(1)}, u32[]{:S(2)}, u32[]{:S(2)}) %all-to-all-start.1) | async-done | bytes 196640 | tf_op jit(solution)/shard_map/all_to_all | solution.py:451
  47.8 1.3 %shard_map.71 = (f32[36,16,32]{2,1,0:T(8,128)}, f32[4,6]{1,0:T(4,128)}) custom-call(s32[1]{0:T(128)} %bitcast.refs_0_, s32[1]{0:T(128)} %bitcast.1.refs_1_, f32[384,128]{1,0:T(8,128)S(1)} %bitcast.16, f32[96,128]{1,0:T(8,128)S(1)} %get-tuple-element.16.refs_3_, f32[96,128]{1,0:T(8,128)S(1)} %collective-permute-done.refs_4_, ...), custom_call_target="tpu_custom_call" | custom-call | tf_op jit(solution)/shard_map/pallas_call | solution.py:436
Async XLA Ops:
  35.2 12.6 %all-to-all-start.1 = ((f32[384,1,128]{2,1,0:T(1,128)}), f32[384,1,128]{2,1,0:T(1,128)S(1)}, u32[]{:S(2)}, u32[]{:S(2)}) async-start(f32[384,1,128]{2,1,0:T(1,128)} %bitcast.18), calls=%async_computation.1 | async-start | bytes 393216 | tf_op jit(solution)/shard_map/all_to_all | solution.py:451
  39.3 2.0 %collective-permute-start = (f32[96,128]{1,0:T(8,128)S(1)}, f32[96,128]{1,0:T(8,128)S(1)}, u32[]{:S(2)}, u32[]{:S(2)}) collective-permute-start(f32[96,128]{1,0:T(8,128)S(1)} %get-tuple-element.17), channel_id=1, source_target_pairs={{0,1},{1,0},{2,3},{3,2},{4,5},{5,4},{6,7},{7,6},{8,9},{9,8},{10,11... | collective-permute-start | bytes 147464 | tf_op jit(solution)/shard_map/ppermute | solution.py:508
  39.6 4.6 %collective-permute-start.1 = (f32[96,128]{1,0:T(8,128)S(1)}, f32[96,128]{1,0:T(8,128)S(1)}, u32[]{:S(2)}, u32[]{:S(2)}) collective-permute-start(f32[96,128]{1,0:T(8,128)S(1)} %get-tuple-element.18), channel_id=1, source_target_pairs={{0,2},{1,3},{2,0},{3,1},{4,6},{5,7},{6,4},{7,5},{8,10},{9,11},{10,... | collective-permute-start | bytes 147464 | tf_op jit(solution)/shard_map/ppermute | solution.py:508
  41.3 4.5 %collective-permute-start.2 = (f32[96,128]{1,0:T(8,128)S(1)}, f32[96,128]{1,0:T(8,128)S(1)}, u32[]{:S(2)}, u32[]{:S(2)}) collective-permute-start(f32[96,128]{1,0:T(8,128)S(1)} %get-tuple-element.19), channel_id=1, source_target_pairs={{0,3},{1,2},{2,1},{3,0},{4,7},{5,6},{6,5},{7,4},{8,11},{9,10},{10,... | collective-permute-start | bytes 147464 | tf_op jit(solution)/shard_map/ppermute | solution.py:508

commit v9 on v8

--- a/solution.py
+++ b/solution.py
@@ -60,8 +60,6 @@
 def send_kernel(
     devices,
     groups,
-    place_ref,
-    group_ref,
     count_hbm,
     samples_hbm,
     scan_hbm,
@@ -135,7 +133,7 @@
         load.wait()
 
     def one_scan(s, carry):
-        limit = count_ref[s] - group_ref[0] * group_points
+        limit = count_ref[s] - lax.axis_index("grp") * group_points
         for h in range(per_scan // 8):
             ids = src_ref[s, pl.ds(h * 8, 8), :]
             lane = mod(ids, LANES)
@@ -185,7 +183,7 @@
     return index ^ k if groups & (groups - 1) == 0 else (index + k) % groups
 
 
-def pair_kernel(devices, groups, place_ref, samples_ref, recv_ref, flat_ref, back_hbm, back_ref, point_ref, mate_ref, note_ref, sems):
+def pair_kernel(devices, groups, samples_ref, recv_ref, flat_ref, back_hbm, back_ref, point_ref, mate_ref, note_ref, sems):
     scan_local, _, tiles, _ = samples_ref.shape
     slots = flat_ref.shape[1]
     cap = slots // devices
@@ -218,7 +216,7 @@
             ]
             point_ref[a, :, c * LANES : (c + 1) * LANES] = jnp.concatenate(stack, axis=0).T
     span, slot_rows, sum_rows, grad_row, grad_lane, rows = back_layout(scan_local, groups, cap)
-    near_group = div(place_ref[0] * scan_local, scans * scan_local // groups)
+    near_group = div(lax.axis_index("scan") * scan_local, scans * scan_local // groups)
     share = scan_local // groups
     slot_lane = div(iota((slot_rows, LANES), 1), span)
     sum_lane = div(iota((sum_rows, LANES), 1), scan_local)
@@ -307,7 +305,7 @@
         )
 
 
-def held_kernel(devices, groups, scan_local, scan_ref, group_ref, flat_ref, *refs):
+def held_kernel(devices, groups, scan_local, flat_ref, *refs):
     out_refs, stage_ref = refs[:-1], refs[-1]
     slots = flat_ref.shape[1]
     cap = slots // devices
@@ -316,7 +314,7 @@
     every = flat_ref[...]
     row = every[ROW_MATE : ROW_MATE + 1].astype(jnp.int32)
     other = div(div(iota((1, slots), 1), cap), groups) * scan_local + every[ROW_FLAG : ROW_FLAG + 1].astype(jnp.int32) - 1
-    own = scan_ref[0] * scan_local + row
+    own = lax.axis_index("scan") * scan_local + row
     row_hot = iota((scan_local, slots), 0) == row
     column = iota((scan_total, slots), 0)
     mix = ((column == own).astype(jnp.float32) - (column == other).astype(jnp.float32)).astype(jnp.bfloat16)
@@ -343,16 +341,16 @@
                 tile = jnp.where(div(lane, columns) == k, value, tile) if pack > 1 else value
             stage_ref[c, r * scan_local : (r + 1) * scan_local, :] = tile
     for k, out_ref in enumerate(out_refs):
-        out_ref[...] = stage_ref[partner(group_ref[0], k, groups)]
-
-
-def close_kernel(devices, groups, cap, scan_ref, group_ref, back_ref, *refs):
+        out_ref[...] = stage_ref[partner(lax.axis_index("grp"), k, groups)]
+
+
+def close_kernel(devices, groups, cap, back_ref, *refs):
     part_refs, (hess_ref, grad_ref, every_ref, hold_ref) = refs[:groups], refs[groups:]
     scan_local, columns = hess_ref.shape[1:]
     per_block = part_refs[0].shape[0] // scan_local
     span, slot_rows, sum_rows, grad_row, grad_lane, block = back_layout(scan_local, groups, cap)
     senders = devices // groups
-    first = group_ref[0] * (senders * block)
+    first = lax.axis_index("grp") * (senders * block)
     lane_block = div(iota((slot_rows, LANES), 1), span)
     per_chunk = LANES // span
     for chunk in range(senders // per_chunk):
@@ -369,7 +367,7 @@
     mate = every[ROW_MATE : ROW_MATE + 1].astype(jnp.int32)
     column = div(div(iota((1, total), 1), span), groups) * scan_local + mate
     row_hot = iota((scan_local, total), 0) == row
-    offset = scan_ref[0] * scan_local - group_ref[0] * columns
+    offset = lax.axis_index("scan") * scan_local - lax.axis_index("grp") * columns
     line = iota((columns, total), 0)
     mix = (line == row + offset).astype(jnp.float32) - (line == column).astype(jnp.float32)
     mix = mix.astype(jnp.bfloat16)
@@ -380,7 +378,7 @@
         part = back_ref[c * senders * block : c * senders * block + sum_rows, :]
         for d in range(c * senders + 1, (c + 1) * senders):
             part = part + back_ref[d * block : d * block + sum_rows, :]
-        sums = sums + jnp.where(group_ref[0] != c, part, 0.0)
+        sums = sums + jnp.where(lax.axis_index("grp") != c, part, 0.0)
     near = back_ref[pl.ds(first + grad_row, 1), :]
     for u in range(1, senders):
         near = near + back_ref[pl.ds(first + u * block + grad_row, 1), :]
@@ -418,7 +416,7 @@
         spot = grad_lane + q * part + iota((part, LANES), 0) == iota((part, LANES), 1)
         value = jnp.sum(jnp.where(spot, near, 0.0), axis=1, keepdims=True)
         own = jnp.where(iota((part, LANES), 1) == q, value, own)
-    hold = hold_ref[pl.ds(group_ref[0] * part, part), :] + own
+    hold = hold_ref[pl.ds(lax.axis_index("grp") * part, part), :] + own
     grad_ref[...] = hold[:, 0:FIELDS]
 
 
@@ -460,8 +458,6 @@
     slots = devices * cap
     scan_total = scan_local * (devices // groups)
     columns, pack, per_block = layout(scan_local, groups, scan_total)
-    group = lax.axis_index("grp").astype(jnp.int32).reshape(1)
-    scan = lax.axis_index("scan").astype(jnp.int32).reshape(1)
     back_rows = back_layout(scan_local, groups, cap)[-1]
 
     def bind(kernel, *args):
@@ -470,7 +466,7 @@
     sent, samples = pl.pallas_call(
         bind(send_kernel, devices, groups),
         out_shape=(near(devices * block, LANES), near(*samples.shape)),
-        in_specs=[pl.BlockSpec(memory_space=pltpu.SMEM)] * 2 + [pl.BlockSpec(memory_space=pl.ANY)] * 5,
+        in_specs=[pl.BlockSpec(memory_space=pl.ANY)] * 5,
         scratch_shapes=[
             pltpu.SMEM(point_count.shape, jnp.int32),
             pltpu.VMEM(corr_scan.shape, jnp.int32),
@@ -479,12 +475,12 @@
             pltpu.VMEM((COORDS, entries, LANES), jnp.float32),
             pltpu.SemaphoreType.DMA((5,)),
         ],
-    )(scan, group, point_count, samples, corr_scan, corr_tile, corr_src)
+    )(point_count, samples, corr_scan, corr_tile, corr_src)
     received = exchange(sent, AXES)
     flat, back = call(
         bind(pair_kernel, devices, groups),
         (near(WIDTH, slots), f32(devices * back_rows, LANES)),
-        1,
+        0,
         2,
         [
             pltpu.VMEM((devices * back_rows, LANES), jnp.float32),
@@ -494,29 +490,29 @@
             pltpu.SemaphoreType.DMA((slots // LANES,)),
         ],
         (pl.BlockSpec(memory_space=pltpu.VMEM), pl.BlockSpec(memory_space=pl.ANY)),
-    )(scan, samples, received)
+    )(samples, received)
     back = exchange(back, AXES)
     share = near(per_block * scan_local, LANES)
     shares = call(
         bind(held_kernel, devices, groups, scan_local),
         (share,) * groups,
-        2,
+        0,
         1,
         [pltpu.VMEM((groups,) + share.shape, jnp.float32)],
-    )(scan, group, flat)
+    )(flat)
     shares = [shares[0]] + [
         lax.ppermute(shares[k], "grp", [(g, partner(g, k, groups)) for g in range(groups)]) for k in range(1, groups)
     ]
     hess, grad = call(
         bind(close_kernel, devices, groups, cap),
         (f32(FIELDS * FIELDS, scan_local, columns), f32(scan_local // groups, FIELDS)),
-        2,
+        0,
         1 + groups,
         [
             pltpu.VMEM((HEAD, (devices // groups) * groups * cap), jnp.float32),
             pltpu.VMEM((scan_local, LANES), jnp.float32),
         ],
-    )(scan, group, back, *shares)
+    )(back, *shares)
     return hess.reshape(FIELDS, FIELDS, scan_local, columns).transpose(2, 0, 1, 3), grad
 
 

time: 49.3 us -> 49.3 us (level)
  no operation moved by 1% of the time
where the time goes in v9:
time: 49.3 us; the launch traced here: 49 us
  blocking collectives  28.1 us (57%)
  Pallas kernels  8.22 us (17%)
  waiting for transfers between devices  6.48 us (13%)
  starting transfers between devices  5.59 us (11%)
  between operations  0.67 us (1%)
    all_to_all x1, blocking collectives, exchange(): lax.all_to_all(x.reshape(count, 1, width), axes, split_axis=0, concat_axi...  28.1 us
    pallas_call x3, Pallas kernels, run(): return body(*args)  4.49 us
    ppermute x3, waiting for transfers between devices, local(): lax.ppermute(shares[k], 'grp', [(g, partner(g, k, groups)) for g in range...  4.48 us
    pallas_call x1, Pallas kernels, local(): pl.pallas_call(bind(send_kernel, devices, groups), out_shape=(near(device...  3.73 us
    all_to_all x1, starting transfers between devices, exchange(): lax.all_to_all(x.reshape(count, 1, width), axes, split_axis=0, concat_axi...  3.62 us
    all_to_all x1, waiting for transfers between devices, exchange(): lax.all_to_all(x.reshape(count, 1, width), axes, split_axis=0, concat_axi...  2 us
    ppermute x3, starting transfers between devices, local(): lax.ppermute(shares[k], 'grp', [(g, partner(g, k, groups)) for g in range...  1.97 us
  transfers between devices with their start and end apart: 4, of which 3 were waited for; matrix products, arithmetic and copies ran while one was open for 0% of the time, Pallas kernels for 1%

profile of v9, /device:TPU:0, one launch (start us, length us, event | category | flops | bytes accessed | tf_op | source)
XLA Modules:
  0.0 49.0 jit_solution(7556664672920383411)
XLA Ops:
  0.6 3.7 %shard_map.68 = (f32[1568,128]{1,0:T(8,128)S(1)}, f32[16,6,16,128]{3,2,1,0:T(8,128)S(1)}) custom-call(s32[16]{0:T(128)} %refs_0_.1, f32[16,6,16,128]{3,2,1,0:T(8,128)} %bitcast.15, s32[16,16]{1,0:T(8,128)} %refs_2_.1, s32[16,16]{1,0:T(8,128)} %refs_3_.1, s32[16,16,128]{2,1,0:T(8,128)} %refs_4_.1), custom_call_target="tpu_custom_call" | custom-call | tf_op jit(solution)/shard_map/pallas_call | solution.py:466
  4.4 28.1 %all_to_all.10 = f32[1568,1,128]{2,1,0:T(1,128)S(1)} all-to-all(f32[1568,1,128]{2,1,0:T(1,128)S(1)} %bitcast.13), channel_id=1, replica_groups=mesh['scan'=8,'grp'=4] {'scan','grp'}, dimensions={0} | all-to-all | bytes 1605632 | tf_op jit(solution)/shard_map/all_to_all | solution.py:449
  32.4 2.7 %shard_map.69 = (f32[32,512]{1,0:T(8,128)S(1)}, f32[384,128]{1,0:T(8,128)}) custom-call(f32[16,6,16,128]{3,2,1,0:T(8,128)S(1)} %get-tuple-element.12.refs_0_, f32[1568,128]{1,0:T(8,128)S(1)} %bitcast.12), custom_call_target="tpu_custom_call" | custom-call | tf_op jit(solution)/shard_map/pallas_call | solution.py:434
  35.2 3.6 %all-to-all-start.1 = ((f32[384,1,128]{2,1,0:T(1,128)}), f32[384,1,128]{2,1,0:T(1,128)S(1)}, u32[]{:S(2)}, u32[]{:S(2)}) async-start(f32[384,1,128]{2,1,0:T(1,128)} %bitcast.16), calls=%async_computation.1 | async-start | bytes 393216 | tf_op jit(solution)/shard_map/all_to_all | solution.py:449
  38.8 0.5 %shard_map.70 = (f32[96,128]{1,0:T(8,128)S(1)}, f32[96,128]{1,0:T(8,128)S(1)}, f32[96,128]{1,0:T(8,128)S(1)}, f32[96,128]{1,0:T(8,128)S(1)}) custom-call(f32[32,512]{1,0:T(8,128)S(1)} %get-tuple-element.15.refs_0_), custom_call_target="tpu_custom_call" | custom-call | tf_op jit(solution)/shard_map/pallas_call | solution.py:434
  39.3 0.3 collective-permute-start
  39.6 1.6 %collective-permute-start.1 = (f32[96,128]{1,0:T(8,128)S(1)}, f32[96,128]{1,0:T(8,128)S(1)}, u32[]{:S(2)}, u32[]{:S(2)}) collective-permute-start(f32[96,128]{1,0:T(8,128)S(1)} %get-tuple-element.18), channel_id=1, source_target_pairs={{0,2},{1,3},{2,0},{3,1},{4,6},{5,7},{6,4},{7,5},{8,10},{9,11},{10,... | collective-permute-start | bytes 147464 | tf_op jit(solution)/shard_map/ppermute | solution.py:504
  41.3 0.0 collective-permute-start.2
  41.3 0.0 collective-permute-done.refs_2_
  41.3 2.9 %collective-permute-done.1.refs_3_ = f32[96,128]{1,0:T(8,128)S(1)} collective-permute-done((f32[96,128]{1,0:T(8,128)S(1)}, f32[96,128]{1,0:T(8,128)S(1)}, u32[]{:S(2)}, u32[]{:S(2)}) %collective-permute-start.1) | collective-permute-done | bytes 49184 | tf_op jit(solution)/shard_map/ppermute | solution.py:504
  44.2 1.5 %collective-permute-done.2.refs_4_ = f32[96,128]{1,0:T(8,128)S(1)} collective-permute-done((f32[96,128]{1,0:T(8,128)S(1)}, f32[96,128]{1,0:T(8,128)S(1)}, u32[]{:S(2)}, u32[]{:S(2)}) %collective-permute-start.2) | collective-permute-done | bytes 49184 | tf_op jit(solution)/shard_map/ppermute | solution.py:504
  45.8 2.0 %all-to-all-done.1 = f32[384,1,128]{2,1,0:T(1,128)S(1)} async-done(((f32[384,1,128]{2,1,0:T(1,128)}), f32[384,1,128]{2,1,0:T(1,128)S(1)}, u32[]{:S(2)}, u32[]{:S(2)}) %all-to-all-start.1) | async-done | bytes 196640 | tf_op jit(solution)/shard_map/all_to_all | solution.py:449
  47.8 1.3 %shard_map.71 = (f32[36,16,32]{2,1,0:T(8,128)}, f32[4,6]{1,0:T(4,128)}) custom-call(f32[384,128]{1,0:T(8,128)S(1)} %bitcast.14, f32[96,128]{1,0:T(8,128)S(1)} %get-tuple-element.16.refs_1_, f32[96,128]{1,0:T(8,128)S(1)} %collective-permute-done.refs_2_, f32[96,128]{1,0:T(8,128)S(1)} %collective-permute-done.1.refs_3_, ...), custom_call_target="tpu_custom_call" | custom-call | tf_op jit(solution)/shard_map/pallas_call | solution.py:434
Async XLA Ops:
  35.2 12.6 %all-to-all-start.1 = ((f32[384,1,128]{2,1,0:T(1,128)}), f32[384,1,128]{2,1,0:T(1,128)S(1)}, u32[]{:S(2)}, u32[]{:S(2)}) async-start(f32[384,1,128]{2,1,0:T(1,128)} %bitcast.16), calls=%async_computation.1 | async-start | bytes 393216 | tf_op jit(solution)/shard_map/all_to_all | solution.py:449
  39.3 2.0 %collective-permute-start = (f32[96,128]{1,0:T(8,128)S(1)}, f32[96,128]{1,0:T(8,128)S(1)}, u32[]{:S(2)}, u32[]{:S(2)}) collective-permute-start(f32[96,128]{1,0:T(8,128)S(1)} %get-tuple-element.17), channel_id=1, source_target_pairs={{0,1},{1,0},{2,3},{3,2},{4,5},{5,4},{6,7},{7,6},{8,9},{9,8},{10,11... | collective-permute-start | bytes 147464 | tf_op jit(solution)/shard_map/ppermute | solution.py:504
  39.6 4.6 %collective-permute-start.1 = (f32[96,128]{1,0:T(8,128)S(1)}, f32[96,128]{1,0:T(8,128)S(1)}, u32[]{:S(2)}, u32[]{:S(2)}) collective-permute-start(f32[96,128]{1,0:T(8,128)S(1)} %get-tuple-element.18), channel_id=1, source_target_pairs={{0,2},{1,3},{2,0},{3,1},{4,6},{5,7},{6,4},{7,5},{8,10},{9,11},{10,... | collective-permute-start | bytes 147464 | tf_op jit(solution)/shard_map/ppermute | solution.py:504
  41.3 4.5 %collective-permute-start.2 = (f32[96,128]{1,0:T(8,128)S(1)}, f32[96,128]{1,0:T(8,128)S(1)}, u32[]{:S(2)}, u32[]{:S(2)}) collective-permute-start(f32[96,128]{1,0:T(8,128)S(1)} %get-tuple-element.19), channel_id=1, source_target_pairs={{0,3},{1,2},{2,1},{3,0},{4,7},{5,6},{6,5},{7,4},{8,11},{9,10},{10,... | collective-permute-start | bytes 147464 | tf_op jit(solution)/shard_map/ppermute | solution.py:504

commit v10 on v9

--- a/solution.py
+++ b/solution.py
@@ -14,7 +14,7 @@
 ROW_MATE = MAT + 1
 HEAD = MAT + 3
 WIDTH = 32
-FAR = 2.0**100
+SENT = COORDS + 1
 BOTH_LANES = (((1,), (1,)), ((), ()))
 AXES = ("scan", "grp")
 
@@ -54,7 +54,7 @@
     per_scan = entries_shape[1]
     entries = scan_local * per_scan
     cap = 2 * entries // devices
-    return scan_local, tiles, per_scan, entries, cap, COORDS * cap + 1
+    return scan_local, tiles, per_scan, entries, cap, SENT * cap + 1
 
 
 def send_kernel(
@@ -127,7 +127,7 @@
     towards = (iota((devices, entries), 0).astype(jnp.float32) == device_row).astype(jnp.float32).astype(jnp.bfloat16)
     notes = dot(towards, picked, BOTH_LANES)
     for d in range(devices):
-        out_ref[pl.ds(d * block + COORDS * cap, 1), :] = notes[d : d + 1]
+        out_ref[pl.ds(d * block + SENT * cap, 1), :] = notes[d : d + 1]
 
     for load in loads[2:]:
         load.wait()
@@ -144,9 +144,9 @@
                 for a in range(COORDS):
                     row = jnp.broadcast_to(samples_ref[s, a, t : t + 1, :], (8, LANES))
                     found[a] = jnp.where(here, jnp.take_along_axis(row, lane, axis=1), found[a])
-            found[0] = jnp.where(ids < limit, found[0], FAR)
+            found.append((ids < limit).astype(jnp.float32))
             at = pl.multiple_of(s * per_scan + h * 8, 8)
-            for a in range(COORDS):
+            for a in range(SENT):
                 data_ref[a, pl.ds(at, 8), :] = found[a]
         present = iota((tiles, LANES), 0) * LANES + iota((tiles, LANES), 1) < limit
         for a in range(COORDS, FIELDS):
@@ -155,9 +155,9 @@
 
     lax.fori_loop(0, scan_local, one_scan, 0, unroll=8)
 
-    thirds = [jnp.concatenate(part, axis=1) for part in zip(*[pieces(data_ref[a], 3) for a in range(COORDS)])]
+    thirds = [jnp.concatenate(part, axis=1) for part in zip(*[pieces(data_ref[a], 3) for a in range(SENT)])]
     moved = dot(jnp.concatenate([place] * 3, axis=1), jnp.concatenate(thirds, axis=0))
-    for a in range(COORDS):
+    for a in range(SENT):
         for d in range(devices):
             out_ref[pl.ds(d * block + a * cap, cap), :] = moved[d * cap : (d + 1) * cap, a * LANES : (a + 1) * LANES]
 
@@ -187,10 +187,10 @@
     scan_local, _, tiles, _ = samples_ref.shape
     slots = flat_ref.shape[1]
     cap = slots // devices
-    block = COORDS * cap + 1
+    block = SENT * cap + 1
     scans = devices // groups
     for d in range(devices):
-        note_ref[pl.ds(d, 1), :] = recv_ref[pl.ds(d * block + COORDS * cap, 1), :]
+        note_ref[pl.ds(d, 1), :] = recv_ref[pl.ds(d * block + SENT * cap, 1), :]
     notes = note_ref[...].astype(jnp.bfloat16)
     mine = div(iota((devices, slots), 1), cap) == iota((devices, slots), 0)
     rows = []
@@ -210,7 +210,7 @@
         mate_ref[a] = (parts[0] + parts[1]) + parts[2]
     per_chunk = LANES // cap
     for c in range(slots // LANES):
-        for a in range(COORDS):
+        for a in range(SENT):
             stack = [
                 recv_ref[pl.ds(d * block + a * cap, cap), :] for d in range(c * per_chunk, (c + 1) * per_chunk)
             ]
@@ -229,12 +229,10 @@
 
         def step(k, sums):
             at = pl.ds(pl.multiple_of(k * 8, 8), 8)
-            px, py, pz = [point_ref[a, at, lanes] for a in range(COORDS)]
-            present = px < FAR
-            px = jnp.where(present, px, 0.0)
+            px, py, pz, mask = [point_ref[a, at, lanes] for a in range(SENT)]
             qx, qy, qz, nx, ny, nz = [mate_ref[a, at, lanes] for a in range(FIELDS)]
             residual = nx * (px - qx) + ny * (py - qy) + nz * (pz - qz)
-            weight = jnp.where(present, 1.0 / (1.0 + residual * residual), 0.0)
+            weight = mask / (1.0 + residual * residual)
             jac = [py * nz - pz * ny, pz * nx - px * nz, px * ny - py * nx, nx, ny, nz]
             scaled = [weight * j for j in jac]
             terms = [scaled[i] * jac[j] for i, j in PAIRS] + [residual * s for s in scaled]
@@ -242,8 +240,7 @@
 
         zero = jnp.zeros((8, LANES), jnp.float32)
         sums = lax.fori_loop(0, LANES // 8, step, (zero,) * (MAT + FIELDS), unroll=16)
-        filled = flag_row[:, lanes] > 0.0
-        lines = [jnp.where(filled, jnp.sum(s, axis=0, keepdims=True), 0.0) for s in sums]
+        lines = [jnp.sum(s, axis=0, keepdims=True) for s in sums]
         blank = jnp.zeros((1, LANES), jnp.float32)
         lines[MAT:MAT] = [flag_row[:, lanes], mate_row[:, lanes], blank]
         lines += [blank] * (WIDTH - len(lines))
@@ -472,7 +469,7 @@
             pltpu.VMEM(corr_scan.shape, jnp.int32),
             pltpu.VMEM(corr_tile.shape, jnp.int32),
             pltpu.VMEM(corr_src.shape, jnp.int32),
-            pltpu.VMEM((COORDS, entries, LANES), jnp.float32),
+            pltpu.VMEM((SENT, entries, LANES), jnp.float32),
             pltpu.SemaphoreType.DMA((5,)),
         ],
     )(point_count, samples, corr_scan, corr_tile, corr_src)
@@ -484,7 +481,7 @@
         2,
         [
             pltpu.VMEM((devices * back_rows, LANES), jnp.float32),
-            pltpu.VMEM((COORDS, LANES, slots), jnp.float32),
+            pltpu.VMEM((SENT, LANES, slots), jnp.float32),
             pltpu.VMEM((FIELDS, LANES, slots), jnp.float32),
             pltpu.VMEM((devices, LANES), jnp.float32),
             pltpu.SemaphoreType.DMA((slots // LANES,)),

time: 49.3 us -> 55.7 us (1.13)
  blocking collectives: 28.1 us -> 35.5 us
  starting transfers between devices: 5.59 us -> 4.52 us
    all_to_all x1, blocking collectives: 28.1 us -> 35.5 us  [exchange(): lax.all_to_all(x.reshape(count, 1, width), axes, split_axis=0, concat_axi...]
    all_to_all x1, starting transfers between devices: 3.62 us -> 2.6 us  [exchange(): lax.all_to_all(x.reshape(count, 1, width), axes, split_axis=0, concat_axi...]
where the time goes in v10:
time: 55.7 us; the launch traced here: 55.4 us
  blocking collectives  35.5 us (64%)
  Pallas kernels  8.23 us (15%)
  waiting for transfers between devices  6.52 us (12%)
  starting transfers between devices  4.52 us (8%)
  between operations  0.67 us (1%)
    all_to_all x1, blocking collectives, exchange(): lax.all_to_all(x.reshape(count, 1, width), axes, split_axis=0, concat_axi...  35.5 us
    pallas_call x3, Pallas kernels, run(): return body(*args)  4.48 us
    ppermute x3, waiting for transfers between devices, local(): lax.ppermute(shares[k], 'grp', [(g, partner(g, k, groups)) for g in range...  4.42 us
    pallas_call x1, Pallas kernels, local(): pl.pallas_call(bind(send_kernel, devices, groups), out_shape=(near(device...  3.75 us
    all_to_all x1, starting transfers between devices, exchange(): lax.all_to_all(x.reshape(count, 1, width), axes, split_axis=0, concat_axi...  2.6 us
    all_to_all x1, waiting for transfers between devices, exchange(): lax.all_to_all(x.reshape(count, 1, width), axes, split_axis=0, concat_axi...  2.1 us
    ppermute x3, starting transfers between devices, local(): lax.ppermute(shares[k], 'grp', [(g, partner(g, k, groups)) for g in range...  1.93 us
  transfers between devices with their start and end apart: 4, of which 3 were waited for; matrix products, arithmetic and copies ran while one was open for 0% of the time, Pallas kernels for 1%

profile of v10, /device:TPU:0, one launch (start us, length us, event | category | flops | bytes accessed | tf_op | source)
XLA Modules:
  0.0 55.4 jit_solution(2233033950638792822)
XLA Ops:
  0.6 3.7 %shard_map.68 = (f32[2080,128]{1,0:T(8,128)S(1)}, f32[16,6,16,128]{3,2,1,0:T(8,128)S(1)}) custom-call(s32[16]{0:T(128)} %refs_0_.1, f32[16,6,16,128]{3,2,1,0:T(8,128)} %bitcast.15, s32[16,16]{1,0:T(8,128)} %refs_2_.1, s32[16,16]{1,0:T(8,128)} %refs_3_.1, s32[16,16,128]{2,1,0:T(8,128)} %refs_4_.1), custom_call_target="tpu_custom_call" | custom-call | tf_op jit(solution)/shard_map/pallas_call | solution.py:463
  4.4 35.5 %all_to_all.10 = f32[2080,1,128]{2,1,0:T(1,128)S(1)} all-to-all(f32[2080,1,128]{2,1,0:T(1,128)S(1)} %bitcast.13), channel_id=1, replica_groups=mesh['scan'=8,'grp'=4] {'scan','grp'}, dimensions={0} | all-to-all | bytes 2129920 | tf_op jit(solution)/shard_map/all_to_all | solution.py:446
  39.9 2.7 %shard_map.69 = (f32[32,512]{1,0:T(8,128)S(1)}, f32[384,128]{1,0:T(8,128)}) custom-call(f32[16,6,16,128]{3,2,1,0:T(8,128)S(1)} %get-tuple-element.12.refs_0_, f32[2080,128]{1,0:T(8,128)S(1)} %bitcast.12), custom_call_target="tpu_custom_call" | custom-call | tf_op jit(solution)/shard_map/pallas_call | solution.py:431
  42.6 2.6 %all-to-all-start.1 = ((f32[384,1,128]{2,1,0:T(1,128)}), f32[384,1,128]{2,1,0:T(1,128)S(1)}, u32[]{:S(2)}, u32[]{:S(2)}) async-start(f32[384,1,128]{2,1,0:T(1,128)} %bitcast.16), calls=%async_computation.1 | async-start | bytes 393216 | tf_op jit(solution)/shard_map/all_to_all | solution.py:446
  45.2 0.5 shard_map.70
  45.7 0.2 collective-permute-start
  45.9 1.7 %collective-permute-start.1 = (f32[96,128]{1,0:T(8,128)S(1)}, f32[96,128]{1,0:T(8,128)S(1)}, u32[]{:S(2)}, u32[]{:S(2)}) collective-permute-start(f32[96,128]{1,0:T(8,128)S(1)} %get-tuple-element.18), channel_id=1, source_target_pairs={{0,2},{1,3},{2,0},{3,1},{4,6},{5,7},{6,4},{7,5},{8,10},{9,11},{10,... | collective-permute-start | bytes 147464 | tf_op jit(solution)/shard_map/ppermute | solution.py:501
  47.6 0.1 collective-permute-start.2
  47.7 0.0 collective-permute-done.refs_2_
  47.7 3.0 %collective-permute-done.1.refs_3_ = f32[96,128]{1,0:T(8,128)S(1)} collective-permute-done((f32[96,128]{1,0:T(8,128)S(1)}, f32[96,128]{1,0:T(8,128)S(1)}, u32[]{:S(2)}, u32[]{:S(2)}) %collective-permute-start.1) | collective-permute-done | bytes 49184 | tf_op jit(solution)/shard_map/ppermute | solution.py:501
  50.7 1.4 %collective-permute-done.2.refs_4_ = f32[96,128]{1,0:T(8,128)S(1)} collective-permute-done((f32[96,128]{1,0:T(8,128)S(1)}, f32[96,128]{1,0:T(8,128)S(1)}, u32[]{:S(2)}, u32[]{:S(2)}) %collective-permute-start.2) | collective-permute-done | bytes 49184 | tf_op jit(solution)/shard_map/ppermute | solution.py:501
  52.1 2.1 %all-to-all-done.1 = f32[384,1,128]{2,1,0:T(1,128)S(1)} async-done(((f32[384,1,128]{2,1,0:T(1,128)}), f32[384,1,128]{2,1,0:T(1,128)S(1)}, u32[]{:S(2)}, u32[]{:S(2)}) %all-to-all-start.1) | async-done | bytes 196640 | tf_op jit(solution)/shard_map/all_to_all | solution.py:446
  54.2 1.3 %shard_map.71 = (f32[36,16,32]{2,1,0:T(8,128)}, f32[4,6]{1,0:T(4,128)}) custom-call(f32[384,128]{1,0:T(8,128)S(1)} %bitcast.14, f32[96,128]{1,0:T(8,128)S(1)} %get-tuple-element.16.refs_1_, f32[96,128]{1,0:T(8,128)S(1)} %collective-permute-done.refs_2_, f32[96,128]{1,0:T(8,128)S(1)} %collective-permute-done.1.refs_3_, ...), custom_call_target="tpu_custom_call" | custom-call | tf_op jit(solution)/shard_map/pallas_call | solution.py:431
Async XLA Ops:
  42.6 11.6 %all-to-all-start.1 = ((f32[384,1,128]{2,1,0:T(1,128)}), f32[384,1,128]{2,1,0:T(1,128)S(1)}, u32[]{:S(2)}, u32[]{:S(2)}) async-start(f32[384,1,128]{2,1,0:T(1,128)} %bitcast.16), calls=%async_computation.1 | async-start | bytes 393216 | tf_op jit(solution)/shard_map/all_to_all | solution.py:446
  45.7 1.9 %collective-permute-start = (f32[96,128]{1,0:T(8,128)S(1)}, f32[96,128]{1,0:T(8,128)S(1)}, u32[]{:S(2)}, u32[]{:S(2)}) collective-permute-start(f32[96,128]{1,0:T(8,128)S(1)} %get-tuple-element.17), channel_id=1, source_target_pairs={{0,1},{1,0},{2,3},{3,2},{4,5},{5,4},{6,7},{7,6},{8,9},{9,8},{10,11... | collective-permute-start | bytes 147464 | tf_op jit(solution)/shard_map/ppermute | solution.py:501
  45.9 4.8 %collective-permute-start.1 = (f32[96,128]{1,0:T(8,128)S(1)}, f32[96,128]{1,0:T(8,128)S(1)}, u32[]{:S(2)}, u32[]{:S(2)}) collective-permute-start(f32[96,128]{1,0:T(8,128)S(1)} %get-tuple-element.18), channel_id=1, source_target_pairs={{0,2},{1,3},{2,0},{3,1},{4,6},{5,7},{6,4},{7,5},{8,10},{9,11},{10,... | collective-permute-start | bytes 147464 | tf_op jit(solution)/shard_map/ppermute | solution.py:501
  47.6 4.5 %collective-permute-start.2 = (f32[96,128]{1,0:T(8,128)S(1)}, f32[96,128]{1,0:T(8,128)S(1)}, u32[]{:S(2)}, u32[]{:S(2)}) collective-permute-start(f32[96,128]{1,0:T(8,128)S(1)} %get-tuple-element.19), channel_id=1, source_target_pairs={{0,3},{1,2},{2,1},{3,0},{4,7},{5,6},{6,5},{7,4},{8,11},{9,10},{10,... | collective-permute-start | bytes 147464 | tf_op jit(solution)/shard_map/ppermute | solution.py:501

commit v11 on v10

--- a/solution.py
+++ b/solution.py
@@ -67,6 +67,7 @@
     src_hbm,
     out_ref,
     samples_ref,
+    limit_ref,
     count_ref,
     scan_ref,
     tile_ref,
@@ -81,7 +82,8 @@
         (tile_hbm, tile_ref),
         (count_hbm, count_ref),
         (src_hbm, src_ref),
-        (samples_hbm, samples_ref),
+        (samples_hbm.at[:, 0:COORDS], samples_ref.at[:, 0:COORDS]),
+        (samples_hbm.at[:, COORDS:FIELDS], samples_ref.at[:, COORDS:FIELDS]),
     )
     loads = [pltpu.make_async_copy(far, here, sems.at[k]) for k, (far, here) in enumerate(pairs)]
     for load in loads:
@@ -129,7 +131,7 @@
     for d in range(devices):
         out_ref[pl.ds(d * block + SENT * cap, 1), :] = notes[d : d + 1]
 
-    for load in loads[2:]:
+    for load in loads[2:-1]:
         load.wait()
 
     def one_scan(s, carry):
@@ -148,9 +150,7 @@
             at = pl.multiple_of(s * per_scan + h * 8, 8)
             for a in range(SENT):
                 data_ref[a, pl.ds(at, 8), :] = found[a]
-        present = iota((tiles, LANES), 0) * LANES + iota((tiles, LANES), 1) < limit
-        for a in range(COORDS, FIELDS):
-            samples_ref[s, a] = jnp.where(present, samples_ref[s, a], 0.0)
+        limit_ref[pl.ds(s, 1), :] = jnp.full((1, LANES), limit, jnp.int32)
         return carry
 
     lax.fori_loop(0, scan_local, one_scan, 0, unroll=8)
@@ -160,6 +160,7 @@
     for a in range(SENT):
         for d in range(devices):
             out_ref[pl.ds(d * block + a * cap, cap), :] = moved[d * cap : (d + 1) * cap, a * LANES : (a + 1) * LANES]
+    loads[-1].wait()
 
 
 def turn(x, amount):
@@ -183,7 +184,7 @@
     return index ^ k if groups & (groups - 1) == 0 else (index + k) % groups
 
 
-def pair_kernel(devices, groups, samples_ref, recv_ref, flat_ref, back_hbm, back_ref, point_ref, mate_ref, note_ref, sems):
+def pair_kernel(devices, groups, limit_ref, samples_ref, recv_ref, flat_ref, back_hbm, back_ref, point_ref, mate_ref, note_ref, sems):
     scan_local, _, tiles, _ = samples_ref.shape
     slots = flat_ref.shape[1]
     cap = slots // devices
@@ -203,8 +204,12 @@
     code_row = (mate_row * tiles + tile_row).astype(jnp.int32)
     table = scan_local * tiles
     chosen = (iota((table, slots), 0) == code_row).astype(jnp.float32).astype(jnp.bfloat16)
+    spot = iota((tiles, LANES), 0) * LANES + iota((tiles, LANES), 1)
     for a in range(FIELDS):
-        values = jnp.concatenate([samples_ref[b, a] for b in range(scan_local)], axis=0)
+        values = [samples_ref[b, a] for b in range(scan_local)]
+        if a >= COORDS:
+            values = [jnp.where(spot < limit_ref[b : b + 1, :], value, 0.0) for b, value in enumerate(values)]
+        values = jnp.concatenate(values, axis=0)
         turned = jnp.concatenate([values[h : h + LANES].T for h in range(0, table, LANES)], axis=1)
         parts = [dot(part, chosen) for part in pieces(turned, 3)]
         mate_ref[a] = (parts[0] + parts[1]) + parts[2]
@@ -460,9 +465,13 @@
     def bind(kernel, *args):
         return lambda *refs: kernel(*args, *refs)
 
-    sent, samples = pl.pallas_call(
+    sent, samples, limits = pl.pallas_call(
         bind(send_kernel, devices, groups),
-        out_shape=(near(devices * block, LANES), near(*samples.shape)),
+        out_shape=(
+            near(devices * block, LANES),
+            near(*samples.shape),
+            pltpu.VMEM((scan_local, LANES), jnp.int32),
+        ),
         in_specs=[pl.BlockSpec(memory_space=pl.ANY)] * 5,
         scratch_shapes=[
             pltpu.SMEM(point_count.shape, jnp.int32),
@@ -470,7 +479,7 @@
             pltpu.VMEM(corr_tile.shape, jnp.int32),
             pltpu.VMEM(corr_src.shape, jnp.int32),
             pltpu.VMEM((SENT, entries, LANES), jnp.float32),
-            pltpu.SemaphoreType.DMA((5,)),
+            pltpu.SemaphoreType.DMA((6,)),
         ],
     )(point_count, samples, corr_scan, corr_tile, corr_src)
     received = exchange(sent, AXES)
@@ -478,7 +487,7 @@
         bind(pair_kernel, devices, groups),
         (near(WIDTH, slots), f32(devices * back_rows, LANES)),
         0,
-        2,
+        3,
         [
             pltpu.VMEM((devices * back_rows, LANES), jnp.float32),
             pltpu.VMEM((SENT, LANES, slots), jnp.float32),
@@ -487,7 +496,7 @@
             pltpu.SemaphoreType.DMA((slots // LANES,)),
         ],
         (pl.BlockSpec(memory_space=pltpu.VMEM), pl.BlockSpec(memory_space=pl.ANY)),
-    )(samples, received)
+    )(limits, samples, received)
     back = exchange(back, AXES)
     share = near(per_block * scan_local, LANES)
     shares = call(

time: 55.7 us -> 55.7 us (level)
  no operation moved by 1% of the time
where the time goes in v11:
time: 55.7 us; the launch traced here: 55.4 us
  blocking collectives  35.5 us (64%)
  Pallas kernels  8.21 us (15%)
  waiting for transfers between devices  6.52 us (12%)
  starting transfers between devices  4.52 us (8%)
  between operations  0.67 us (1%)
    all_to_all x1, blocking collectives, exchange(): lax.all_to_all(x.reshape(count, 1, width), axes, split_axis=0, concat_axi...  35.5 us
    pallas_call x3, Pallas kernels, run(): return body(*args)  4.56 us
    ppermute x3, waiting for transfers between devices, local(): lax.ppermute(shares[k], 'grp', [(g, partner(g, k, groups)) for g in range...  4.41 us
    pallas_call x1, Pallas kernels, local(): pl.pallas_call(bind(send_kernel, devices, groups), out_shape=(near(device...  3.65 us
    all_to_all x1, starting transfers between devices, exchange(): lax.all_to_all(x.reshape(count, 1, width), axes, split_axis=0, concat_axi...  2.6 us
    all_to_all x1, waiting for transfers between devices, exchange(): lax.all_to_all(x.reshape(count, 1, width), axes, split_axis=0, concat_axi...  2.11 us
    ppermute x3, starting transfers between devices, local(): lax.ppermute(shares[k], 'grp', [(g, partner(g, k, groups)) for g in range...  1.93 us
  transfers between devices with their start and end apart: 4, of which 3 were waited for; matrix products, arithmetic and copies ran while one was open for 0% of the time, Pallas kernels for 1%

profile of v11, /device:TPU:0, one launch (start us, length us, event | category | flops | bytes accessed | tf_op | source)
XLA Modules:
  0.0 55.4 jit_solution(13317547652292565494)
XLA Ops:
  0.6 3.7 %shard_map.68 = (f32[2080,128]{1,0:T(8,128)S(1)}, f32[16,6,16,128]{3,2,1,0:T(8,128)S(1)}, s32[16,128]{1,0:T(8,128)S(1)}) custom-call(s32[16]{0:T(128)} %refs_0_.1, f32[16,6,16,128]{3,2,1,0:T(8,128)} %bitcast.15, s32[16,16]{1,0:T(8,128)} %refs_2_.1, s32[16,16]{1,0:T(8,128)} %refs_3_.1, s32[16,16,128]{2,1,0:T(8,128)} %refs_4_.1), custom_call_target="tpu_custom_call" | custom-call | tf_op jit(solution)/shard_map/pallas_call | solution.py:468
  4.3 35.5 %all_to_all.10 = f32[2080,1,128]{2,1,0:T(1,128)S(1)} all-to-all(f32[2080,1,128]{2,1,0:T(1,128)S(1)} %bitcast.13), channel_id=1, replica_groups=mesh['scan'=8,'grp'=4] {'scan','grp'}, dimensions={0} | all-to-all | bytes 2129920 | tf_op jit(solution)/shard_map/all_to_all | solution.py:451
  39.8 2.8 %shard_map.69 = (f32[32,512]{1,0:T(8,128)S(1)}, f32[384,128]{1,0:T(8,128)}) custom-call(s32[16,128]{1,0:T(8,128)S(1)} %get-tuple-element.13.refs_0_, f32[16,6,16,128]{3,2,1,0:T(8,128)S(1)} %get-tuple-element.14.refs_1_, f32[2080,128]{1,0:T(8,128)S(1)} %bitcast.12), custom_call_target="tpu_custom_call" | custom-call | tf_op jit(solution)/shard_map/pallas_call | solution.py:436
  42.6 2.6 %all-to-all-start.1 = ((f32[384,1,128]{2,1,0:T(1,128)}), f32[384,1,128]{2,1,0:T(1,128)S(1)}, u32[]{:S(2)}, u32[]{:S(2)}) async-start(f32[384,1,128]{2,1,0:T(1,128)} %bitcast.16), calls=%async_computation.1 | async-start | bytes 393216 | tf_op jit(solution)/shard_map/all_to_all | solution.py:451
  45.2 0.5 shard_map.70
  45.7 0.2 collective-permute-start
  45.9 1.7 %collective-permute-start.1 = (f32[96,128]{1,0:T(8,128)S(1)}, f32[96,128]{1,0:T(8,128)S(1)}, u32[]{:S(2)}, u32[]{:S(2)}) collective-permute-start(f32[96,128]{1,0:T(8,128)S(1)} %get-tuple-element.20), channel_id=1, source_target_pairs={{0,2},{1,3},{2,0},{3,1},{4,6},{5,7},{6,4},{7,5},{8,10},{9,11},{10,... | collective-permute-start | bytes 147464 | tf_op jit(solution)/shard_map/ppermute | solution.py:510
  47.5 0.1 collective-permute-start.2
  47.6 0.0 collective-permute-done.refs_2_
  47.6 3.0 %collective-permute-done.1.refs_3_ = f32[96,128]{1,0:T(8,128)S(1)} collective-permute-done((f32[96,128]{1,0:T(8,128)S(1)}, f32[96,128]{1,0:T(8,128)S(1)}, u32[]{:S(2)}, u32[]{:S(2)}) %collective-permute-start.1) | collective-permute-done | bytes 49184 | tf_op jit(solution)/shard_map/ppermute | solution.py:510
  50.6 1.4 %collective-permute-done.2.refs_4_ = f32[96,128]{1,0:T(8,128)S(1)} collective-permute-done((f32[96,128]{1,0:T(8,128)S(1)}, f32[96,128]{1,0:T(8,128)S(1)}, u32[]{:S(2)}, u32[]{:S(2)}) %collective-permute-start.2) | collective-permute-done | bytes 49184 | tf_op jit(solution)/shard_map/ppermute | solution.py:510
  52.0 2.1 %all-to-all-done.1 = f32[384,1,128]{2,1,0:T(1,128)S(1)} async-done(((f32[384,1,128]{2,1,0:T(1,128)}), f32[384,1,128]{2,1,0:T(1,128)S(1)}, u32[]{:S(2)}, u32[]{:S(2)}) %all-to-all-start.1) | async-done | bytes 196640 | tf_op jit(solution)/shard_map/all_to_all | solution.py:451
  54.1 1.3 %shard_map.71 = (f32[36,16,32]{2,1,0:T(8,128)}, f32[4,6]{1,0:T(4,128)}) custom-call(f32[384,128]{1,0:T(8,128)S(1)} %bitcast.14, f32[96,128]{1,0:T(8,128)S(1)} %get-tuple-element.18.refs_1_, f32[96,128]{1,0:T(8,128)S(1)} %collective-permute-done.refs_2_, f32[96,128]{1,0:T(8,128)S(1)} %collective-permute-done.1.refs_3_, ...), custom_call_target="tpu_custom_call" | custom-call | tf_op jit(solution)/shard_map/pallas_call | solution.py:436
Async XLA Ops:
  42.6 11.6 %all-to-all-start.1 = ((f32[384,1,128]{2,1,0:T(1,128)}), f32[384,1,128]{2,1,0:T(1,128)S(1)}, u32[]{:S(2)}, u32[]{:S(2)}) async-start(f32[384,1,128]{2,1,0:T(1,128)} %bitcast.16), calls=%async_computation.1 | async-start | bytes 393216 | tf_op jit(solution)/shard_map/all_to_all | solution.py:451
  45.7 1.9 %collective-permute-start = (f32[96,128]{1,0:T(8,128)S(1)}, f32[96,128]{1,0:T(8,128)S(1)}, u32[]{:S(2)}, u32[]{:S(2)}) collective-permute-start(f32[96,128]{1,0:T(8,128)S(1)} %get-tuple-element.19), channel_id=1, source_target_pairs={{0,1},{1,0},{2,3},{3,2},{4,5},{5,4},{6,7},{7,6},{8,9},{9,8},{10,11... | collective-permute-start | bytes 147464 | tf_op jit(solution)/shard_map/ppermute | solution.py:510
  45.9 4.7 %collective-permute-start.1 = (f32[96,128]{1,0:T(8,128)S(1)}, f32[96,128]{1,0:T(8,128)S(1)}, u32[]{:S(2)}, u32[]{:S(2)}) collective-permute-start(f32[96,128]{1,0:T(8,128)S(1)} %get-tuple-element.20), channel_id=1, source_target_pairs={{0,2},{1,3},{2,0},{3,1},{4,6},{5,7},{6,4},{7,5},{8,10},{9,11},{10,... | collective-permute-start | bytes 147464 | tf_op jit(solution)/shard_map/ppermute | solution.py:510
  47.5 4.5 %collective-permute-start.2 = (f32[96,128]{1,0:T(8,128)S(1)}, f32[96,128]{1,0:T(8,128)S(1)}, u32[]{:S(2)}, u32[]{:S(2)}) collective-permute-start(f32[96,128]{1,0:T(8,128)S(1)} %get-tuple-element.21), channel_id=1, source_target_pairs={{0,3},{1,2},{2,1},{3,0},{4,7},{5,6},{6,5},{7,4},{8,11},{9,10},{10,... | collective-permute-start | bytes 147464 | tf_op jit(solution)/shard_map/ppermute | solution.py:510
